TPU v7x, 32 devices: a whole 2x2x4 slice. The times are simulated.
32 devices in a mesh: pod: 2 (over x), data: 4 (over z), tensor: 4 (over y, core).
Axes of the slice: x: 2, y: 2, z: 4, core: 2. Of those that a mesh axis runs over, the one named last changes fastest.
Arguments:
- token_ids: int32 [4096], P(('pod', 'data')), parts along dimension 0
- embed_table: bfloat16 [32000, 2048], P('tensor')
- norm_gain: bfloat16 [2048], replicated
- w_in: bfloat16 [2048, 5632], P(None, 'tensor')
- w_out: bfloat16 [5632, 2048], P('tensor')
- d_out: bfloat16 [4096, 2048], P(('pod', 'data', 'tensor')), parts along dimension 0
Outputs:
- output 1: bfloat16 [4096, 2048], P(('pod', 'data', 'tensor')), parts along dimension 0
- output 2: float32 [64000, 2048], P(('pod', 'tensor')), parts along dimension 0
- output 3: float32 [4096, 5632], P('pod', 'tensor'), parts along dimension 0
- output 4: float32 [11264, 2048], P(('pod', 'tensor')), parts along dimension 0
There are 2 independent parts. A program takes and returns all parts, laid end to end along the dimension named above; an argument that names none is the same for every part.
All inputs are finite; a program needn't handle non-finite values.
Results may differ from a plain program's by a relative error of at most 0.00496674.
Values are sent between devices in bfloat16 or wider.
A program may use at most 1 GiB of HBM per device.

v0:
```python
import jax
import jax.numpy as jnp
from jax import lax
from jax.sharding import PartitionSpec as P

NORM_EPS = 1e-6


def gelu_tanh(value):
    return jax.nn.gelu(value, approximate=True)


def solution(mesh):
    tok_spec = P(("pod", "data", "tensor"), None)

    def per_device(token_ids, embed_table, norm_gain, w_in, w_out, d_out):
        shard_rows = embed_table.shape[0]
        tp_rank = lax.axis_index("tensor")
        local_ids = token_ids - tp_rank * shard_rows
        is_owned = (local_ids >= 0) & (local_ids < shard_rows)
        picked = jnp.take(embed_table, jnp.where(is_owned, local_ids, 0), axis=0)
        partial_rows = jnp.where(is_owned[:, None], picked, jnp.zeros_like(picked))
        embedded = lax.psum_scatter(partial_rows, "tensor", scatter_dimension=0, tiled=True)
        gain_f32 = norm_gain.astype(jnp.float32)
        x_f32 = embedded.astype(jnp.float32)
        inv_rms = lax.rsqrt(jnp.mean(x_f32 * x_f32, axis=-1, keepdims=True) + NORM_EPS)
        x_hat = x_f32 * inv_rms
        normed = (x_hat * gain_f32).astype(jnp.bfloat16)
        normed_all = lax.all_gather(normed, "tensor", axis=0, tiled=True)
        pre_gelu = jnp.dot(normed_all, w_in, preferred_element_type=jnp.float32).astype(jnp.bfloat16)
        hidden_f32, gelu_pull = jax.vjp(gelu_tanh, pre_gelu.astype(jnp.float32))
        hidden = hidden_f32.astype(jnp.bfloat16)
        mlp_part = jnp.dot(hidden, w_out, preferred_element_type=jnp.float32)
        mlp_out = lax.psum_scatter(mlp_part, "tensor", scatter_dimension=0, tiled=True)
        block_out = (x_f32 + mlp_out).astype(jnp.bfloat16)

        grad_all = lax.all_gather(d_out, "tensor", axis=0, tiled=True)
        grad_hidden = lax.dot_general(grad_all, w_out, (((1,), (1,)), ((), ())), preferred_element_type=jnp.float32)
        grad_pre = gelu_pull(grad_hidden)[0].astype(jnp.bfloat16)
        grad_w_out = lax.dot_general(hidden, grad_all, (((0,), (0,)), ((), ())), preferred_element_type=jnp.float32)
        grad_w_in = lax.dot_general(normed_all, grad_pre, (((0,), (0,)), ((), ())), preferred_element_type=jnp.float32)
        norm_part = lax.dot_general(grad_pre, w_in, (((1,), (1,)), ((), ())), preferred_element_type=jnp.float32)
        d_normed = lax.psum_scatter(norm_part, "tensor", scatter_dimension=0, tiled=True)
        d_hat = d_normed * gain_f32
        d_norm_in = inv_rms * (d_hat - x_hat * jnp.mean(d_hat * x_hat, axis=-1, keepdims=True))
        d_embed = (d_out.astype(jnp.float32) + d_norm_in).astype(jnp.bfloat16)
        d_embed_all = lax.all_gather(d_embed, "tensor", axis=0, tiled=True)
        grad_table = jax.ops.segment_sum(d_embed_all.astype(jnp.float32), jnp.where(is_owned, local_ids, shard_rows), num_segments=shard_rows)
        grad_table = lax.psum(grad_table, "data")
        grad_w_in = lax.psum(grad_w_in, "data")
        grad_w_out = lax.psum(grad_w_out, "data")
        return block_out, grad_table, grad_w_in, grad_w_out

    return jax.shard_map(
        per_device,
        mesh=mesh,
        in_specs=(P(("pod", "data")), P("tensor", None), P(None), P(None, "tensor"), P("tensor", None), tok_spec),
        out_specs=(tok_spec, P(("pod", "tensor"), None), P("pod", "tensor"), P(("pod", "tensor"), None)),
        check_vma=False,
    )
```

profile of v0, /device:TPU:0, one launch (start us, length us, event | category | flops | bytes accessed | tf_op | source)
XLA Modules:
  0.0 3316.5 jit_solution(5785538331295364821)
XLA Ops:
  7.2 0.0 reduce-scatter.4.cloned.1.call-start
  7.2 0.7 compare_and_fusion
  7.9 11.3 gather_fusion
  19.2 0.0 copy-start.3
  19.2 1.6 select_select_fusion
  20.8 0.0 reduce-scatter.4.cloned.1.call-update
  20.9 0.0 all-gather.6.cloned.1.call-start
  20.9 0.7 all-gather.6.cloned.1.call-update
  21.6 0.0 all-gather.4.cloned.1.call-start
  21.7 0.0 copy-done.3
  21.7 42.2 %reduce-scatter.4.cloned.1.call-done = bf16[128,2048]{1,0:T(8,128)(2,1)} async-done(((bf16[512,2048]{1,0:T(8,128)(2,1)}), bf16[128,2048]{1,0:T(8,128)(2,1)}) %reduce-scatter.4.cloned.1.call-update) | async-done | bytes 524304 | tf_op jit(solution)/shard_map/reduce_scatter | solution.py:23
  63.9 1.2 fusion.19
  65.2 2.0 fusion.13
  67.2 0.0 all-gather.4.cloned.1.call-update
  67.2 0.0 reduce-scatter.8.cloned.1.call-start
  67.3 20.6 all-gather.6.cloned.1.call-done
  87.8 8.3 fusion.29
  96.1 16.2 all-gather.4.cloned.1.call-done
  112.3 0.0 copy-start.6
  112.3 6.8 convolution_convert_fusion
  119.2 0.0 copy-done.6
  119.2 0.0 copy-start.8
  119.2 9.5 fusion.27
  128.7 0.0 reduce-scatter.8.cloned.1.call-update
  128.7 0.0 reduce-scatter.6.cloned.1.call-start
  128.7 0.0 copy-done.8
  128.7 7.9 fusion.23
  136.6 0.0 copy-start
  136.6 0.0 copy-start.1
  136.6 0.0 reduce-scatter.6.cloned.1.call-update
  136.7 0.0 copy-start.2
  136.7 0.0 copy-start.4
  136.7 0.2 all-gather.8.cloned.1.call-start
  136.9 35.7 %reduce-scatter.8.cloned.1.call-done = f32[128,2048]{1,0:T(8,128)} async-done(((f32[512,2048]{1,0:T(8,128)}), f32[128,2048]{1,0:T(8,128)}) %reduce-scatter.8.cloned.1.call-update) | async-done | bytes 1048592 | tf_op jit(solution)/shard_map/reduce_scatter | solution.py:43
  172.7 0.0 copy-done
  172.7 1.5 fusion.14
  174.2 45.3 %reduce-scatter.6.cloned.1.call-done = f32[128,2048]{1,0:T(8,128)} async-done(((f32[512,2048]{1,0:T(8,128)}), f32[128,2048]{1,0:T(8,128)}) %reduce-scatter.6.cloned.1.call-update) | async-done | bytes 1048592 | tf_op jit(solution)/shard_map/reduce_scatter | solution.py:34
  219.4 0.0 copy-done.1
  219.5 3.0 fusion.18
  222.4 0.0 all-gather.8.cloned.1.call-update
  222.5 0.0 all-reduce.3.cloned.1.call-start
  222.5 0.0 copy-done.2
  222.5 0.0 copy-done.4
  222.6 0.0 copy-start.5
  222.6 0.0 copy-start.7
  222.6 0.0 copy-start.9
  222.6 8.5 fusion.21
  231.1 0.0 copy-done.5
  231.1 0.0 copy-done.7
  231.1 0.0 copy-done.9
  231.1 6.9 fusion.25
  238.0 7.0 all-gather.8.cloned.1.call-done
  244.9 4.1 convert_element_type.43
  249.0 21.2 broadcast_in_dim.42
  270.2 92.6 %scatter_fusion = f32[8000,2048]{1,0:T(8,128)} fusion(f32[8000,2048]{1,0:T(8,128)} %broadcast_in_dim.42, s32[512]{0:T(512)S(1)} %subtract_select_fusion, f32[512,2048]{1,0:T(8,128)} %convert_element_type.43), kind=kCustom, calls=%fused_computation.1 | custom fusion | flops 1048576 | bytes 12584960 | tf_op jit(solution)/shard_map/scatter-add | solution.py:48
  362.8 0.0 all-reduce.3.cloned.1.call-update
  362.8 2883.7 %all-reduce.3.cloned.1.call-done = (f32[8000,2048]{1,0:T(8,128)}, f32[2048,1408]{1,0:T(8,128)}, f32[1408,2048]{1,0:T(8,128)}) async-done(((f32[8000,2048]{1,0:T(8,128)}, f32[2048,1408]{1,0:T(8,128)}, f32[1408,2048]{1,0:T(8,128)}), (f32[8000,2048]{1,0:T(8,128)}, f32[2048,1408]{1,0:T(8,128)}, f32[1408,2048]{1,0:T(8,128)})) %all-reduce.3.cloned.1.call-update) | async-done | bytes 88604688 | tf_op jit(solution)/shard_map/psum | solution.py:49
  3246.5 43.1 %copy.14 = f32[8000,2048]{1,0:T(8,128)} copy(f32[8000,2048]{1,0:T(8,128)} %get-tuple-element.13) | data formatting | bytes 131072000
  3289.6 9.4 copy.15
  3299.1 10.6 copy.16
  (5 shorter events, 0.0 us)
Async XLA Ops:
  7.2 56.8 %reduce-scatter.4.cloned.1.call-start = ((), (), s32[]{:S(2)}) async-start(), calls=%async_computation.3 | async-start | bytes 2621440 | tf_op jit(solution)/shard_map/reduce_scatter | solution.py:23
  19.2 2.5 copy-start.3
  20.9 67.0 %all-gather.6.cloned.1.call-start = ((), (), s32[]{:S(2)}) async-start(), calls=%async_computation.6 | async-start | bytes 2621440 | tf_op jit(solution)/shard_map/all_gather | solution.py:37
  21.6 90.7 %all-gather.4.cloned.1.call-start = ((), (), s32[]{:S(2)}) async-start(), calls=%async_computation.4 | async-start | bytes 2621440 | tf_op jit(solution)/shard_map/all_gather | solution.py:29
  67.2 105.4 %reduce-scatter.8.cloned.1.call-start = ((), (), s32[]{:S(2)}) async-start(), calls=%async_computation.7 | async-start | bytes 5242880 | tf_op jit(solution)/shard_map/reduce_scatter | solution.py:43
  112.3 6.8 copy-start.6
  119.2 9.6 copy-start.8
  128.7 90.8 %reduce-scatter.6.cloned.1.call-start = ((), (), s32[]{:S(2)}) async-start(), calls=%async_computation.5 | async-start | bytes 5242880 | tf_op jit(solution)/shard_map/reduce_scatter | solution.py:34
  136.6 36.0 %copy-start = (bf16[128,2048]{1,0:T(8,128)(2,1)S(1)}, bf16[128,2048]{1,0:T(8,128)(2,1)}, u32[]{:S(2)}) copy-start(bf16[128,2048]{1,0:T(8,128)(2,1)} %reduce-scatter.4.cloned.1.call-done) | copy-start | bytes 1572868
  136.6 82.8 %copy-start.1 = (bf16[128,2048]{1,0:T(8,128)(2,1)S(1)}, bf16[128,2048]{1,0:T(8,128)(2,1)}, u32[]{:S(2)}) copy-start(bf16[128,2048]{1,0:T(8,128)(2,1)} %param.11) | copy-start | bytes 1572868
  136.7 85.9 %copy-start.2 = (s32[512]{0:T(512)S(1)}, s32[512]{0:T(512)}, u32[]{:S(2)}) copy-start(s32[512]{0:T(512)} %param.6) | copy-start | bytes 6148
  136.7 85.9 %copy-start.4 = (bf16[512,2048]{1,0:T(8,128)(2,1)S(1)}, bf16[512,2048]{1,0:T(8,128)(2,1)}, u32[]{:S(2)}) copy-start(bf16[512,2048]{1,0:T(8,128)(2,1)} %all-gather.6.cloned.1.call-done) | copy-start | bytes 6291460
  136.7 108.2 %all-gather.8.cloned.1.call-start = ((), (), s32[]{:S(2)}) async-start(), calls=%async_computation.8 | async-start | bytes 2621440 | tf_op jit(solution)/shard_map/all_gather | solution.py:47
  222.5 3024.1 %all-reduce.3.cloned.1.call-start = ((), (), s32[]{:S(2)}) async-start(), calls=%async_computation.9 | async-start | bytes 177209344 | tf_op jit(solution)/shard_map/psum | solution.py:49
  222.6 8.5 copy-start.5
  222.6 8.5 copy-start.7
  222.6 8.5 copy-start.9
Sparse Core Ops, SparseCore 0:
  21.0 42.9 reduce-scatter.3
  65.5 22.2 all-gather.5
  90.0 22.3 all-gather.3
  128.8 43.8 reduce-scatter.7
  175.6 43.8 reduce-scatter.5
  222.6 22.3 all-gather.7
  363.0 2883.5 all-reduce.2
where the time goes:
time: 3320 us
  waiting for transfers between devices  3050 us (92%)
  other arithmetic  107 us (3%)
  local copies, waits for them, and re-layouts  95.7 us (3%)
  matrix products  47.8 us (1%)
    psum x1, waiting for transfers between devices, per_device(): grad_table = lax.psum(grad_table, 'data')  2880 us
    scatter-add x1, other arithmetic, per_device(): jax.ops.segment_sum(d_embed_all.astype(jnp.float32), jnp.where(is_owned,...  92.6 us
  transfers between devices with their start and end apart: 7, of which 7 were waited for; matrix products, arithmetic and copies ran while one was open for 1% of the time, Pallas kernels for 0%

commit v1 on v0

v1 whole, which is shorter than its diff:
```python
import functools

import jax
import jax.numpy as jnp
from jax import lax
from jax.experimental import pallas as pl
from jax.experimental.pallas import tpu as pltpu
from jax.sharding import PartitionSpec as P

NORM_EPS = 1e-6
GELU_A = 0.7978845608028654
GELU_B = 0.044715
MESH = pl.DeviceIdType.MESH
NT = (((1,), (1,)), ((), ()))
TN = (((0,), (0,)), ((), ()))
F32, BF16 = jnp.float32, jnp.bfloat16
HOPS = (1, -1, 2, -2)

R_IDS, R_DZ, R_DY, R_DC, R_NZ, R_NC, R_XZ, R_XY, R_XC = (4 * i for i in range(9))
R_XM, R_X, R_PC, R_PY, N_R = 36, 37, 39, 41, 43
S_IDS, S_DZ, S_DY, S_DC, S_NZ, S_NC, S_XZ, S_XY, S_XC = 0, 3, 8, 12, 16, 21, 25, 30, 34
S_XM, S_X, S_PC, S_PY, N_S = 38, 39, 41, 43, 45
L_W1, L_W2, L_XM, L_DO, L_N, L_D, L_H, L_DU, L_DX, N_L = 0, 1, 2, 3, 4, 8, 12, 13, 14, 15


def tiles(total, step, body):
    full = total // step

    def one(j, carry):
        body(pl.multiple_of(j * step, step), step)
        return carry

    lax.fori_loop(0, full, one, 0)
    if total % step:
        body(full * step, total % step)


def rows_loop(total, body):
    def one(j, carry):
        body(pl.multiple_of(j * 16, 16))
        return carry

    lax.fori_loop(0, total // 16, one, 0)


def group_kernel(ids_ref, xm_hbm, w1_hbm, w2_hbm, g_ref, do_hbm,
                 out_ref, ids_o, n_o, d_o, h_o, du_o, dx_o,
                 w1, w2, n, d, xm, xr, xc, xy, dh, hs, dus, pd, pf, rd, rf, sd, sf, yd, yf, dxo, idl,
                 lsem, ssem, rsem):
    t, m = do_hbm.shape
    f = w1_hbm.shape[1]
    z = lax.axis_index("data")
    r = lax.axis_index("tensor")
    y, c = lax.div(r, 2), lax.rem(r, 2)
    partner = {"tensor": 2 * y + 1 - c}
    across = {"tensor": 2 * (1 - y) + c}
    half = lax.div(z, 2)
    inner = z + half * (3 - 2 * z)
    order = [b + half * (3 - 2 * b) for b in (1 - inner, 2, 3)]
    middle = inner == 1
    beyond = {"data": z + 2 * half - 1}

    def row(zz, cc, yy=0):
        return pl.multiple_of(zz * (4 * t) + cc * (2 * t) + yy * t, t)

    def blk(ref, zz, cc, yy):
        return ref.at[pl.ds(row(zz, cc, yy), t)]

    def duo(ref, zz, cc):
        return ref.at[pl.ds(row(zz, cc), 2 * t)]

    def remote(src, dst, s, q, dev):
        return pltpu.make_async_remote_copy(
            src_ref=src, dst_ref=dst, send_sem=ssem.at[s], recv_sem=rsem.at[q], device_id=dev, device_id_type=MESH
        )

    def local(src, dst, i):
        return pltpu.make_async_copy(src, dst, lsem.at[i])

    def arrived(ref, q):
        remote(ref, ref, 0, q, partner).wait_recv()

    def along(src, dst, s, q, act):
        for i, hop in enumerate(HOPS):
            to = z + hop

            @pl.when((to >= 0) & (to <= 3))
            def _():
                act(remote(src, dst, s + i, q + z, {"data": to}))

    def forward(src, s, q, act):
        @pl.when(middle)
        def _():
            act(remote(src, src, s + 4, q + order[2], beyond))

    def start(cp):
        cp.start()

    def sent(cp):
        cp.wait_send()

    barrier = pltpu.get_barrier_semaphore()
    pl.semaphore_signal(barrier, inc=1, device_id=partner, device_id_type=MESH)
    pl.semaphore_signal(barrier, inc=1, device_id=across, device_id_type=MESH)
    for k in range(3):
        pl.semaphore_signal(barrier, inc=1, device_id={"data": order[k]}, device_id_type=MESH)

    own_d = blk(d, z, c, y)
    local(do_hbm, own_d, L_DO).start()
    local(xm_hbm, xm, L_XM).start()
    local(w2_hbm, w2, L_W2).start()
    local(w1_hbm, w1, L_W1).start()
    pl.semaphore_wait(barrier, 5)

    local(do_hbm, own_d, L_DO).wait()
    remote(own_d, own_d, S_DY + z, R_DY + z, across).start()
    along(own_d, own_d, S_DZ, R_DZ, start)
    local(xm_hbm, xm, L_XM).wait()
    xm_out = remote(xm.at[pl.ds(row(0, 1 - c), 2 * t)], xr, S_XM, R_XM, partner)
    xm_out.start()
    for k in range(3):
        remote(ids_ref, idl.at[z], S_IDS + k, R_IDS + z, {"data": order[k]}).start()
    idl[z] = ids_ref[...]

    arrived(xr, R_XM)
    for b in range(2):
        def join(i, b=b):
            at = pl.ds(b * t + i, 16)
            xc[at, :] = xm[pl.ds(row(0, c, b) + i, 16), :] + xr[at, :]

        rows_loop(t, join)
        half_x = pl.ds(b * t, t)
        remote(xc.at[half_x], xy.at[half_x], S_X + b, R_X + b, across).start()

    def d_pair(zz, act):
        act(remote(duo(d, zz, c), duo(d, zz, c), S_DC + zz, R_DC + zz, partner))

    arrived(blk(d, z, c, 1 - y), R_DY + z)
    d_pair(z, start)
    arrived(duo(d, z, 1 - c), R_DC + z)
    local(w2_hbm, w2, L_W2).wait()

    def grad_hidden(zz):
        at = pl.ds(row(zz, 0), 4 * t)

        def body(off, w):
            dh[:, pl.ds(off, w)] = lax.dot_general(d[at, :], w2[pl.ds(off, w), :], NT, preferred_element_type=F32)

        tiles(f, 256, body)

    def hidden(zz):
        at = pl.ds(row(zz, 0), 4 * t)

        def body(off, w):
            to = pl.ds(off, w)
            u = jnp.dot(n[at, :], w1[:, to], preferred_element_type=F32).astype(BF16).astype(F32)
            uu = u * u
            th = jnp.tanh(GELU_A * (u + GELU_B * (uu * u)))
            cdf = 0.5 * (1.0 + th)
            hs[:, to] = (u * cdf).astype(BF16)
            slope = cdf + (0.5 * GELU_A) * u * (1.0 - th * th) * (1.0 + (3.0 * GELU_B) * uu)
            dus[:, to] = (dh[:, to] * slope).astype(BF16)

        tiles(f, 256, body)

    def keep(zz, act):
        at = pl.ds(row(zz, 0), 4 * t)
        act(local(hs, h_o.at[at], L_H))
        act(local(dus, du_o.at[at], L_DU))

    def keep_inputs(zz, act):
        at = pl.ds(row(zz, 0), 4 * t)
        act(local(n.at[at], n_o.at[at], L_N + zz))
        act(local(d.at[at], d_o.at[at], L_D + zz))

    def local_wait(cp):
        cp.wait()

    grad_hidden(z)

    def d_across(zz, act):
        act(remote(blk(d, zz, c, y), blk(d, zz, c, y), S_DY + zz, R_DY + zz, across))

    arrived(blk(d, order[0], c, y), R_DZ + order[0])
    d_across(order[0], start)

    gain = g_ref[...].astype(F32)
    for b in range(2):
        arrived(xy.at[pl.ds(b * t, t)], R_X + b)
        local_sent = remote(xc.at[pl.ds(b * t, t)], xy.at[pl.ds(b * t, t)], S_X + b, R_X + b, across)
        local_sent.wait_send()

        def norm(i, b=b):
            at = pl.ds(b * t + i, 16)
            x16 = xc[at, :] + xy[at, :]
            xc[at, :] = x16
            x = x16.astype(F32)
            s = lax.rsqrt(jnp.mean(x * x, axis=-1, keepdims=True) + NORM_EPS)
            n[pl.ds(row(z, c, b) + i, 16), :] = ((x * s) * gain).astype(BF16)

        rows_loop(t, norm)

    def n_pair(zz, act):
        act(remote(duo(n, zz, c), duo(n, zz, c), S_NC + zz, R_NC + zz, partner))

    n_pair(z, start)
    along(duo(n, z, c), duo(n, z, c), S_NZ, R_NZ, start)
    arrived(duo(n, z, 1 - c), R_NC + z)
    local(w1_hbm, w1, L_W1).wait()
    hidden(z)
    keep(z, start)
    keep_inputs(z, start)

    def part_dn(off, w):
        pd[:, pl.ds(off, w)] = lax.dot_general(dus[...], w1[pl.ds(off, w), :], NT, preferred_element_type=F32)

    def part_y(off, w):
        pf[:, pl.ds(off, w)] = jnp.dot(hs[...], w2[:, pl.ds(off, w)], preferred_element_type=F32)

    def part_pair(src, dst, i):
        return remote(src.at[pl.ds(row(0, 1 - c), 2 * t)], dst, S_PC + i, R_PC + i, partner)

    def part_across(src, dst, i):
        return remote(src, dst, S_PY + i, R_PY + i, across)

    def gather_part(part, got, total):
        def add(i):
            total[pl.ds(i, 16), :] = part[pl.ds(row(0, c, 1 - y) + i, 16), :] + got[pl.ds((1 - y) * t + i, 16), :]

        rows_loop(t, add)

    tiles(m, 256, part_dn)
    part_pair(pd, rd, 0).start()
    arrived(blk(d, order[2], c, y), R_DZ + order[2])
    forward(blk(d, order[2], c, y), S_DZ, R_DZ, start)
    arrived(rd, R_PC)
    gather_part(pd, rd, sd)
    part_across(sd, yd, 0).start()
    tiles(m, 256, part_y)
    part_pair(pf, rf, 1).start()
    arrived(blk(d, order[1], c, y), R_DZ + order[1])
    d_across(order[1], start)
    d_across(order[2], start)
    arrived(rf, R_PC + 1)
    gather_part(pf, rf, sf)
    part_across(sf, yf, 1).start()

    arrived(yd, R_PY)

    def grad_x(i):
        at, own = pl.ds(i, 16), pl.ds(y * t + i, 16)
        dn = pd[pl.ds(row(0, c, y) + i, 16), :] + rd[own, :] + yd[at, :]
        x = xc[own, :].astype(F32)
        s = lax.rsqrt(jnp.mean(x * x, axis=-1, keepdims=True) + NORM_EPS)
        xh = x * s
        dhat = dn * gain
        dxn = s * (dhat - xh * jnp.mean(dhat * xh, axis=-1, keepdims=True))
        dxo[at, :] = (d[pl.ds(row(z, c, y) + i, 16), :].astype(F32) + dxn).astype(BF16)

    rows_loop(t, grad_x)

    def dx_across(zz, src, act):
        act(remote(src, blk(dx_o, zz, c, y), S_XY + zz, R_XY + zz, across))

    def dx_pair(zz, act):
        act(remote(duo(dx_o, zz, c), duo(dx_o, zz, c), S_XC + zz, R_XC + zz, partner))

    dx_across(z, dxo, start)
    along(dxo, blk(dx_o, z, c, y), S_XZ, R_XZ, start)
    local(dxo, blk(dx_o, z, c, y), L_DX).start()

    def unit(k):
        zz = order[k]
        arrived(duo(n, zz, c), R_NZ + zz)
        if k == 2:
            forward(duo(n, zz, c), S_NZ, R_NZ, start)
        n_pair(zz, start)
        arrived(blk(d, zz, c, 1 - y), R_DY + zz)
        d_pair(zz, start)
        arrived(duo(d, zz, 1 - c), R_DC + zz)
        keep(z if k == 0 else order[k - 1], local_wait)
        grad_hidden(zz)
        arrived(duo(n, zz, 1 - c), R_NC + zz)
        hidden(zz)
        keep(zz, start)
        keep_inputs(zz, start)

    def dx_got(k):
        zz = order[k]
        arrived(blk(dx_o, zz, c, y), R_XZ + zz)
        if k == 2:
            forward(blk(dx_o, zz, c, y), S_XZ, R_XZ, start)
        dx_across(zz, blk(dx_o, zz, c, y), start)

    unit(0)
    unit(1)
    dx_got(0)
    unit(2)
    dx_got(1)
    dx_got(2)
    arrived(yf, R_PY + 1)

    def block_out(i):
        own = pl.ds(y * t + i, 16)
        total = pf[pl.ds(row(0, c, y) + i, 16), :] + rf[own, :] + yf[pl.ds(i, 16), :]
        out_ref[pl.ds(i, 16), :] = (xc[own, :].astype(F32) + total).astype(BF16)

    rows_loop(t, block_out)
    local(dxo, blk(dx_o, z, c, y), L_DX).wait()
    for zz in (z, *order):
        arrived(blk(dx_o, zz, c, 1 - y), R_XY + zz)
        dx_pair(zz, start)
    for k in range(3):
        arrived(idl.at[order[k]], R_IDS + order[k])
    ids_o[...] = idl[...]

    keep(order[2], local_wait)
    for zz in (z, *order):
        keep_inputs(zz, local_wait)
        arrived(duo(dx_o, zz, 1 - c), R_XC + zz)
        d_across(zz, sent)
        d_pair(zz, sent)
        n_pair(zz, sent)
        dx_pair(zz, sent)
    dx_across(z, dxo, sent)
    for k in range(3):
        dx_across(order[k], blk(dx_o, order[k], c, y), sent)
        remote(ids_ref, idl.at[z], S_IDS + k, R_IDS + z, {"data": order[k]}).wait_send()
    along(own_d, own_d, S_DZ, R_DZ, sent)
    along(duo(n, z, c), duo(n, z, c), S_NZ, R_NZ, sent)
    along(dxo, blk(dx_o, z, c, y), S_XZ, R_XZ, sent)
    forward(blk(d, order[2], c, y), S_DZ, R_DZ, sent)
    forward(duo(n, order[2], c), S_NZ, R_NZ, sent)
    forward(blk(dx_o, order[2], c, y), S_XZ, R_XZ, sent)
    xm_out.wait_send()
    part_pair(pd, rd, 0).wait_send()
    part_pair(pf, rf, 1).wait_send()
    part_across(sd, yd, 0).wait_send()
    part_across(sf, yf, 1).wait_send()


def run_group(ids, xm, w1, w2, gain, d_out):
    t, m = d_out.shape
    f = w1.shape[1]
    any_, vmem = pl.BlockSpec(memory_space=pl.ANY), pl.BlockSpec(memory_space=pltpu.VMEM)
    V = pltpu.VMEM
    sds = jax.ShapeDtypeStruct
    dots = 2 * 4 * t * m * f
    return pl.pallas_call(
        group_kernel,
        out_shape=(
            sds((t, m), BF16), sds((4, *ids.shape), jnp.int32), sds((16 * t, m), BF16), sds((16 * t, m), BF16),
            sds((16 * t, f), BF16), sds((16 * t, f), BF16), sds((16 * t, m), BF16),
        ),
        in_specs=[vmem, any_, any_, any_, vmem, any_],
        out_specs=(vmem, vmem, any_, any_, any_, any_, any_),
        scratch_shapes=[
            V((m, f), BF16), V((f, m), BF16), V((16 * t, m), BF16), V((16 * t, m), BF16),
            V((4 * t, m), BF16), V((2 * t, m), BF16), V((2 * t, m), BF16), V((2 * t, m), BF16),
            V((4 * t, f), F32), V((4 * t, f), BF16), V((4 * t, f), BF16),
            V((4 * t, m), F32), V((4 * t, m), F32), V((2 * t, m), F32), V((2 * t, m), F32),
            V((t, m), F32), V((t, m), F32), V((t, m), F32), V((t, m), F32),
            V((t, m), BF16), V((4, *ids.shape), jnp.int32),
            pltpu.SemaphoreType.DMA((N_L,)), pltpu.SemaphoreType.DMA((N_S,)), pltpu.SemaphoreType.DMA((N_R,)),
        ],
        compiler_params=pltpu.CompilerParams(collective_id=0, has_side_effects=True, vmem_limit_bytes=67043328),
        cost_estimate=pl.CostEstimate(flops=10 * dots, bytes_accessed=64 * 16 * t * m, transcendentals=16 * t * f),
        name="group_step",
    )(ids, xm, w1, w2, gain, d_out)


def table_kernel(key_ref, first_ref, dx_hbm, out_ref, dxb, dxf, sem):
    step = pl.program_id(0)
    tall = out_ref.shape[0]
    count = dxb.shape[0]

    @pl.when(step == 0)
    def _():
        cp = pltpu.make_async_copy(dx_hbm, dxb, sem)
        cp.start()
        cp.wait()

        def widen(i):
            dxf[pl.ds(i, 16), :] = dxb[pl.ds(i, 16), :].astype(F32)

        rows_loop(count, widen)

    out_ref[...] = jnp.zeros_like(out_ref)

    def add(j, carry):
        key = key_ref[j]
        to = pl.ds(lax.div(key, count) - step * tall, 1)
        out_ref[to, :] += dxf[pl.ds(lax.rem(key, count), 1), :]
        return carry

    lax.fori_loop(first_ref[step], first_ref[step + 1], add, 0)


def table_grad(ids_all, dx_all, shard_rows, tall):
    count, m = dx_all.shape
    rank0 = lax.axis_index("tensor") * shard_rows
    local_ids = ids_all.reshape(count) - rank0
    owned = (local_ids >= 0) & (local_ids < shard_rows)
    rows = jnp.where(owned, local_ids, shard_rows)
    keys = rows * count + lax.iota(jnp.int32, count)
    place = jnp.sum((keys[None, :] < keys[:, None]).astype(jnp.int32), axis=1)
    ordered = jnp.sum(jnp.where(place[:, None] == lax.iota(jnp.int32, count)[None, :], keys[:, None], 0), axis=0)
    steps = shard_rows // tall
    first = jnp.sum((rows[None, :] < (lax.iota(jnp.int32, steps + 1) * tall)[:, None]).astype(jnp.int32), axis=1)
    return pl.pallas_call(
        table_kernel,
        out_shape=jax.ShapeDtypeStruct((shard_rows, m), F32),
        grid_spec=pltpu.PrefetchScalarGridSpec(
            num_scalar_prefetch=2,
            grid=(steps,),
            in_specs=[pl.BlockSpec(memory_space=pl.ANY)],
            out_specs=pl.BlockSpec((tall, m), lambda i, *_: (i, 0)),
            scratch_shapes=[
                pltpu.VMEM((count, m), BF16), pltpu.VMEM((count, m), F32), pltpu.SemaphoreType.DMA,
            ],
        ),
        compiler_params=pltpu.CompilerParams(dimension_semantics=("arbitrary",), vmem_limit_bytes=50 << 20),
        cost_estimate=pl.CostEstimate(flops=count * m, bytes_accessed=4 * shard_rows * m, transcendentals=0),
        name="table_grad",
    )(ordered, first, dx_all)


def solution(mesh):
    tok_spec = P(("pod", "data", "tensor"), None)

    def per_device(token_ids, embed_table, norm_gain, w_in, w_out, d_out):
        shard_rows = embed_table.shape[0]
        t = d_out.shape[0]
        ids = token_ids.reshape(2, 2, t).transpose(1, 0, 2).reshape(4 * t)
        local_ids = ids - lax.axis_index("tensor") * shard_rows
        owned = (local_ids >= 0) & (local_ids < shard_rows)
        picked = jnp.take(embed_table, jnp.where(owned, local_ids, 0), axis=0)
        masked = jnp.where(owned[:, None], picked, jnp.zeros_like(picked))
        out, ids_all, n_all, d_all, h_all, du_all, dx_all = run_group(
            ids.reshape(-1, 128), masked, w_in, w_out, norm_gain.reshape(1, -1), d_out
        )
        grad_w_in = lax.dot_general(n_all, du_all, TN, preferred_element_type=F32)
        grad_w_out = lax.dot_general(h_all, d_all, TN, preferred_element_type=F32)
        tall = next(k for k in (320, 64, 8) if shard_rows % k == 0)
        grad_table = table_grad(ids_all, dx_all, shard_rows, tall)
        return out, grad_table, grad_w_in, grad_w_out

    return jax.shard_map(
        per_device,
        mesh=mesh,
        in_specs=(P(("pod", "data")), P("tensor", None), P(None), P(None, "tensor"), P("tensor", None), tok_spec),
        out_specs=(tok_spec, P(("pod", "tensor"), None), P("pod", "tensor"), P(("pod", "tensor"), None)),
        check_vma=False,
    )
```

time: 3320 us -> 298 us (0.09)
  waiting for transfers between devices: 3050 us -> 0 us
  Pallas kernels: 0 us -> 241 us
  other arithmetic: 107 us -> 8.46 us
  local copies, waits for them, and re-layouts: 95.7 us -> 15.4 us
    psum x1 -> x0, waiting for transfers between devices: 2880 us -> none  [per_device(): grad_table = lax.psum(grad_table, 'data')]
    pallas_call x0 -> x2, Pallas kernels: none -> 241 us  [the longest x1 204 us: run_group(): pl.pallas_call(group_kernel, out_shape=(sds((t, m), BF16), sds((4, *ids.s...]
    reduce_scatter x3 -> x0, waiting for transfers between devices: 123 us -> none  [the longest x1 45.3 us: per_device(): lax.psum_scatter(mlp_part, 'tensor', scatter_dimension=0, tiled=True)]
    scatter-add x1 -> x0, other arithmetic: 92.6 us -> none  [per_device(): jax.ops.segment_sum(d_embed_all.astype(jnp.float32), jnp.where(is_owned,...]
    unnamed x23 -> x7, local copies, waits for them, and re-layouts: 63.2 us -> 0.81 us
    all_gather x3 -> x0, waiting for transfers between devices: 43.7 us -> none  [the longest x1 20.6 us: per_device(): grad_all = lax.all_gather(d_out, 'tensor', axis=0, tiled=True)]
  transfers between devices with their start and end apart: 7 -> 0, of which waited for: 7 -> 0; matrix products, arithmetic and copies ran while one was open for 1% -> 0% of each run, Pallas kernels for 0% -> 0%
where the time goes in v1:
time: 298 us; the launch traced here: 300 us
  Pallas kernels  241 us (81%)
  matrix products  34.5 us (12%)
  local copies, waits for them, and re-layouts  15.4 us (5%)
  other arithmetic  8.46 us (3%)
    pallas_call x1, Pallas kernels, run_group(): pl.pallas_call(group_kernel, out_shape=(sds((t, m), BF16), sds((4, *ids.s...  204 us
    pallas_call x1, Pallas kernels, table_grad(): pl.pallas_call(table_kernel, out_shape=jax.ShapeDtypeStruct((shard_rows,...  36.6 us
    dot_general x1, matrix products, per_device(): grad_w_in = lax.dot_general(n_all, du_all, TN, preferred_element_type=F32)  18.9 us
    dot_general x1, matrix products, per_device(): grad_w_out = lax.dot_general(h_all, d_all, TN, preferred_element_type=F32)  15.6 us
    gather x1, local copies, waits for them, and re-layouts, per_device(): picked = jnp.take(embed_table, jnp.where(owned, local_ids, 0), axis=0)  12.1 us

profile of v1, /device:TPU:0, one launch (start us, length us, event | category | flops | bytes accessed | tf_op | source)
XLA Modules:
  0.0 300.0 jit_solution(3810420947696792601)
XLA Ops:
  0.6 0.5 iota_multiply_fusion
  1.1 0.7 broadcast_subtract_fusion.1
  1.9 1.3 copy.14
  3.1 1.3 reshape.99.g_ref
  4.4 12.1 %gather_fusion = bf16[512,2048]{1,0:T(8,128)(2,1)S(1)} fusion(bf16[8000,2048]{1,0:T(8,128)(2,1)} %param.7, s32[1024]{0:T(1024)S(1)} %pad_clamp_fusion), kind=kCustom, calls=%fused_computation | custom fusion | bytes 4196352 | tf_op jit(solution)/shard_map/jit(_take)/gather | solution.py:437
  16.5 1.6 select_select_fusion.xm_hbm
  18.2 204.3 %group_step.1 = (bf16[128,2048]{1,0:T(8,128)(2,1)}, s32[4,4,128]{2,1,0:T(4,128)}, bf16[2048,2048]{1,0:T(8,128)(2,1)}, bf16[2048,2048]{1,0:T(8,128)(2,1)}, bf16[2...) custom-call(s32[4,128]{1,0:T(4,128)} %bitcast.21, ...), custom_call_target="tpu_custom_call" | custom-call | flops 29527900160 | bytes 268435456 | tf_op jit(solution)/shard_map/group_step/pallas_call | solution.py:349
  222.4 0.7 broadcast_subtract_fusion
  223.1 0.9 convert_reduce_fusion.1.first_ref
  224.0 1.8 convert_reduce_fusion
  225.8 2.2 select_reduce_fusion.key_ref
  228.0 0.0 copy-start.1
  228.0 0.0 copy-start.2
  228.1 18.9 %fusion = f32[2048,1408]{1,0:T(8,128)} fusion(bf16[2048,2048]{1,0:T(8,128)(2,1)} %get-tuple-element.14, bf16[2048,1408]{1,0:T(8,128)(2,1)} %get-tuple-element.15), kind=kOutput, calls=%fused_computation.17 | convolution fusion | flops 11811160064 | bytes 25690112 | tf_op jit(solution)/shard_map/dot_general | solution.py:442
  247.0 0.0 copy-done.1
  247.0 0.0 copy-done.2
  247.0 15.6 %fusion.1 = f32[1408,2048]{1,0:T(8,128)} fusion(bf16[2048,1408]{1,0:T(8,128)(2,1)S(1)} %copy-done.2, bf16[2048,2048]{1,0:T(8,128)(2,1)S(1)} %copy-done.1), kind=kOutput, calls=%fused_computation.18 | convolution fusion | flops 11811160064 | bytes 25690112 | tf_op jit(solution)/shard_map/dot_general | solution.py:443
  262.6 0.0 copy-start
  262.6 36.6 %table_grad.1 = f32[8000,2048]{1,0:T(8,128)} custom-call(s32[2048]{0:T(1024)S(1)} %select_reduce_fusion.key_ref, s32[26]{0:T(128)S(1)} %convert_reduce_fusion.1.first_ref, bf16[2048,2048]{1,0:T(8,128)(2,1)} %get-tuple-element.13.dx_hbm), custom_call_target="tpu_custom_call" | custom-call | flops 4194304 | bytes 65536000 | tf_op jit(solution)/shard_map/table_grad/pallas_call | solution.py:410
  299.2 0.0 copy-done
  299.2 0.8 copy.18
  (5 shorter events, 0.0 us)
Async XLA Ops:
  228.0 18.9 %copy-start.1 = (bf16[2048,2048]{1,0:T(8,128)(2,1)S(1)}, bf16[2048,2048]{1,0:T(8,128)(2,1)}, u32[]{:S(2)}) copy-start(bf16[2048,2048]{1,0:T(8,128)(2,1)} %get-tuple-element.17) | copy-start | bytes 25165828
  228.0 18.9 %copy-start.2 = (bf16[2048,1408]{1,0:T(8,128)(2,1)S(1)}, bf16[2048,1408]{1,0:T(8,128)(2,1)}, u32[]{:S(2)}) copy-start(bf16[2048,1408]{1,0:T(8,128)(2,1)} %get-tuple-element.16) | copy-start | bytes 17301508
  262.6 36.6 %copy-start = (bf16[128,2048]{1,0:T(8,128)(2,1)S(1)}, bf16[128,2048]{1,0:T(8,128)(2,1)}, u32[]{:S(2)}) copy-start(bf16[128,2048]{1,0:T(8,128)(2,1)} %get-tuple-element.26) | copy-start | bytes 1572868

commit v2 on v1

v2 whole, which is shorter than its diff:
```python
import functools

import jax
import jax.numpy as jnp
from jax import lax
from jax.experimental import pallas as pl
from jax.experimental.pallas import tpu as pltpu
from jax.sharding import PartitionSpec as P

NORM_EPS = 1e-6
GELU_A = 0.7978845608028654
GELU_B = 0.044715
MESH = pl.DeviceIdType.MESH
NT = (((1,), (1,)), ((), ()))
TN = (((0,), (0,)), ((), ()))
F32, BF16, I32 = jnp.float32, jnp.bfloat16, jnp.int32
LANES = 128
XQ = 4
PQ = 4

R_IDS, R_DZ, R_DY, R_DC, R_NZ, R_NC, R_XZ, R_XY, R_XC = 0, 4, 8, 12, 16, 24, 28, 32, 36
R_XM, R_X, R_NO, R_PC, R_PY, N_R = 40, 44, 48, 52, 60, 68
S_IDS, S_DZ, S_DY, S_DC, S_NZ, S_NC, S_XZ, S_XY, S_XC = 0, 3, 8, 12, 16, 26, 30, 35, 39
S_XM, S_X, S_NO, S_PC, S_PY, N_S = 43, 47, 51, 55, 63, 71
L_W1, L_W2, L_XM, L_DO, L_DX, L_DW, N_L = 0, 1, 5, 6, 7, 8, 10


def loop(lo, hi, body):
    def one(j, carry):
        body(j)
        return carry

    lax.fori_loop(lo, hi, one, 0)


def tiles(total, step, body):
    full = total // step
    loop(0, full, lambda j: body(pl.multiple_of(j * step, step), step))
    if total % step:
        body(full * step, total % step)


def rows_loop(total, body):
    loop(0, total // 16, lambda j: body(pl.multiple_of(j * 16, 16)))


def sort_keys(ids, keys, place, ordered, first, shard_rows, tall, rank0):
    reps, per, _ = ids.shape
    count = reps * per * LANES
    t = per * LANES // 4
    shift = t.bit_length() - 1
    lines = reps * per
    lane = lax.broadcasted_iota(I32, (per, LANES), 1)
    spot = lax.broadcasted_iota(I32, (per, LANES), 0) * LANES + lane
    block = jnp.right_shift(spot, shift)
    kept = (block & 1) * (2 * t) + jnp.right_shift(block, 1) * t + (spot & (t - 1))
    for k in range(reps):
        row = ids[k] - rank0
        row = jnp.where((row >= 0) & (row < shard_rows), row, shard_rows)
        keys[k * per : (k + 1) * per, :] = (row * count + (k * per * LANES + kept)).astype(F32)
    place[...] = jnp.zeros_like(place)
    ordered[...] = jnp.zeros_like(ordered)
    up = lax.broadcasted_iota(I32, (LANES, LANES), 0)
    over = lax.broadcasted_iota(I32, (LANES, LANES), 1)
    same = up == over
    overf = over.astype(F32)

    def column(ref, b):
        return jnp.sum(jnp.where(same, jnp.broadcast_to(ref[pl.ds(b, 1), :], (LANES, LANES)), 0.0), axis=1, keepdims=True)

    def count_below(b):
        col = column(keys, b)

        def one(a):
            at = pl.ds(a, 1)
            place[at, :] += jnp.sum(jnp.where(col < keys[at, :], 1.0, 0.0), axis=0, keepdims=True)

        loop(0, lines, one)

    loop(0, lines, count_below)

    def put(b):
        col, spot_of = column(keys, b), column(place, b)

        def one(a):
            want = overf + (a * LANES).astype(F32)
            ordered[pl.ds(a, 1), :] += jnp.sum(jnp.where(spot_of == want, col, 0.0), axis=0, keepdims=True)

        loop(0, lines, one)
        edge = overf * float(tall * count)
        first[...] += jnp.sum(jnp.where(col < edge, 1.0, 0.0), axis=0, keepdims=True)

    first[...] = jnp.zeros_like(first)
    loop(0, lines, put)


def group_kernel(shard_rows, tall, ids_ref, xm_hbm, w1_hbm, w2_hbm, g_ref, do_hbm,
                 out_ref, ord_o, first_o, dx_o, dw1_o, dw2_o,
                 w1, w2, n, d, xm, xc, xy, hs, dus, pd, pf, rd, rf, yd, yf, dxo, idl, keys, place, ordered, first,
                 lsem, ssem, rsem):
    t, m = do_hbm.shape
    f = w1_hbm.shape[1]
    tq, mq = 2 * t // XQ, m // PQ
    z = lax.axis_index("data")
    r = lax.axis_index("tensor")
    y, c = lax.div(r, 2), lax.rem(r, 2)
    partner = {"tensor": 2 * y + 1 - c}
    across = {"tensor": 2 * (1 - y) + c}
    half = lax.div(z, 2)
    inner = z + half * (3 - 2 * z)
    order = [b + half * (3 - 2 * b) for b in (1 - inner, 2, 3)]
    middle, end = inner == 1, inner == 0

    def row(zz, cc, yy=0):
        return pl.multiple_of(zz * (4 * t) + cc * (2 * t) + yy * t, t)

    def blk(ref, zz, cc, yy):
        return ref.at[pl.ds(row(zz, cc, yy), t)]

    def duo(ref, zz, cc):
        return ref.at[pl.ds(row(zz, cc), 2 * t)]

    def remote(src, dst, s, q, dev):
        return pltpu.make_async_remote_copy(
            src_ref=src, dst_ref=dst, send_sem=ssem.at[s], recv_sem=rsem.at[q], device_id=dev, device_id_type=MESH
        )

    def local(src, dst, i):
        return pltpu.make_async_copy(src, dst, lsem.at[i])

    def arrived(ref, q):
        remote(ref, ref, 0, q, partner).wait_recv()

    def start(cp):
        cp.start()

    def sent(cp):
        cp.wait_send()

    def along(src, dst, s, q, act):
        for i, hop in enumerate((1, -1)):
            to = z + hop

            @pl.when((to >= 0) & (to <= 3))
            def _():
                act(remote(src, dst, s + i, q + z, {"data": to}))

    def pass_on(k, ref, s, q, act):
        act(remote(ref, ref, s + 2 + k, q + order[k], {"data": order[1] if k == 0 else order[0]}))

    barrier = pltpu.get_barrier_semaphore()
    pl.semaphore_signal(barrier, inc=1, device_id=partner, device_id_type=MESH)
    pl.semaphore_signal(barrier, inc=1, device_id=across, device_id_type=MESH)
    for k in range(3):
        pl.semaphore_signal(barrier, inc=1, device_id={"data": order[k]}, device_id_type=MESH)

    own_d = blk(d, z, c, y)
    local(do_hbm, own_d, L_DO).start()
    local(xm_hbm, xm, L_XM).start()
    local(w2_hbm, w2, L_W2).start()
    local(w1_hbm, w1, L_W1).start()
    pl.semaphore_wait(barrier, 5)

    def piece(q):
        return pl.ds(q * tq, tq)

    local(do_hbm, own_d, L_DO).wait()
    remote(own_d, own_d, S_DY + z, R_DY + z, across).start()
    along(own_d, own_d, S_DZ, R_DZ, start)
    local(xm_hbm, xm, L_XM).wait()

    def xm_part(q):
        return remote(xm.at[pl.ds(row(0, 1 - c) + q * tq, tq)], xc.at[piece(q)], S_XM + q, R_XM + q, partner)

    def x_part(q):
        return remote(xc.at[piece(q)], xy.at[piece(q)], S_X + q, R_X + q, across)

    for q in range(XQ):
        xm_part(q).start()
    for k in range(3):
        remote(ids_ref, idl.at[z], S_IDS + k, R_IDS + z, {"data": order[k]}).start()
    idl[z] = ids_ref[...]
    for q in range(XQ):
        arrived(xc.at[piece(q)], R_XM + q)

        def join(i, q=q):
            at = pl.ds(q * tq + i, 16)
            xc[at, :] += xm[pl.ds(row(0, c) + q * tq + i, 16), :]

        rows_loop(tq, join)
        x_part(q).start()

    def d_got(k):
        arrived(blk(d, order[k], c, y), R_DZ + order[k])

    def d_on(k):
        pass_on(k, blk(d, order[k], c, y), S_DZ, R_DZ, start)

    def d_across(zz, act):
        act(remote(blk(d, zz, c, y), blk(d, zz, c, y), S_DY + zz, R_DY + zz, across))

    def d_pair(zz, act):
        act(remote(duo(d, zz, c), duo(d, zz, c), S_DC + zz, R_DC + zz, partner))

    d_got(0)

    @pl.when(middle)
    def _():
        d_on(0)
        d_got(1)
        d_on(1)

    arrived(blk(d, z, c, 1 - y), R_DY + z)
    d_pair(z, start)
    arrived(duo(d, z, 1 - c), R_DC + z)
    local(w2_hbm, w2, L_W2).wait()

    def grad_hidden(zz, dh):
        at = pl.ds(row(zz, 0), 4 * t)

        def body(off, w):
            dh[:, pl.ds(off, w)] = lax.dot_general(d[at, :], w2[pl.ds(off, w), :], NT, preferred_element_type=F32)

        tiles(f, 256, body)

    def hidden(zz, dh):
        at = pl.ds(row(zz, 0), 4 * t)

        def body(off, w):
            to = pl.ds(off, w)
            u = jnp.dot(n[at, :], w1[:, to], preferred_element_type=F32).astype(BF16).astype(F32)
            uu = u * u
            th = jnp.tanh(GELU_A * (u + GELU_B * (uu * u)))
            cdf = 0.5 * (1.0 + th)
            hs[at, to] = (u * cdf).astype(BF16)
            slope = cdf + (0.5 * GELU_A) * u * (1.0 - th * th) * (1.0 + (3.0 * GELU_B) * uu)
            dus[at, to] = (dh[:, to] * slope).astype(BF16)

        tiles(f, 256, body)

    grad_hidden(z, pf)
    d_across(order[0], start)

    gain = jnp.concatenate([g_ref[pl.ds(i, 1), :] for i in range(m // LANES)], axis=1)

    def n_own(q, act):
        at = n.at[pl.ds(row(z, c) + q * tq, tq)]
        act(remote(at, at, S_NO + q, R_NO + q, partner))

    def n_along(b, act):
        ref = blk(n, z, c, b)
        along(ref, ref, S_NZ + 5 * b, R_NZ + 4 * b, act)

    for q in range(XQ):
        arrived(xy.at[piece(q)], R_X + q)
        x_part(q).wait_send()

        def norm(i, q=q):
            at = pl.ds(q * tq + i, 16)
            x16 = xc[at, :] + xy[at, :]
            xc[at, :] = x16
            x = x16.astype(F32)
            s = lax.rsqrt(jnp.mean(x * x, axis=-1, keepdims=True) + NORM_EPS)
            n[pl.ds(row(z, c) + q * tq + i, 16), :] = ((x * s) * gain).astype(BF16)

        rows_loop(tq, norm)
        n_own(q, start)
        if q == XQ // 2 - 1:
            n_along(0, start)

            @pl.when(middle)
            def _():
                d_got(2)
                d_on(2)

        if q == XQ - 1:
            n_along(1, start)
    for q in range(XQ):
        arrived(n.at[pl.ds(row(z, 1 - c) + q * tq, tq)], R_NO + q)
    local(w1_hbm, w1, L_W1).wait()
    hidden(z, pf)

    own_rows = pl.ds(row(z, 0), 4 * t)

    def cols(q):
        return pl.ds(pl.multiple_of(q * mq, mq), mq)

    def part_pair(src, dst, i, q):
        return remote(src.at[pl.ds(row(0, 1 - c), 2 * t), cols(q)], dst.at[:, cols(q)], S_PC + PQ * i + q, R_PC + PQ * i + q, partner)

    def part_across(got, dst, i, q):
        src = got.at[pl.ds(pl.multiple_of((1 - y) * t, t), t), cols(q)]
        return remote(src, dst.at[:, cols(q)], S_PY + PQ * i + q, R_PY + PQ * i + q, across)

    def sums_out(part, got, dst, i):
        def each(q):
            arrived(got.at[:, cols(q)], R_PC + PQ * i + q)

            def add(k):
                at = pl.ds((1 - y) * t + k, 16)
                got[at, cols(q)] += part[pl.ds(row(0, c, 1 - y) + k, 16), cols(q)]

            rows_loop(t, add)
            part_across(got, dst, i, q).start()

        loop(0, PQ, each)

    def dn_part(q):
        pd[:, cols(q)] = lax.dot_general(dus[own_rows, :], w1[cols(q), :], NT, preferred_element_type=F32)
        part_pair(pd, rd, 0, q).start()

    def y_part(q):
        pf[:, cols(q)] = jnp.dot(hs[own_rows, :], w2[:, cols(q)], preferred_element_type=F32)
        part_pair(pf, rf, 1, q).start()

    loop(0, PQ, dn_part)
    sums_out(pd, rd, yd, 0)
    loop(0, PQ, y_part)

    @pl.when(end)
    def _():
        d_got(1)

    d_across(order[1], start)

    def n_got(k):
        for b in range(2):
            arrived(blk(n, order[k], c, b), R_NZ + 4 * b + order[k])

    def n_on(k):
        for b in range(2):
            pass_on(k, blk(n, order[k], c, b), S_NZ + 5 * b, R_NZ + 4 * b, start)

    def n_pair(zz, act):
        act(remote(duo(n, zz, c), duo(n, zz, c), S_NC + zz, R_NC + zz, partner))

    n_got(0)
    n_pair(order[0], start)

    @pl.when(middle)
    def _():
        n_on(0)
        n_got(1)
        n_on(1)
        n_pair(order[1], start)

    for k in range(3):
        arrived(idl.at[order[k]], R_IDS + order[k])
    sort_keys(idl, keys, place, ordered, first, shard_rows, tall, r * shard_rows)
    ord_o[...] = ordered[...].astype(I32)
    first_o[...] = first[...].astype(I32)

    for q in range(PQ):
        arrived(yd.at[:, cols(q)], R_PY + q)

    def grad_x(i):
        at, own = pl.ds(i, 16), pl.ds(y * t + i, 16)
        dn = pd[pl.ds(row(0, c, y) + i, 16), :] + rd[own, :] + yd[at, :]
        x = xc[own, :].astype(F32)
        s = lax.rsqrt(jnp.mean(x * x, axis=-1, keepdims=True) + NORM_EPS)
        xh = x * s
        dhat = dn * gain
        dxn = s * (dhat - xh * jnp.mean(dhat * xh, axis=-1, keepdims=True))
        dxo[at, :] = (d[pl.ds(row(z, c, y) + i, 16), :].astype(F32) + dxn).astype(BF16)

    rows_loop(t, grad_x)

    def dx_across(zz, src, act):
        act(remote(src, blk(dx_o, zz, c, y), S_XY + zz, R_XY + zz, across))

    def dx_pair(zz, act):
        act(remote(duo(dx_o, zz, c), duo(dx_o, zz, c), S_XC + zz, R_XC + zz, partner))

    dx_across(z, dxo, start)
    local(dxo, blk(dx_o, z, c, y), L_DX).start()

    @pl.when(end)
    def _():
        d_got(2)

    d_across(order[2], start)
    sums_out(pf, rf, yf, 1)
    for q in range(PQ):
        part_pair(pd, rd, 0, q).wait_send()

    def unit(k):
        zz = order[k]
        arrived(blk(d, zz, c, 1 - y), R_DY + zz)
        d_pair(zz, start)
        arrived(duo(d, zz, 1 - c), R_DC + zz)
        grad_hidden(zz, pd)
        arrived(duo(n, zz, 1 - c), R_NC + zz)
        hidden(zz, pd)

    def dx_got(k):
        zz = order[k]
        arrived(blk(dx_o, zz, c, y), R_XZ + zz)
        dx_across(zz, blk(dx_o, zz, c, y), start)

    def dx_on(k):
        pass_on(k, blk(dx_o, order[k], c, y), S_XZ, R_XZ, start)

    unit(0)

    @pl.when(middle)
    def _():
        n_got(2)
        n_on(2)
        n_pair(order[2], start)

    along(dxo, blk(dx_o, z, c, y), S_XZ, R_XZ, start)

    @pl.when(end)
    def _():
        n_got(1)
        n_pair(order[1], start)

    unit(1)

    @pl.when(middle)
    def _():
        for k in range(2):
            dx_got(k)
            dx_on(k)

    @pl.when(end)
    def _():
        n_got(2)
        n_pair(order[2], start)

    unit(2)

    tw = 2 * t

    def stage(i, width):
        return pd.at[pl.ds(pl.multiple_of(lax.rem(i, 2) * tw, tw), tw), pl.ds(0, width)]

    def flush(i, dst):
        return local(stage(i, dst.shape[1]), dst.at[pl.ds(pl.multiple_of(i * tw, tw), tw)], L_DW + lax.rem(i, 2))

    def weight_tile(i, lhs, rhs, dst):
        @pl.when(i >= 2)
        def _():
            flush(i - 2, dst).wait()

        at = pl.ds(pl.multiple_of(i * tw, tw), tw)
        stage(i, dst.shape[1])[...] = lax.dot_general(lhs[:, at], rhs[...], TN, preferred_element_type=F32)
        flush(i, dst).start()

    n1, n2 = m // tw, f // tw

    @pl.when(end)
    def _():
        dx_got(0)

    loop(0, n1 // 2, lambda i: weight_tile(i, n, dus, dw1_o))

    @pl.when(end)
    def _():
        dx_got(1)

    @pl.when(middle)
    def _():
        dx_got(2)
        dx_on(2)

    loop(n1 // 2, n1, lambda i: weight_tile(i, n, dus, dw1_o))
    for i in (n1 - 2, n1 - 1):
        flush(i, dw1_o).wait()

    @pl.when(end)
    def _():
        dx_got(2)

    loop(0, n2, lambda i: weight_tile(i, hs, d, dw2_o))
    for i in (n2 - 2, n2 - 1):
        flush(i, dw2_o).wait()
    if f % tw:
        rest = pd.at[pl.ds(0, f % tw)]
        rest[...] = lax.dot_general(hs[:, n2 * tw :], d[...], TN, preferred_element_type=F32)
        last = local(rest, dw2_o.at[pl.ds(n2 * tw, f % tw)], L_DW)
        last.start()
    for q in range(PQ):
        arrived(yf.at[:, cols(q)], R_PY + PQ + q)

    def block_out(i):
        own = pl.ds(y * t + i, 16)
        total = pf[pl.ds(row(0, c, y) + i, 16), :] + rf[own, :] + yf[pl.ds(i, 16), :]
        out_ref[pl.ds(i, 16), :] = (xc[own, :].astype(F32) + total).astype(BF16)

    rows_loop(t, block_out)
    local(dxo, blk(dx_o, z, c, y), L_DX).wait()
    for zz in (z, *order):
        arrived(blk(dx_o, zz, c, 1 - y), R_XY + zz)
        dx_pair(zz, start)
    if f % tw:
        last.wait()

    for zz in (z, *order):
        d_across(zz, sent)
        d_pair(zz, sent)
    for k in range(3):
        n_pair(order[k], sent)
        remote(ids_ref, idl.at[z], S_IDS + k, R_IDS + z, {"data": order[k]}).wait_send()
        dx_across(order[k], blk(dx_o, order[k], c, y), sent)
    dx_across(z, dxo, sent)
    along(own_d, own_d, S_DZ, R_DZ, sent)
    along(dxo, blk(dx_o, z, c, y), S_XZ, R_XZ, sent)
    for b in range(2):
        n_along(b, sent)

    @pl.when(middle)
    def _():
        for k in range(3):
            pass_on(k, blk(d, order[k], c, y), S_DZ, R_DZ, sent)
            pass_on(k, blk(dx_o, order[k], c, y), S_XZ, R_XZ, sent)
            for b in range(2):
                pass_on(k, blk(n, order[k], c, b), S_NZ + 5 * b, R_NZ + 4 * b, sent)

    for q in range(XQ):
        xm_part(q).wait_send()
        n_own(q, sent)
    for q in range(PQ):
        part_pair(pf, rf, 1, q).wait_send()
        part_across(rd, yd, 0, q).wait_send()
        part_across(rf, yf, 1, q).wait_send()
    for zz in (z, *order):
        arrived(duo(dx_o, zz, 1 - c), R_XC + zz)
        dx_pair(zz, sent)


def run_group(ids, xm, w1, w2, gain, d_out, shard_rows, tall):
    t, m = d_out.shape
    f = w1.shape[1]
    lines = 4 * ids.shape[0]
    any_, vmem = pl.BlockSpec(memory_space=pl.ANY), pl.BlockSpec(memory_space=pltpu.VMEM)
    V = pltpu.VMEM
    sds = jax.ShapeDtypeStruct
    dots = 2 * 4 * t * m * f
    return pl.pallas_call(
        functools.partial(group_kernel, shard_rows, tall),
        out_shape=(
            sds((t, m), BF16), sds((lines, LANES), I32), sds((1, LANES), I32), sds((16 * t, m), BF16),
            sds((m, f), F32), sds((f, m), F32),
        ),
        in_specs=[vmem, any_, any_, any_, vmem, any_],
        out_specs=(vmem, vmem, vmem, any_, any_, any_),
        scratch_shapes=[
            V((m, f), BF16), V((f, m), BF16), V((16 * t, m), BF16), V((16 * t, m), BF16),
            V((4 * t, m), BF16), V((2 * t, m), BF16), V((2 * t, m), BF16),
            V((16 * t, f), BF16), V((16 * t, f), BF16),
            V((4 * t, m), F32), V((4 * t, m), F32), V((2 * t, m), F32), V((2 * t, m), F32),
            V((t, m), F32), V((t, m), F32),
            V((t, m), BF16), V((4, *ids.shape), I32),
            V((lines, LANES), F32), V((lines, LANES), F32), V((lines, LANES), F32), V((1, LANES), F32),
            pltpu.SemaphoreType.DMA((N_L,)), pltpu.SemaphoreType.DMA((N_S,)), pltpu.SemaphoreType.DMA((N_R,)),
        ],
        compiler_params=pltpu.CompilerParams(collective_id=0, has_side_effects=True, vmem_limit_bytes=67043328),
        cost_estimate=pl.CostEstimate(flops=18 * dots, bytes_accessed=64 * 16 * t * m, transcendentals=16 * t * f),
        name="group_step",
    )(ids, xm, w1, w2, gain, d_out)


def lookup_kernel(shard_rows, ids_smem, ids_col, table, out_ref, got, sem):
    total, m = out_ref.shape
    t = total // 4
    per = 32
    chunks = total // per
    r = lax.axis_index("tensor")

    def fetch(k):
        def one(i):
            p = k * per + i
            pltpu.make_async_copy(table.at[lax.div(lax.rem(ids_smem[p], shard_rows), 8)], got.at[p], sem.at[k]).start()

        def some(j, carry):
            for u in range(8):
                one(j * 8 + u)
            return carry

        lax.fori_loop(0, per // 8, some, 0)

    loop(0, chunks, fetch)
    spot = lax.broadcasted_iota(I32, (per, 8 * per), 1)
    token = lax.broadcasted_iota(I32, (per, 8 * per), 0)

    def pick(k):
        at = pl.ds(pl.multiple_of(k * per, per), per)
        pltpu.make_async_copy(got.at[at], got.at[at], sem.at[k]).wait()
        row = ids_col[at, :] - r * shard_rows
        owned = (row >= 0) & (row < shard_rows)
        want = jnp.where(owned, (row & 7) + 8 * token, -1)
        chosen = jnp.where(want == spot, 1.0, 0.0).astype(BF16)
        rows = jnp.dot(chosen, got[at].reshape(8 * per, m), preferred_element_type=F32)
        p = k * per
        b = lax.div(p, t)
        to = lax.rem(b, 2) * (2 * t) + lax.div(b, 2) * t + lax.rem(p, t)
        out_ref[pl.ds(pl.multiple_of(to, per), per), :] = rows.astype(BF16)

    loop(0, chunks, pick)


def look_up(ids, table):
    shard_rows, m = table.shape
    total = ids.shape[0]
    return pl.pallas_call(
        functools.partial(lookup_kernel, shard_rows),
        out_shape=jax.ShapeDtypeStruct((total, m), BF16),
        grid_spec=pltpu.PrefetchScalarGridSpec(
            num_scalar_prefetch=1,
            grid=(1,),
            in_specs=[pl.BlockSpec((total, 1), lambda i, *_: (0, 0)), pl.BlockSpec(memory_space=pl.ANY)],
            out_specs=pl.BlockSpec((total, m), lambda i, *_: (0, 0)),
            scratch_shapes=[pltpu.VMEM((total, 8, m), BF16), pltpu.SemaphoreType.DMA((total // 32,))],
        ),
        compiler_params=pltpu.CompilerParams(vmem_limit_bytes=48 << 20),
        cost_estimate=pl.CostEstimate(flops=16 * total * m, bytes_accessed=20 * total * m, transcendentals=0),
        name="look_up",
    )(ids, ids.reshape(total, 1), table.reshape(shard_rows // 8, 8, m))


PHASE = 8


def table_kernel(key_ref, first_ref, dw1_ref, dw2_ref, dx_hbm, out_ref, dw1_o, dw2_o, dxb, dxf, sem):
    step = pl.program_id(0)
    tall = out_ref.shape[0]
    count = dxb.shape[0]
    each = count // PHASE

    def fetch(k):
        at = pl.ds(pl.multiple_of(k * each, each), each)
        return pltpu.make_async_copy(dx_hbm.at[at], dxb.at[at], sem.at[k])

    @pl.when(step == 0)
    def _():
        loop(0, PHASE, lambda k: fetch(k).start())

    @pl.when(step < PHASE)
    def _():
        dw1_o[...] = dw1_ref[...]
        dw2_o[...] = dw2_ref[...]
        fetch(step).wait()

        def widen(i):
            at = pl.ds(step * each + i, 16)
            dxf[at, :] = dxb[at, :].astype(F32)

        rows_loop(each, widen)

    @pl.when(step >= PHASE)
    def _():
        tile = step - PHASE
        out_ref[...] = jnp.zeros_like(out_ref)

        def add(j):
            key = key_ref[j]
            to = pl.ds(lax.div(key, count) - tile * tall, 1)
            out_ref[to, :] += dxf[pl.ds(lax.rem(key, count), 1), :]

        loop(first_ref[tile], first_ref[tile + 1], add)


def table_grad(ordered, first, dx_all, dw1, dw2, shard_rows, tall):
    count, m = dx_all.shape
    f = dw1.shape[1]

    def early(i, *_):
        return (jnp.minimum(i, PHASE - 1), 0)

    dw_specs = [pl.BlockSpec((m // PHASE, f), early), pl.BlockSpec((f // PHASE, m), early)]
    sds = jax.ShapeDtypeStruct
    return pl.pallas_call(
        table_kernel,
        out_shape=(sds((shard_rows, m), F32), sds((m, f), F32), sds((f, m), F32)),
        grid_spec=pltpu.PrefetchScalarGridSpec(
            num_scalar_prefetch=2,
            grid=(PHASE + shard_rows // tall,),
            in_specs=[*dw_specs, pl.BlockSpec(memory_space=pl.ANY)],
            out_specs=[pl.BlockSpec((tall, m), lambda i, *_: (jnp.maximum(i - PHASE, 0), 0)), *dw_specs],
            scratch_shapes=[
                pltpu.VMEM((count, m), BF16), pltpu.VMEM((count, m), F32), pltpu.SemaphoreType.DMA((PHASE,)),
            ],
        ),
        compiler_params=pltpu.CompilerParams(dimension_semantics=("arbitrary",), vmem_limit_bytes=56 << 20),
        cost_estimate=pl.CostEstimate(flops=count * m, bytes_accessed=4 * shard_rows * m + 16 * m * f, transcendentals=0),
        name="table_grad",
    )(ordered, first, dw1, dw2, dx_all)


def solution(mesh):
    tok_spec = P(("pod", "data", "tensor"), None)

    def per_device(token_ids, embed_table, norm_gain, w_in, w_out, d_out):
        shard_rows = embed_table.shape[0]
        tall = next(k for k in (320, 64, 8) if shard_rows % k == 0)
        masked = look_up(token_ids, embed_table)
        gain = norm_gain.astype(F32).reshape(-1, LANES)
        ids = token_ids.reshape(-1, LANES)
        out, ordered, first, dx_all, dw1, dw2 = run_group(ids, masked, w_in, w_out, gain, d_out, shard_rows, tall)
        grad_table, grad_w_in, grad_w_out = table_grad(
            ordered.reshape(-1), first.reshape(-1), dx_all, dw1, dw2, shard_rows, tall
        )
        return out, grad_table, grad_w_in, grad_w_out

    return jax.shard_map(
        per_device,
        mesh=mesh,
        in_specs=(P(("pod", "data")), P("tensor", None), P(None), P(None, "tensor"), P("tensor", None), tok_spec),
        out_specs=(tok_spec, P(("pod", "tensor"), None), P("pod", "tensor"), P(("pod", "tensor"), None)),
        check_vma=False,
    )
```

time: 298 us -> 239 us (0.80)
  matrix products: 34.5 us -> 0 us
  local copies, waits for them, and re-layouts: 15.4 us -> 3.61 us
  other arithmetic: 8.46 us -> 1.29 us
  Pallas kernels: 241 us -> 234 us
    dot_general x2 -> x0, matrix products: 34.5 us -> none  [the longest x1 18.9 us: per_device(): grad_w_in = lax.dot_general(n_all, du_all, TN, preferred_element_type=F32)]
    gather x1 -> x0, local copies, waits for them, and re-layouts: 12.1 us -> none  [per_device(): picked = jnp.take(embed_table, jnp.where(owned, local_ids, 0), axis=0)]
    pallas_call x2 -> x3, Pallas kernels: 241 us -> 234 us  [the longest x1 173 us: run_group(): pl.pallas_call(functools.partial(group_kernel, shard_rows, tall), out_sha...]
    reduce_sum x3 -> x0, other arithmetic: 4.88 us -> none  [the longest x1 2.22 us: table_grad(): jnp.sum(jnp.where(place[:, None] == lax.iota(jnp.int32, count)[None, :],...]
where the time goes in v2:
time: 239 us
  Pallas kernels  234 us (98%)
  local copies, waits for them, and re-layouts  3.61 us (2%)
    pallas_call x1, Pallas kernels, run_group(): pl.pallas_call(functools.partial(group_kernel, shard_rows, tall), out_sha...  173 us
    pallas_call x1, Pallas kernels, table_grad(): pl.pallas_call(table_kernel, out_shape=(sds((shard_rows, m), F32), sds((m...  51.5 us
    pallas_call x1, Pallas kernels, look_up(): pl.pallas_call(functools.partial(lookup_kernel, shard_rows), out_shape=ja...  9.38 us

profile of v2, /device:TPU:0, one launch (start us, length us, event | category | flops | bytes accessed | tf_op | source)
XLA Modules:
  0.0 239.5 jit_solution(9615503407530854819)
XLA Ops:
  0.6 1.3 bitcast_convert_fusion.g_ref
  1.9 0.8 copy.10.ids_col
  2.7 0.0 copy-start.1
  2.8 0.7 copy-done.1
  3.4 9.4 %look_up.1.xm_hbm = bf16[512,2048]{1,0:T(8,128)(2,1)S(1)} custom-call(s32[512]{0:T(512)S(1)} %copy-done.1, s32[512,1]{1,0:T(8,128)S(1)} %copy.10.ids_col, bf16[1000,8,2048]{2,1,0:T(8,128)(2,1)} %bitcast.10), custom_call_target="tpu_custom_call" | custom-call | flops 16777216 | bytes 20971520 | tf_op jit(solution)/shard_map/look_up/pallas_call | solution.py:606
  12.8 0.0 copy-start
  12.8 1.3 copy-done
  14.1 173.0 %group_step.1 = (bf16[128,2048]{1,0:T(8,128)(2,1)}, s32[16,128]{1,0:T(8,128)}, s32[1,128]{1,0:T(1,128)}, bf16[2048,2048]{1,0:T(8,128)(2,1)}, f32[2048,1408]{1,0:T(8,128)}, /*index=5*/f32[1408,2048]{1,0:T(8,128)}) custom-call(s32[4,128]{1,0:T(4,128)} %bitcast.9, bf16[512,2048]{1,0:T(8,128)(2,1)} %copy-done, bf16[2048,1408]{1,0:T(8,128)(2,1)} %w1_hbm.1, ...), custom_call_target="tpu_custom_call" | custom-call | flops 53150220288 | bytes 268435456 | tf_op jit(solution)/shard_map/group_step/pallas_call | solution.py:540
  187.2 0.0 copy-start.2
  187.2 51.5 %table_grad.1 = (f32[8000,2048]{1,0:T(8,128)}, f32[2048,1408]{1,0:T(8,128)}, f32[1408,2048]{1,0:T(8,128)}) custom-call(s32[2048]{0:T(1024)} %bitcast.11, s32[128]{0:T(128)} %bitcast.12, f32[2048,1408]{1,0:T(8,128)} %get-tuple-element.16.dw1_ref, f32[1408,2048]{1,0:T(8,128)} %get-tuple-element.17.dw2_ref, bf16[2048,2048]{1,0:T(8,128)(2,1)} %get-tuple-element.18.dx_hbm), custom_call_target="tpu_custom_call" | custom-call | flops 4194304 | bytes 111673344 | tf_op jit(solution)/shard_map/table_grad/pallas_call | solution.py:673
  238.7 0.0 copy-done.2
  238.7 0.8 copy.12
Async XLA Ops:
  2.7 0.7 copy-start.1
  12.8 1.3 copy-start
  187.2 51.5 %copy-start.2 = (bf16[128,2048]{1,0:T(8,128)(2,1)S(1)}, bf16[128,2048]{1,0:T(8,128)(2,1)}, u32[]{:S(2)}) copy-start(bf16[128,2048]{1,0:T(8,128)(2,1)} %get-tuple-element.26) | copy-start | bytes 1572868

commit v3 on v2

v3 whole, which is shorter than its diff:
```python
import functools

import jax
import jax.numpy as jnp
from jax import lax
from jax.experimental import pallas as pl
from jax.experimental.pallas import tpu as pltpu
from jax.sharding import PartitionSpec as P

NORM_EPS = 1e-6
GELU_A = 0.7978845608028654
GELU_B = 0.044715
MESH = pl.DeviceIdType.MESH
NT = (((1,), (1,)), ((), ()))
TN = (((0,), (0,)), ((), ()))
F32, BF16, I32 = jnp.float32, jnp.bfloat16, jnp.int32
LANES = 128
XQ = 4
PQ = 4

R_IDS, R_DZ, R_DY, R_DC, R_NZ, R_NC, R_XZ, R_XY, R_XC = 0, 4, 8, 12, 16, 24, 28, 36, 44
R_XM, R_X, R_NO, R_PC, R_PY, N_R = 48, 52, 56, 60, 68, 72
S_IDS, S_DZ, S_DY, S_DC, S_NZ, S_NC, S_XZ, S_XY, S_XC = 0, 3, 8, 12, 16, 26, 30, 40, 48
S_XM, S_X, S_NO, S_PC, S_PY, N_S = 52, 56, 60, 64, 72, 76
L_W1, L_W2, L_XM, L_DO, L_DX, L_YS, L_YB, L_DW, N_L = 0, 1, 2, 3, 4, 5, 6, 7, 9


def loop(lo, hi, body):
    def one(j, carry):
        body(j)
        return carry

    lax.fori_loop(lo, hi, one, 0)


def tiles(total, step, body):
    full = total // step
    loop(0, full, lambda j: body(pl.multiple_of(j * step, step), step))
    if total % step:
        body(full * step, total % step)


def rows_loop(total, body):
    loop(0, total // 16, lambda j: body(pl.multiple_of(j * 16, 16)))


def sort_keys(ids, keys, place, ordered, first, shard_rows, tall, rank0):
    reps, per, _ = ids.shape
    count = reps * per * LANES
    t = per * LANES // 4
    shift = t.bit_length() - 1
    lines = reps * per
    lane = lax.broadcasted_iota(I32, (per, LANES), 1)
    spot = lax.broadcasted_iota(I32, (per, LANES), 0) * LANES + lane
    block = jnp.right_shift(spot, shift)
    kept = (block & 1) * (2 * t) + jnp.right_shift(block, 1) * t + (spot & (t - 1))
    for k in range(reps):
        row = ids[k] - rank0
        row = jnp.where((row >= 0) & (row < shard_rows), row, shard_rows)
        keys[k * per : (k + 1) * per, :] = (row * count + (k * per * LANES + kept)).astype(F32)
    place[...] = jnp.zeros_like(place)
    ordered[...] = jnp.zeros_like(ordered)
    up = lax.broadcasted_iota(I32, (LANES, LANES), 0)
    over = lax.broadcasted_iota(I32, (LANES, LANES), 1)
    same = up == over
    overf = over.astype(F32)

    def column(ref, b):
        return jnp.sum(jnp.where(same, jnp.broadcast_to(ref[pl.ds(b, 1), :], (LANES, LANES)), 0.0), axis=1, keepdims=True)

    def count_below(b):
        col = column(keys, b)

        def one(a):
            at = pl.ds(a, 1)
            place[at, :] += jnp.sum(jnp.where(col < keys[at, :], 1.0, 0.0), axis=0, keepdims=True)

        loop(0, lines, one)

    loop(0, lines, count_below)

    def put(b):
        col, spot_of = column(keys, b), column(place, b)

        def one(a):
            want = overf + (a * LANES).astype(F32)
            ordered[pl.ds(a, 1), :] += jnp.sum(jnp.where(spot_of == want, col, 0.0), axis=0, keepdims=True)

        loop(0, lines, one)
        edge = overf * float(tall * count)
        first[...] += jnp.sum(jnp.where(col < edge, 1.0, 0.0), axis=0, keepdims=True)

    first[...] = jnp.zeros_like(first)
    loop(0, lines, put)


def group_kernel(shard_rows, tall, ids_ref, xm_hbm, w1_hbm, w2_hbm, g_ref, do_hbm,
                 base_o, ysum_o, ord_o, first_o, dx_o, dw1_o, dw2_o,
                 w1, w2, n, d, xm, xc, xy, hs, dus, pd, pf, rd, rf, yd, yb, dxo, idl, keys, place, ordered, first,
                 lsem, ssem, rsem):
    t, m = do_hbm.shape
    f = w1_hbm.shape[1]
    tq, mq = 2 * t // XQ, m // PQ
    z = lax.axis_index("data")
    r = lax.axis_index("tensor")
    y, c = lax.div(r, 2), lax.rem(r, 2)
    partner = {"tensor": 2 * y + 1 - c}
    across = {"tensor": 2 * (1 - y) + c}
    half = lax.div(z, 2)
    inner = z + half * (3 - 2 * z)
    order = [b + half * (3 - 2 * b) for b in (1 - inner, 2, 3)]
    middle, end = inner == 1, inner == 0

    def row(zz, cc, yy=0):
        return pl.multiple_of(zz * (4 * t) + cc * (2 * t) + yy * t, t)

    def blk(ref, zz, cc, yy):
        return ref.at[pl.ds(row(zz, cc, yy), t)]

    def duo(ref, zz, cc):
        return ref.at[pl.ds(row(zz, cc), 2 * t)]

    def remote(src, dst, s, q, dev):
        return pltpu.make_async_remote_copy(
            src_ref=src, dst_ref=dst, send_sem=ssem.at[s], recv_sem=rsem.at[q], device_id=dev, device_id_type=MESH
        )

    def local(src, dst, i):
        return pltpu.make_async_copy(src, dst, lsem.at[i])

    def arrived(ref, q):
        remote(ref, ref, 0, q, partner).wait_recv()

    def start(cp):
        cp.start()

    def sent(cp):
        cp.wait_send()

    def along(src, dst, s, q, act):
        for i, hop in enumerate((1, -1)):
            to = z + hop

            @pl.when((to >= 0) & (to <= 3))
            def _():
                act(remote(src, dst, s + i, q + z, {"data": to}))

    def pass_on(k, ref, s, q, act):
        act(remote(ref, ref, s + 2 + k, q + order[k], {"data": order[1] if k == 0 else order[0]}))

    barrier = pltpu.get_barrier_semaphore()
    pl.semaphore_signal(barrier, inc=1, device_id=partner, device_id_type=MESH)
    pl.semaphore_signal(barrier, inc=1, device_id=across, device_id_type=MESH)
    for k in range(3):
        pl.semaphore_signal(barrier, inc=1, device_id={"data": order[k]}, device_id_type=MESH)

    own_d = blk(d, z, c, y)
    local(do_hbm, own_d, L_DO).start()
    local(xm_hbm, xm, L_XM).start()
    local(w2_hbm, w2, L_W2).start()
    local(w1_hbm, w1, L_W1).start()
    pl.semaphore_wait(barrier, 5)

    def piece(q):
        return pl.ds(q * tq, tq)

    local(do_hbm, own_d, L_DO).wait()
    along(own_d, own_d, S_DZ, R_DZ, start)
    local(xm_hbm, xm, L_XM).wait()

    def xm_part(q):
        return remote(xm.at[pl.ds(row(0, 1 - c) + q * tq, tq)], xc.at[piece(q)], S_XM + q, R_XM + q, partner)

    def x_part(q):
        return remote(xc.at[piece(q)], xy.at[piece(q)], S_X + q, R_X + q, across)

    def d_got(k):
        arrived(blk(d, order[k], c, y), R_DZ + order[k])

    def d_on(k):
        pass_on(k, blk(d, order[k], c, y), S_DZ, R_DZ, start)

    def d_across(zz, act):
        act(remote(blk(d, zz, c, y), blk(d, zz, c, y), S_DY + zz, R_DY + zz, across))

    def d_pair(zz, act):
        act(remote(duo(d, zz, c), duo(d, zz, c), S_DC + zz, R_DC + zz, partner))

    for q in range(XQ):
        xm_part(q).start()
    for k in range(3):
        remote(ids_ref, idl.at[z], S_IDS + k, R_IDS + z, {"data": order[k]}).start()
    idl[z] = ids_ref[...]
    for q in range(XQ):
        arrived(xc.at[piece(q)], R_XM + q)

        def join(i, q=q):
            at = pl.ds(q * tq + i, 16)
            xc[at, :] += xm[pl.ds(row(0, c) + q * tq + i, 16), :]

        rows_loop(tq, join)
        x_part(q).start()
    d_across(z, start)
    d_got(0)

    @pl.when(middle)
    def _():
        d_on(0)
        d_got(1)
        d_on(1)

    gain = jnp.concatenate([g_ref[pl.ds(i, 1), :] for i in range(m // LANES)], axis=1).astype(F32)

    def n_own(q, act):
        at = n.at[pl.ds(row(z, c) + q * tq, tq)]
        act(remote(at, at, S_NO + q, R_NO + q, partner))

    def n_along(b, act):
        ref = blk(n, z, c, b)
        along(ref, ref, S_NZ + 5 * b, R_NZ + 4 * b, act)

    for q in range(XQ):
        arrived(xy.at[piece(q)], R_X + q)
        x_part(q).wait_send()

        def norm(i, q=q):
            at = pl.ds(q * tq + i, 16)
            x16 = xc[at, :] + xy[at, :]
            xc[at, :] = x16
            x = x16.astype(F32)
            s = lax.rsqrt(jnp.mean(x * x, axis=-1, keepdims=True) + NORM_EPS)
            n[pl.ds(row(z, c) + q * tq + i, 16), :] = ((x * s) * gain).astype(BF16)

        rows_loop(tq, norm)
        n_own(q, start)
        if q == XQ // 2 - 1:
            n_along(0, start)

            @pl.when(middle)
            def _():
                d_got(2)
                d_on(2)

        if q == XQ - 1:
            n_along(1, start)
    d_across(order[0], start)

    def hidden(zz, slopes):
        at = pl.ds(row(zz, 0), 4 * t)

        def body(off, w):
            to = pl.ds(off, w)
            u = jnp.dot(n[at, :], w1[:, to], preferred_element_type=F32).astype(BF16).astype(F32)
            uu = u * u
            th = jnp.tanh(GELU_A * (u + GELU_B * (uu * u)))
            cdf = 0.5 * (1.0 + th)
            hs[at, to] = (u * cdf).astype(BF16)
            slopes[:, to] = cdf + (0.5 * GELU_A) * u * (1.0 - th * th) * (1.0 + (3.0 * GELU_B) * uu)

        tiles(f, 256, body)

    def grad_hidden(zz, slopes):
        at = pl.ds(row(zz, 0), 4 * t)

        def body(off, w):
            to = pl.ds(off, w)
            dh = lax.dot_general(d[at, :], w2[to, :], NT, preferred_element_type=F32)
            dus[at, to] = (dh * slopes[:, to]).astype(BF16)

        tiles(f, 256, body)

    for q in range(XQ):
        arrived(n.at[pl.ds(row(z, 1 - c) + q * tq, tq)], R_NO + q)
    local(w1_hbm, w1, L_W1).wait()
    hidden(z, pf)
    arrived(blk(d, z, c, 1 - y), R_DY + z)
    d_pair(z, start)
    arrived(duo(d, z, 1 - c), R_DC + z)
    local(w2_hbm, w2, L_W2).wait()
    grad_hidden(z, pf)

    own_rows = pl.ds(row(z, 0), 4 * t)
    far = pl.multiple_of((1 - y) * t, t)

    def cols(q):
        return pl.ds(pl.multiple_of(q * mq, mq), mq)

    def part_pair(src, dst, i, q):
        return remote(src.at[pl.ds(row(0, 1 - c), 2 * t), cols(q)], dst.at[:, cols(q)], S_PC + PQ * i + q, R_PC + PQ * i + q, partner)

    def part_across(q):
        return remote(rd.at[pl.ds(far, t), cols(q)], yd.at[:, cols(q)], S_PY + q, R_PY + q, across)

    def sum_part(part, got, i, q):
        arrived(got.at[:, cols(q)], R_PC + PQ * i + q)

        def add(k):
            got[pl.ds(far + k, 16), cols(q)] += part[pl.ds(row(0, c, 1 - y) + k, 16), cols(q)]

        rows_loop(t, add)

    def dn_part(q):
        pd[:, cols(q)] = lax.dot_general(dus[own_rows, :], w1[cols(q), :], NT, preferred_element_type=F32)
        part_pair(pd, rd, 0, q).start()

    def y_part(q):
        pf[:, cols(q)] = jnp.dot(hs[own_rows, :], w2[:, cols(q)], preferred_element_type=F32)
        part_pair(pf, rf, 1, q).start()

    def dn_out(q):
        sum_part(pd, rd, 0, q)
        part_across(q).start()

    loop(0, PQ, dn_part)
    loop(0, PQ, dn_out)
    loop(0, PQ, y_part)

    @pl.when(end)
    def _():
        d_got(1)

    d_across(order[1], start)

    def n_got(k):
        for b in range(2):
            arrived(blk(n, order[k], c, b), R_NZ + 4 * b + order[k])

    def n_on(k):
        for b in range(2):
            pass_on(k, blk(n, order[k], c, b), S_NZ + 5 * b, R_NZ + 4 * b, start)

    def n_pair(zz, act):
        act(remote(duo(n, zz, c), duo(n, zz, c), S_NC + zz, R_NC + zz, partner))

    n_got(0)
    n_pair(order[0], start)

    @pl.when(middle)
    def _():
        n_on(0)
        n_got(1)
        n_on(1)
        n_pair(order[1], start)

    for k in range(3):
        arrived(idl.at[order[k]], R_IDS + order[k])
    sort_keys(idl, keys, place, ordered, first, shard_rows, tall, r * shard_rows)
    ord_o[...] = ordered[...].astype(I32)
    first_o[...] = first[...].astype(I32)

    for q in range(PQ):
        arrived(yd.at[:, cols(q)], R_PY + q)

    def grad_x(i):
        at, own = pl.ds(i, 16), pl.ds(y * t + i, 16)
        dn = pd[pl.ds(row(0, c, y) + i, 16), :] + rd[own, :] + yd[at, :]
        x = xc[own, :].astype(F32)
        s = lax.rsqrt(jnp.mean(x * x, axis=-1, keepdims=True) + NORM_EPS)
        xh = x * s
        dhat = dn * gain
        dxn = s * (dhat - xh * jnp.mean(dhat * xh, axis=-1, keepdims=True))
        dxo[at, :] = (d[pl.ds(row(z, c, y) + i, 16), :].astype(F32) + dxn).astype(BF16)

    rows_loop(t, grad_x)
    th = t // 2

    def dx_part(zz, yy, h):
        return dx_o.at[pl.ds(pl.multiple_of(row(zz, c, yy) + h * th, th), th)]

    def dx_own(h):
        return dxo.at[pl.ds(h * th, th)]

    def dx_across(zz, src, h, act):
        act(remote(src, dx_part(zz, y, h), S_XY + 4 * h + zz, R_XY + 4 * h + zz, across))

    def dx_along(act):
        for h in range(2):
            along(dx_own(h), dx_part(z, y, h), S_XZ + 5 * h, R_XZ + 4 * h, act)

    def dx_pair(zz, act):
        act(remote(duo(dx_o, zz, c), duo(dx_o, zz, c), S_XC + zz, R_XC + zz, partner))

    def dx_got(k, on):
        zz = order[k]
        for h in range(2):
            arrived(dx_part(zz, y, h), R_XZ + 4 * h + zz)
            if on:
                pass_on(k, dx_part(zz, y, h), S_XZ + 5 * h, R_XZ + 4 * h, start)
            dx_across(zz, dx_part(zz, y, h), h, start)

    def dx_hand(zz):
        for h in range(2):
            arrived(dx_part(zz, 1 - y, h), R_XY + 4 * h + zz)
        dx_pair(zz, start)

    for h in range(2):
        dx_across(z, dx_own(h), h, start)
    local(dxo, blk(dx_o, z, c, y), L_DX).start()

    @pl.when(end)
    def _():
        d_got(2)

    d_across(order[2], start)

    loop(0, PQ, lambda q: sum_part(pf, rf, 1, q))
    y_send = local(rf.at[pl.ds(far, t)], ysum_o, L_YS)
    y_send.start()

    def base(i):
        own = pl.ds(y * t + i, 16)
        yb[pl.ds(i, 16), :] = xc[own, :].astype(F32) + (pf[pl.ds(row(0, c, y) + i, 16), :] + rf[own, :])

    rows_loop(t, base)
    y_keep = local(yb, base_o, L_YB)
    y_keep.start()
    for q in range(PQ):
        part_pair(pd, rd, 0, q).wait_send()

    def unit(k):
        zz = order[k]
        arrived(blk(d, zz, c, 1 - y), R_DY + zz)
        d_pair(zz, start)
        arrived(duo(n, zz, 1 - c), R_NC + zz)
        hidden(zz, pd)
        arrived(duo(d, zz, 1 - c), R_DC + zz)
        grad_hidden(zz, pd)

    def n_rest(k, on):
        n_got(k)
        if on:
            n_on(k)
        n_pair(order[k], start)

    pl.when(middle)(lambda: n_rest(2, True))
    unit(0)
    dx_along(start)
    pl.when(end)(lambda: n_rest(1, False))
    unit(1)

    @pl.when(middle)
    def _():
        dx_got(0, True)
        dx_got(1, True)

    pl.when(end)(lambda: n_rest(2, False))
    unit(2)

    tw = 2 * t

    def stage(i, width):
        return pd.at[pl.ds(pl.multiple_of(lax.rem(i, 2) * tw, tw), tw), pl.ds(0, width)]

    def flush(i, dst):
        return local(stage(i, dst.shape[1]), dst.at[pl.ds(pl.multiple_of(i * tw, tw), tw)], L_DW + lax.rem(i, 2))

    def weight_tile(i, lhs, rhs, dst):
        @pl.when(i >= 2)
        def _():
            flush(i - 2, dst).wait()

        at = pl.ds(pl.multiple_of(i * tw, tw), tw)
        stage(i, dst.shape[1])[...] = lax.dot_general(lhs[:, at], rhs[...], TN, preferred_element_type=F32)
        flush(i, dst).start()

    n1, n2 = m // tw, f // tw
    pl.when(end)(lambda: dx_got(0, False))
    loop(0, n1 // 2, lambda i: weight_tile(i, n, dus, dw1_o))
    pl.when(end)(lambda: dx_got(1, False))
    pl.when(middle)(lambda: dx_got(2, True))
    loop(n1 // 2, n1, lambda i: weight_tile(i, n, dus, dw1_o))
    for i in (n1 - 2, n1 - 1):
        flush(i, dw1_o).wait()
    pl.when(end)(lambda: dx_got(2, False))
    local(dxo, blk(dx_o, z, c, y), L_DX).wait()
    dx_hand(z)
    dx_hand(order[0])
    loop(0, n2 // 2 + 1, lambda i: weight_tile(i, hs, d, dw2_o))
    dx_hand(order[1])
    loop(n2 // 2 + 1, n2, lambda i: weight_tile(i, hs, d, dw2_o))
    for i in (n2 - 2, n2 - 1):
        flush(i, dw2_o).wait()
    if f % tw:
        rest = pd.at[pl.ds(0, f % tw)]
        rest[...] = lax.dot_general(hs[:, n2 * tw :], d[...], TN, preferred_element_type=F32)
        last = local(rest, dw2_o.at[pl.ds(n2 * tw, f % tw)], L_DW)
        last.start()
    dx_hand(order[2])
    if f % tw:
        last.wait()

    y_send.wait()
    y_keep.wait()
    for zz in (z, *order):
        d_across(zz, sent)
        d_pair(zz, sent)
    for k in range(3):
        n_pair(order[k], sent)
        remote(ids_ref, idl.at[z], S_IDS + k, R_IDS + z, {"data": order[k]}).wait_send()
    along(own_d, own_d, S_DZ, R_DZ, sent)
    dx_along(sent)
    for b in range(2):
        n_along(b, sent)
        dx_across(z, dx_own(b), b, sent)
        for k in range(3):
            dx_across(order[k], dx_part(order[k], y, b), b, sent)

    @pl.when(middle)
    def _():
        for k in range(3):
            pass_on(k, blk(d, order[k], c, y), S_DZ, R_DZ, sent)
            for b in range(2):
                pass_on(k, dx_part(order[k], y, b), S_XZ + 5 * b, R_XZ + 4 * b, sent)
                pass_on(k, blk(n, order[k], c, b), S_NZ + 5 * b, R_NZ + 4 * b, sent)

    for q in range(XQ):
        xm_part(q).wait_send()
        n_own(q, sent)
    for q in range(PQ):
        part_pair(pf, rf, 1, q).wait_send()
        part_across(q).wait_send()
    for zz in (z, *order):
        arrived(duo(dx_o, zz, 1 - c), R_XC + zz)
        dx_pair(zz, sent)


def run_group(ids, xm, w1, w2, gain, d_out, shard_rows, tall):
    t, m = d_out.shape
    f = w1.shape[1]
    lines = 4 * ids.shape[0]
    any_, vmem = pl.BlockSpec(memory_space=pl.ANY), pl.BlockSpec(memory_space=pltpu.VMEM)
    V = pltpu.VMEM
    sds = jax.ShapeDtypeStruct
    dots = 2 * 4 * t * m * f
    return pl.pallas_call(
        functools.partial(group_kernel, shard_rows, tall),
        out_shape=(
            sds((t, m), F32), sds((t, m), F32), sds((lines, LANES), I32), sds((1, LANES), I32), sds((16 * t, m), BF16),
            sds((m, f), F32), sds((f, m), F32),
        ),
        in_specs=[vmem, any_, any_, any_, vmem, any_],
        out_specs=(any_, any_, vmem, vmem, any_, any_, any_),
        scratch_shapes=[
            V((m, f), BF16), V((f, m), BF16), V((16 * t, m), BF16), V((16 * t, m), BF16),
            V((4 * t, m), BF16), V((2 * t, m), BF16), V((2 * t, m), BF16),
            V((16 * t, f), BF16), V((16 * t, f), BF16),
            V((4 * t, m), F32), V((4 * t, m), F32), V((2 * t, m), F32), V((2 * t, m), F32),
            V((t, m), F32), V((t, m), F32),
            V((t, m), BF16), V((4, *ids.shape), I32),
            V((lines, LANES), F32), V((lines, LANES), F32), V((lines, LANES), F32), V((1, LANES), F32),
            pltpu.SemaphoreType.DMA((N_L,)), pltpu.SemaphoreType.DMA((N_S,)), pltpu.SemaphoreType.DMA((N_R,)),
        ],
        compiler_params=pltpu.CompilerParams(collective_id=0, has_side_effects=True, vmem_limit_bytes=67043328),
        cost_estimate=pl.CostEstimate(flops=18 * dots, bytes_accessed=64 * 16 * t * m, transcendentals=16 * t * f),
        name="group_step",
    )(ids, xm, w1, w2, gain, d_out)


def lookup_kernel(shard_rows, ids_smem, ids_vmem, table, out_hbm, got, rows, sem, out_sem):
    total, m = out_hbm.shape
    t = total // 4
    per = 32
    chunks = total // per
    r = lax.axis_index("tensor")

    def fetch(k):
        def some(j, carry):
            for u in range(8):
                p = k * per + j * 8 + u
                at = lax.div(lax.rem(ids_smem[lax.div(p, LANES), lax.rem(p, LANES)], shard_rows), 8)
                pltpu.make_async_copy(table.at[at], got.at[p], sem.at[k]).start()
            return carry

        lax.fori_loop(0, per // 8, some, 0)

    loop(0, chunks, fetch)
    spot = lax.broadcasted_iota(I32, (per, 8 * per), 1)
    token = lax.broadcasted_iota(I32, (per, 8 * per), 0)
    same = lax.broadcasted_iota(I32, (LANES, LANES), 0) == lax.broadcasted_iota(I32, (LANES, LANES), 1)

    def line(b):
        ids = ids_vmem[pl.ds(b, 1), :].astype(F32)
        col = jnp.sum(jnp.where(same, jnp.broadcast_to(ids, (LANES, LANES)), 0.0), axis=1, keepdims=True).astype(I32)
        row = col - r * shard_rows
        row = jnp.where((row >= 0) & (row < shard_rows), row & 7, -8 * per)
        for j in range(LANES // per):
            k = b * (LANES // per) + j
            at = pl.ds(pl.multiple_of(k * per, per), per)
            pltpu.make_async_copy(got.at[at], got.at[at], sem.at[k]).wait()
            want = row[j * per : (j + 1) * per] + 8 * token
            chosen = jnp.where(want == spot, 1.0, 0.0).astype(BF16)
            picked = jnp.dot(chosen, got[at].reshape(8 * per, m), preferred_element_type=F32)
            p = k * per
            nat = lax.div(p, t)
            to = pl.multiple_of(lax.rem(nat, 2) * (2 * t) + lax.div(nat, 2) * t + lax.rem(p, t), per)
            rows[pl.ds(to, per), :] = picked.astype(BF16)
            pltpu.make_async_copy(rows.at[pl.ds(to, per)], out_hbm.at[pl.ds(to, per)], out_sem).start()

    loop(0, total // LANES, line)
    pltpu.make_async_copy(rows, out_hbm, out_sem).wait()


def look_up(ids, table):
    shard_rows, m = table.shape
    total = ids.size
    any_ = pl.BlockSpec(memory_space=pl.ANY)
    return pl.pallas_call(
        functools.partial(lookup_kernel, shard_rows),
        out_shape=jax.ShapeDtypeStruct((total, m), BF16),
        in_specs=[pl.BlockSpec(memory_space=pltpu.SMEM), pl.BlockSpec(memory_space=pltpu.VMEM), any_],
        out_specs=any_,
        scratch_shapes=[
            pltpu.VMEM((total, 8, m), BF16), pltpu.VMEM((total, m), BF16),
            pltpu.SemaphoreType.DMA((total // 32,)), pltpu.SemaphoreType.DMA,
        ],
        compiler_params=pltpu.CompilerParams(vmem_limit_bytes=60 << 20),
        cost_estimate=pl.CostEstimate(flops=16 * total * m, bytes_accessed=20 * total * m, transcendentals=0),
        name="look_up",
    )(ids, ids, table.reshape(shard_rows // 8, 8, m))


RING = 6


def table_kernel(tall, key_ref, first_ref, dw1_in, dw2_in, dx_in, out_hbm, dw1_o, dw2_o, dxb, dxf, w1, w2, ring, dx_sem, in_sem, w_sem, t_sem):
    count, m = dxb.shape
    f = w1.shape[1]
    shift = count.bit_length() - 1
    steps = out_hbm.shape[0] // tall
    each = count // 8

    def dx_piece(k):
        at = pl.ds(pl.multiple_of(k * each, each), each)
        return pltpu.make_async_copy(dx_in.at[at], dxb.at[at], dx_sem.at[k])

    def w_pieces(i, back):
        for src, buf, dst, n in ((dw1_in, w1, dw1_o, m // 8), (dw2_in, w2, dw2_o, f // 8)):
            at = pl.ds(pl.multiple_of(i * n, 8), n)
            if back:
                yield pltpu.make_async_copy(buf.at[at], dst.at[at], w_sem)
            else:
                yield pltpu.make_async_copy(src.at[at], buf.at[at], in_sem.at[i])

    loop(0, 8, lambda k: dx_piece(k).start())

    def w_fetch(i):
        for cp in w_pieces(i, False):
            cp.start()

    loop(0, 8, w_fetch)

    def widen_piece(k):
        dx_piece(k).wait()

        def widen(i):
            at = pl.ds(k * each + i, 16)
            dxf[at, :] = dxb[at, :].astype(F32)

        rows_loop(each, widen)

    loop(0, 8, widen_piece)

    def tile_out(i):
        slot = lax.rem(i, RING)
        return pltpu.make_async_copy(ring.at[slot], out_hbm.at[pl.ds(pl.multiple_of(i * tall, 8), tall)], t_sem.at[slot])

    def tile(i):
        slot = lax.rem(i, RING)
        here = ring.at[slot]
        pl.when(i >= RING)(lambda: tile_out(i - RING).wait())
        here[...] = jnp.zeros_like(here)

        def add(j, key):
            ahead = key_ref[jnp.minimum(j + 1, count - 1)]
            to = pl.ds(jnp.right_shift(key, shift) - i * tall, 1)
            here[to, :] += dxf[pl.ds(key & (count - 1), 1), :]
            return ahead

        low = first_ref[i]
        lax.fori_loop(low, first_ref[i + 1], add, key_ref[jnp.minimum(low, count - 1)])
        tile_out(i).start()

        @pl.when(i < 8)
        def _():
            for cp in w_pieces(i, False):
                cp.wait()
            for cp in w_pieces(i, True):
                cp.start()

    loop(0, steps, tile)
    loop(steps - RING, steps, lambda i: tile_out(i).wait())
    pltpu.make_async_copy(w1, dw1_o, w_sem).wait()
    pltpu.make_async_copy(w2, dw2_o, w_sem).wait()


def table_grad(ordered, first, dx_all, dw1, dw2, shard_rows, tall):
    count, m = dx_all.shape
    f = dw1.shape[1]
    any_ = pl.BlockSpec(memory_space=pl.ANY)
    sds = jax.ShapeDtypeStruct
    V, S = pltpu.VMEM, pltpu.SemaphoreType.DMA
    return pl.pallas_call(
        functools.partial(table_kernel, tall),
        out_shape=(sds((shard_rows, m), F32), sds((m, f), F32), sds((f, m), F32)),
        grid_spec=pltpu.PrefetchScalarGridSpec(
            num_scalar_prefetch=2,
            grid=(1,),
            in_specs=[any_, any_, any_],
            out_specs=[any_, any_, any_],
            scratch_shapes=[
                V((count, m), BF16), V((count, m), F32), V((m, f), F32), V((f, m), F32), V((RING, tall, m), F32),
                S((8,)), S((8,)), S, S((RING,)),
            ],
        ),
        compiler_params=pltpu.CompilerParams(vmem_limit_bytes=67043328),
        cost_estimate=pl.CostEstimate(flops=16 * count * m * f, bytes_accessed=4 * shard_rows * m + 16 * m * f, transcendentals=0),
        name="table_grad",
    )(ordered, first, dw1, dw2, dx_all)


def solution(mesh):
    tok_spec = P(("pod", "data", "tensor"), None)

    def per_device(token_ids, embed_table, norm_gain, w_in, w_out, d_out):
        shard_rows = embed_table.shape[0]
        tall = next(k for k in (160, 8) if shard_rows % k == 0)
        ids = token_ids.reshape(-1, LANES)
        masked = look_up(ids, embed_table)
        gain = norm_gain.reshape(-1, LANES)
        base, ysum, ordered, first, dx_all, dw1, dw2 = run_group(ids, masked, w_in, w_out, gain, d_out, shard_rows, tall)
        other = lax.ppermute(ysum, "tensor", [(0, 2), (1, 3), (2, 0), (3, 1)])
        grad_table, grad_w_in, grad_w_out = table_grad(
            ordered.reshape(-1), first.reshape(-1), dx_all, dw1, dw2, shard_rows, tall
        )
        return (base + other).astype(BF16), grad_table, grad_w_in, grad_w_out

    return jax.shard_map(
        per_device,
        mesh=mesh,
        in_specs=(P(("pod", "data")), P("tensor", None), P(None), P(None, "tensor"), P("tensor", None), tok_spec),
        out_specs=(tok_spec, P(("pod", "tensor"), None), P("pod", "tensor"), P(("pod", "tensor"), None)),
        check_vma=False,
    )
```

time: 239 us -> 218 us (0.912)
  Pallas kernels: 234 us -> 213 us
  local copies, waits for them, and re-layouts: 3.61 us -> 0 us
    pallas_call x1, Pallas kernels: 51.5 us -> 39 us  [table_grad(): pl.pallas_call(functools.partial(table_kernel, tall), out_shape=(sds((sha...]
    pallas_call x1, Pallas kernels: 173 us -> 162 us  [run_group(): pl.pallas_call(functools.partial(group_kernel, shard_rows, tall), out_sha...]
    unnamed x7 -> x0, local copies, waits for them, and re-layouts: 2.79 us -> none
    pallas_call x1, Pallas kernels: 9.38 us -> 12 us  [look_up(): pl.pallas_call(functools.partial(lookup_kernel, shard_rows), out_shape=ja...]
    convert_element_type x0 -> x1, other arithmetic: none -> 2.45 us  [per_device(): return ((base + other).astype(BF16), grad_table, grad_w_in, grad_w_out)]
  transfers between devices with their start and end apart: 0 -> 1, of which waited for: 0 -> 0; matrix products, arithmetic and copies ran while one was open for 0% -> 0% of each run, Pallas kernels for 0% -> 18%
where the time goes in v3:
time: 218 us; the launch traced here: 217 us
  Pallas kernels  213 us (98%)
  other arithmetic  2.45 us (1%)
    pallas_call x1, Pallas kernels, run_group(): pl.pallas_call(functools.partial(group_kernel, shard_rows, tall), out_sha...  162 us
    pallas_call x1, Pallas kernels, table_grad(): pl.pallas_call(functools.partial(table_kernel, tall), out_shape=(sds((sha...  39 us
    pallas_call x1, Pallas kernels, look_up(): pl.pallas_call(functools.partial(lookup_kernel, shard_rows), out_shape=ja...  12 us
  transfers between devices with their start and end apart: 1, of which 0 were waited for; matrix products, arithmetic and copies ran while one was open for 0% of the time, Pallas kernels for 18%

profile of v3, /device:TPU:0, one launch (start us, length us, event | category | flops | bytes accessed | tf_op | source)
XLA Modules:
  0.0 217.4 jit_solution(11867190495057797937)
XLA Ops:
  0.6 12.0 %look_up.1.xm_hbm = bf16[512,2048]{1,0:T(8,128)(2,1)} custom-call(s32[4,128]{1,0:T(4,128)} %bitcast.6, s32[4,128]{1,0:T(4,128)} %bitcast.7, bf16[1000,8,2048]{2,1,0:T(8,128)(2,1)} %bitcast.5), custom_call_target="tpu_custom_call" | custom-call | flops 16777216 | bytes 20971520 | tf_op jit(solution)/shard_map/look_up/pallas_call | solution.py:607
  12.6 162.3 %group_step.1 = (f32[128,2048]{1,0:T(8,128)}, f32[128,2048]{1,0:T(8,128)}, s32[16,128]{1,0:T(8,128)}, s32[1,128]{1,0:T(1,128)}, bf16[2048,2048]{1,0:T(8,128)(2,1...) custom-call(s32[4,128]{1,0:T(4,128)} %bitcast.8, bf16[512,2048]{1,0:T(8,128)(2,1)} %look_up.1.xm_hbm, ...), custom_call_target="tpu_custom_call" | custom-call | flops 53150220288 | bytes 268435456 | tf_op jit(solution)/shard_map/group_step/pallas_call | solution.py:535
  174.9 1.0 collective-permute-start
  175.9 39.0 %table_grad.1 = (f32[8000,2048]{1,0:T(8,128)}, f32[2048,1408]{1,0:T(8,128)}, f32[1408,2048]{1,0:T(8,128)}) custom-call(s32[2048]{0:T(1024)} %bitcast.10, s32[128]{0:T(128)} %bitcast.11, f32[2048,1408]{1,0:T(8,128)} %get-tuple-element.18.dw1_in, f32[1408,2048]{1,0:T(8,128)} %get-tuple-element.19.dw2_in, bf16[2048,2048]{1,0:T(8,128)(2,1)} %get-tuple-element.20.dx_in), custom_call_target="tpu_custom_call" | custom-call | flops 94489280512 | bytes 111673344 | tf_op jit(solution)/shard_map/table_grad/pallas_call | solution.py:702
  214.9 0.0 collective-permute-done
  215.0 2.5 %add_convert_fusion = bf16[128,2048]{1,0:T(8,128)(2,1)} fusion(f32[128,2048]{1,0:T(8,128)} %get-tuple-element.14, f32[128,2048]{1,0:T(8,128)} %collective-permute-done), kind=kLoop, calls=%fused_computation | loop fusion | flops 524288 | bytes 2621440 | tf_op jit(solution)/shard_map/convert_element_type | solution.py:735
Async XLA Ops:
  174.9 40.0 %collective-permute-start = (f32[128,2048]{1,0:T(8,128)}, f32[128,2048]{1,0:T(8,128)}, u32[]{:S(2)}, u32[]{:S(2)}) collective-permute-start(f32[128,2048]{1,0:T(8,128)} %get-tuple-element.15), channel_id=1, source_target_pairs={{0,2},{1,3},{2,0},{3,1},{4,6},{5,7},{6,4},{7,5},{8,10},{9,11},{10,... | collective-permute-start | bytes 3145736 | tf_op jit(solution)/shard_map/ppermute | solution.py:731

commit v4 on v3

--- a/solution.py
+++ b/solution.py
@@ -6,6 +6,7 @@
 from jax.experimental import pallas as pl
 from jax.experimental.pallas import tpu as pltpu
 from jax.sharding import PartitionSpec as P
+
 
 NORM_EPS = 1e-6
 GELU_A = 0.7978845608028654
@@ -22,7 +23,7 @@
 R_XM, R_X, R_NO, R_PC, R_PY, N_R = 48, 52, 56, 60, 68, 72
 S_IDS, S_DZ, S_DY, S_DC, S_NZ, S_NC, S_XZ, S_XY, S_XC = 0, 3, 8, 12, 16, 26, 30, 40, 48
 S_XM, S_X, S_NO, S_PC, S_PY, N_S = 52, 56, 60, 64, 72, 76
-L_W1, L_W2, L_XM, L_DO, L_DX, L_YS, L_YB, L_DW, N_L = 0, 1, 2, 3, 4, 5, 6, 7, 9
+L_W1, L_W2, L_XM, L_DX, L_YS, L_YB, L_DW, L_DO, N_L = 0, 1, 2, 3, 4, 5, 6, 8, 12
 
 
 def loop(lo, hi, body):
@@ -94,8 +95,8 @@
     loop(0, lines, put)
 
 
-def group_kernel(shard_rows, tall, ids_ref, xm_hbm, w1_hbm, w2_hbm, g_ref, do_hbm,
-                 base_o, ysum_o, ord_o, first_o, dx_o, dw1_o, dw2_o,
+def group_kernel(shard_rows, tall, ids_ref, xm_hbm, w1_hbm, w2_hbm, g_ref, do_hbm, do_across, do_below, do_above,
+                 base_o, ysum_o, ord_o, first_o, dx_o, far_o, dw1_o, dw2_o,
                  w1, w2, n, d, xm, xc, xy, hs, dus, pd, pf, rd, rf, yd, yb, dxo, idl, keys, place, ordered, first,
                  lsem, ssem, rsem):
     t, m = do_hbm.shape
@@ -146,7 +147,8 @@
                 act(remote(src, dst, s + i, q + z, {"data": to}))
 
     def pass_on(k, ref, s, q, act):
-        act(remote(ref, ref, s + 2 + k, q + order[k], {"data": order[1] if k == 0 else order[0]}))
+        src, dst = ref if isinstance(ref, tuple) else (ref, ref)
+        act(remote(src, dst, s + 2 + k, q + order[k], {"data": order[1] if k == 0 else order[0]}))
 
     barrier = pltpu.get_barrier_semaphore()
     pl.semaphore_signal(barrier, inc=1, device_id=partner, device_id_type=MESH)
@@ -154,18 +156,24 @@
     for k in range(3):
         pl.semaphore_signal(barrier, inc=1, device_id={"data": order[k]}, device_id_type=MESH)
 
-    own_d = blk(d, z, c, y)
-    local(do_hbm, own_d, L_DO).start()
+    def load_d(act):
+        act(local(do_hbm, blk(d, z, c, y), L_DO))
+        act(local(do_across, blk(d, z, c, 1 - y), L_DO + 1))
+        pl.when(z > 0)(lambda: act(local(do_below, blk(d, z - 1, c, y), L_DO + 2)))
+        pl.when(z < 3)(lambda: act(local(do_above, blk(d, z + 1, c, y), L_DO + 3)))
+
+    def local_wait(cp):
+        cp.wait()
+
     local(xm_hbm, xm, L_XM).start()
+    load_d(start)
+    local(w1_hbm, w1, L_W1).start()
     local(w2_hbm, w2, L_W2).start()
-    local(w1_hbm, w1, L_W1).start()
     pl.semaphore_wait(barrier, 5)
 
     def piece(q):
         return pl.ds(q * tq, tq)
 
-    local(do_hbm, own_d, L_DO).wait()
-    along(own_d, own_d, S_DZ, R_DZ, start)
     local(xm_hbm, xm, L_XM).wait()
 
     def xm_part(q):
@@ -200,14 +208,15 @@
 
         rows_loop(tq, join)
         x_part(q).start()
-    d_across(z, start)
-    d_got(0)
-
-    @pl.when(middle)
-    def _():
-        d_on(0)
-        d_got(1)
-        d_on(1)
+        if q == 0:
+            load_d(local_wait)
+
+            @pl.when(middle)
+            def _():
+                d_on(0)
+                d_on(1)
+
+    d_pair(z, start)
 
     gain = jnp.concatenate([g_ref[pl.ds(i, 1), :] for i in range(m // LANES)], axis=1).astype(F32)
 
@@ -273,8 +282,6 @@
         arrived(n.at[pl.ds(row(z, 1 - c) + q * tq, tq)], R_NO + q)
     local(w1_hbm, w1, L_W1).wait()
     hidden(z, pf)
-    arrived(blk(d, z, c, 1 - y), R_DY + z)
-    d_pair(z, start)
     arrived(duo(d, z, 1 - c), R_DC + z)
     local(w2_hbm, w2, L_W2).wait()
     grad_hidden(z, pf)
@@ -370,6 +377,13 @@
     def dx_own(h):
         return dxo.at[pl.ds(h * th, th)]
 
+    def far_part(h):
+        return far_o.at[pl.ds(h * th, th)]
+
+    def dx_next(k, h):
+        here = dx_part(order[k], y, h)
+        return (here, here) if k == 1 else (here if k == 0 else far_part(h), far_part(h))
+
     def dx_across(zz, src, h, act):
         act(remote(src, dx_part(zz, y, h), S_XY + 4 * h + zz, R_XY + 4 * h + zz, across))
 
@@ -383,10 +397,11 @@
     def dx_got(k, on):
         zz = order[k]
         for h in range(2):
-            arrived(dx_part(zz, y, h), R_XZ + 4 * h + zz)
+            arrived(dx_part(zz, y, h) if k < 2 else far_part(h), R_XZ + 4 * h + zz)
             if on:
-                pass_on(k, dx_part(zz, y, h), S_XZ + 5 * h, R_XZ + 4 * h, start)
-            dx_across(zz, dx_part(zz, y, h), h, start)
+                pass_on(k, dx_next(k, h), S_XZ + 5 * h, R_XZ + 4 * h, start)
+            if k < 2:
+                dx_across(zz, dx_part(zz, y, h), h, start)
 
     def dx_hand(zz):
         for h in range(2):
@@ -471,12 +486,10 @@
     loop(n1 // 2, n1, lambda i: weight_tile(i, n, dus, dw1_o))
     for i in (n1 - 2, n1 - 1):
         flush(i, dw1_o).wait()
-    pl.when(end)(lambda: dx_got(2, False))
     local(dxo, blk(dx_o, z, c, y), L_DX).wait()
     dx_hand(z)
     dx_hand(order[0])
     loop(0, n2 // 2 + 1, lambda i: weight_tile(i, hs, d, dw2_o))
-    dx_hand(order[1])
     loop(n2 // 2 + 1, n2, lambda i: weight_tile(i, hs, d, dw2_o))
     for i in (n2 - 2, n2 - 1):
         flush(i, dw2_o).wait()
@@ -485,24 +498,24 @@
         rest[...] = lax.dot_general(hs[:, n2 * tw :], d[...], TN, preferred_element_type=F32)
         last = local(rest, dw2_o.at[pl.ds(n2 * tw, f % tw)], L_DW)
         last.start()
-    dx_hand(order[2])
+    dx_hand(order[1])
+    pl.when(end)(lambda: dx_got(2, False))
     if f % tw:
         last.wait()
 
     y_send.wait()
     y_keep.wait()
     for zz in (z, *order):
-        d_across(zz, sent)
         d_pair(zz, sent)
     for k in range(3):
+        d_across(order[k], sent)
         n_pair(order[k], sent)
         remote(ids_ref, idl.at[z], S_IDS + k, R_IDS + z, {"data": order[k]}).wait_send()
-    along(own_d, own_d, S_DZ, R_DZ, sent)
     dx_along(sent)
     for b in range(2):
         n_along(b, sent)
         dx_across(z, dx_own(b), b, sent)
-        for k in range(3):
+        for k in range(2):
             dx_across(order[k], dx_part(order[k], y, b), b, sent)
 
     @pl.when(middle)
@@ -510,7 +523,7 @@
         for k in range(3):
             pass_on(k, blk(d, order[k], c, y), S_DZ, R_DZ, sent)
             for b in range(2):
-                pass_on(k, dx_part(order[k], y, b), S_XZ + 5 * b, R_XZ + 4 * b, sent)
+                pass_on(k, dx_next(k, b), S_XZ + 5 * b, R_XZ + 4 * b, sent)
                 pass_on(k, blk(n, order[k], c, b), S_NZ + 5 * b, R_NZ + 4 * b, sent)
 
     for q in range(XQ):
@@ -519,13 +532,13 @@
     for q in range(PQ):
         part_pair(pf, rf, 1, q).wait_send()
         part_across(q).wait_send()
-    for zz in (z, *order):
+    for zz in (z, *order[:2]):
         arrived(duo(dx_o, zz, 1 - c), R_XC + zz)
         dx_pair(zz, sent)
 
 
-def run_group(ids, xm, w1, w2, gain, d_out, shard_rows, tall):
-    t, m = d_out.shape
+def run_group(ids, xm, w1, w2, gain, d_outs, shard_rows, tall):
+    t, m = d_outs[0].shape
     f = w1.shape[1]
     lines = 4 * ids.shape[0]
     any_, vmem = pl.BlockSpec(memory_space=pl.ANY), pl.BlockSpec(memory_space=pltpu.VMEM)
@@ -536,10 +549,10 @@
         functools.partial(group_kernel, shard_rows, tall),
         out_shape=(
             sds((t, m), F32), sds((t, m), F32), sds((lines, LANES), I32), sds((1, LANES), I32), sds((16 * t, m), BF16),
-            sds((m, f), F32), sds((f, m), F32),
+            sds((t, m), BF16), sds((m, f), F32), sds((f, m), F32),
         ),
-        in_specs=[vmem, any_, any_, any_, vmem, any_],
-        out_specs=(any_, any_, vmem, vmem, any_, any_, any_),
+        in_specs=[vmem, any_, any_, any_, vmem, any_, any_, any_, any_],
+        out_specs=(any_, any_, vmem, vmem, any_, any_, any_, any_),
         scratch_shapes=[
             V((m, f), BF16), V((f, m), BF16), V((16 * t, m), BF16), V((16 * t, m), BF16),
             V((4 * t, m), BF16), V((2 * t, m), BF16), V((2 * t, m), BF16),
@@ -553,7 +566,7 @@
         compiler_params=pltpu.CompilerParams(collective_id=0, has_side_effects=True, vmem_limit_bytes=67043328),
         cost_estimate=pl.CostEstimate(flops=18 * dots, bytes_accessed=64 * 16 * t * m, transcendentals=16 * t * f),
         name="group_step",
-    )(ids, xm, w1, w2, gain, d_out)
+    )(ids, xm, w1, w2, gain, *d_outs)
 
 
 def lookup_kernel(shard_rows, ids_smem, ids_vmem, table, out_hbm, got, rows, sem, out_sem):
@@ -562,13 +575,16 @@
     per = 32
     chunks = total // per
     r = lax.axis_index("tensor")
+    spread = (1 << (shard_rows.bit_length() - 1)) - 1
 
     def fetch(k):
         def some(j, carry):
             for u in range(8):
                 p = k * per + j * 8 + u
-                at = lax.div(lax.rem(ids_smem[lax.div(p, LANES), lax.rem(p, LANES)], shard_rows), 8)
-                pltpu.make_async_copy(table.at[at], got.at[p], sem.at[k]).start()
+                row = ids_smem[jnp.right_shift(p, 7), p & (LANES - 1)]
+                near = row - r * shard_rows
+                near = jnp.where((near >= 0) & (near < shard_rows), near, row & spread)
+                pltpu.make_async_copy(table.at[jnp.right_shift(near, 3)], got.at[p], sem.at[k]).start()
             return carry
 
         lax.fori_loop(0, per // 8, some, 0)
@@ -622,43 +638,83 @@
 RING = 6
 
 
-def table_kernel(tall, key_ref, first_ref, dw1_in, dw2_in, dx_in, out_hbm, dw1_o, dw2_o, dxb, dxf, w1, w2, ring, dx_sem, in_sem, w_sem, t_sem):
-    count, m = dxb.shape
-    f = w1.shape[1]
-    shift = count.bit_length() - 1
-    steps = out_hbm.shape[0] // tall
-    each = count // 8
-
-    def dx_piece(k):
-        at = pl.ds(pl.multiple_of(k * each, each), each)
-        return pltpu.make_async_copy(dx_in.at[at], dxb.at[at], dx_sem.at[k])
-
-    def w_pieces(i, back):
-        for src, buf, dst, n in ((dw1_in, w1, dw1_o, m // 8), (dw2_in, w2, dw2_o, f // 8)):
+def pass_kernel(dw1_in, dw2_in, dw1_o, dw2_o, w1, w2, in_sem, w_sem):
+    m, f = w1.shape
+
+    def pieces(i, back):
+        for k, (src, buf, dst, n) in enumerate(((dw1_in, w1, dw1_o, m // 8), (dw2_in, w2, dw2_o, f // 8))):
             at = pl.ds(pl.multiple_of(i * n, 8), n)
             if back:
                 yield pltpu.make_async_copy(buf.at[at], dst.at[at], w_sem)
             else:
-                yield pltpu.make_async_copy(src.at[at], buf.at[at], in_sem.at[i])
-
-    loop(0, 8, lambda k: dx_piece(k).start())
-
-    def w_fetch(i):
-        for cp in w_pieces(i, False):
+                yield pltpu.make_async_copy(src.at[at], buf.at[at], in_sem.at[2 * i + k])
+
+    def fetch(i):
+        for cp in pieces(i, False):
             cp.start()
 
-    loop(0, 8, w_fetch)
-
-    def widen_piece(k):
-        dx_piece(k).wait()
+    def put(i):
+        for come, go in zip(pieces(i, False), pieces(i, True)):
+            come.wait()
+            go.start()
+
+    loop(0, 8, fetch)
+    loop(0, 8, put)
+    pltpu.make_async_copy(w1, dw1_o, w_sem).wait()
+    pltpu.make_async_copy(w2, dw2_o, w_sem).wait()
+
+
+def pass_on_weights(dw1, dw2):
+    m, f = dw1.shape
+    any_ = pl.BlockSpec(memory_space=pl.ANY)
+    return pl.pallas_call(
+        pass_kernel,
+        out_shape=(jax.ShapeDtypeStruct((m, f), F32), jax.ShapeDtypeStruct((f, m), F32)),
+        in_specs=[any_, any_],
+        out_specs=[any_, any_],
+        scratch_shapes=[
+            pltpu.VMEM((m, f), F32), pltpu.VMEM((f, m), F32), pltpu.SemaphoreType.DMA((16,)), pltpu.SemaphoreType.DMA,
+        ],
+        compiler_params=pltpu.CompilerParams(vmem_limit_bytes=60 << 20),
+        cost_estimate=pl.CostEstimate(flops=8000 * m * f, bytes_accessed=16 * m * f, transcendentals=0),
+        name="pass_weights",
+    )(dw1, dw2)
+
+
+def table_kernel(tall, key_ref, first_ref, dx_in, far_own, far_across, far_partner, far_both, out_hbm, dxb, dxf, ring, dx_sem, t_sem):
+    count, _ = dxb.shape
+    t = count // 16
+    shift = count.bit_length() - 1
+    steps = out_hbm.shape[0] // tall
+    z, r = lax.axis_index("data"), lax.axis_index("tensor")
+    y, c = lax.div(r, 2), lax.rem(r, 2)
+    late = lax.div(z, 2)
+
+    def near(k):
+        at = pl.ds(pl.multiple_of(late * (4 * t) + k * (2 * t), t), 2 * t)
+        return at, pltpu.make_async_copy(dx_in.at[at], dxb.at[at], dx_sem.at[k])
+
+    def far(k, src, cc, yy):
+        at = pl.ds(pl.multiple_of((1 - late) * (12 * t) + cc * (2 * t) + yy * t, t), t)
+        return at, pltpu.make_async_copy(src, dxb.at[at], dx_sem.at[6 + k])
+
+    fars = ((far_own, c, y), (far_across, c, 1 - y), (far_partner, 1 - c, y), (far_both, 1 - c, 1 - y))
+    loop(0, 6, lambda k: near(k)[1].start())
+    for k, what in enumerate(fars):
+        far(k, *what)[1].start()
+
+    def widen_piece(at, cp):
+        cp.wait()
 
         def widen(i):
-            at = pl.ds(k * each + i, 16)
-            dxf[at, :] = dxb[at, :].astype(F32)
-
-        rows_loop(each, widen)
-
-    loop(0, 8, widen_piece)
+            rows = pl.ds(pl.multiple_of(at.start + i, 16), 16)
+            dxf[rows, :] = dxb[rows, :].astype(F32)
+
+        rows_loop(at.size, widen)
+
+    loop(0, 6, lambda k: widen_piece(*near(k)))
+    for k, what in enumerate(fars):
+        widen_piece(*far(k, *what))
 
     def tile_out(i):
         slot = lax.rem(i, RING)
@@ -680,58 +736,56 @@
         lax.fori_loop(low, first_ref[i + 1], add, key_ref[jnp.minimum(low, count - 1)])
         tile_out(i).start()
 
-        @pl.when(i < 8)
-        def _():
-            for cp in w_pieces(i, False):
-                cp.wait()
-            for cp in w_pieces(i, True):
-                cp.start()
-
     loop(0, steps, tile)
     loop(steps - RING, steps, lambda i: tile_out(i).wait())
-    pltpu.make_async_copy(w1, dw1_o, w_sem).wait()
-    pltpu.make_async_copy(w2, dw2_o, w_sem).wait()
-
-
-def table_grad(ordered, first, dx_all, dw1, dw2, shard_rows, tall):
+
+
+def table_grad(ordered, first, dx_all, fars, shard_rows, tall):
     count, m = dx_all.shape
-    f = dw1.shape[1]
     any_ = pl.BlockSpec(memory_space=pl.ANY)
-    sds = jax.ShapeDtypeStruct
     V, S = pltpu.VMEM, pltpu.SemaphoreType.DMA
     return pl.pallas_call(
         functools.partial(table_kernel, tall),
-        out_shape=(sds((shard_rows, m), F32), sds((m, f), F32), sds((f, m), F32)),
+        out_shape=jax.ShapeDtypeStruct((shard_rows, m), F32),
         grid_spec=pltpu.PrefetchScalarGridSpec(
             num_scalar_prefetch=2,
             grid=(1,),
-            in_specs=[any_, any_, any_],
-            out_specs=[any_, any_, any_],
+            in_specs=[any_] * 5,
+            out_specs=any_,
             scratch_shapes=[
-                V((count, m), BF16), V((count, m), F32), V((m, f), F32), V((f, m), F32), V((RING, tall, m), F32),
-                S((8,)), S((8,)), S, S((RING,)),
+                V((count, m), BF16), V((count, m), F32), V((RING, tall, m), F32), S((10,)), S((RING,)),
             ],
         ),
-        compiler_params=pltpu.CompilerParams(vmem_limit_bytes=67043328),
-        cost_estimate=pl.CostEstimate(flops=16 * count * m * f, bytes_accessed=4 * shard_rows * m + 16 * m * f, transcendentals=0),
+        compiler_params=pltpu.CompilerParams(vmem_limit_bytes=60 << 20),
+        cost_estimate=pl.CostEstimate(flops=16000 * shard_rows * m // 10, bytes_accessed=4 * shard_rows * m, transcendentals=0),
         name="table_grad",
-    )(ordered, first, dw1, dw2, dx_all)
+    )(ordered, first, dx_all, *fars)
 
 
 def solution(mesh):
     tok_spec = P(("pod", "data", "tensor"), None)
+
+    over_y, over_core = [(0, 2), (1, 3), (2, 0), (3, 1)], [(0, 1), (1, 0), (2, 3), (3, 2)]
 
     def per_device(token_ids, embed_table, norm_gain, w_in, w_out, d_out):
         shard_rows = embed_table.shape[0]
         tall = next(k for k in (160, 8) if shard_rows % k == 0)
         ids = token_ids.reshape(-1, LANES)
+        do_across = lax.ppermute(d_out, "tensor", over_y)
+        do_below = lax.ppermute(d_out, "data", [(0, 1), (1, 2), (2, 3)])
+        do_above = lax.ppermute(d_out, "data", [(1, 0), (2, 1), (3, 2)])
         masked = look_up(ids, embed_table)
         gain = norm_gain.reshape(-1, LANES)
-        base, ysum, ordered, first, dx_all, dw1, dw2 = run_group(ids, masked, w_in, w_out, gain, d_out, shard_rows, tall)
-        other = lax.ppermute(ysum, "tensor", [(0, 2), (1, 3), (2, 0), (3, 1)])
-        grad_table, grad_w_in, grad_w_out = table_grad(
-            ordered.reshape(-1), first.reshape(-1), dx_all, dw1, dw2, shard_rows, tall
+        base, ysum, ordered, first, dx_all, far, dw1, dw2 = run_group(
+            ids, masked, w_in, w_out, gain, (d_out, do_across, do_below, do_above), shard_rows, tall
         )
+        far_across = lax.ppermute(far, "tensor", over_y)
+        far_partner = lax.ppermute(far, "tensor", over_core)
+        other = lax.ppermute(ysum, "tensor", over_y)
+        grad_w_in, grad_w_out = pass_on_weights(dw1, dw2)
+        far_both = lax.ppermute(far_across, "tensor", over_core)
+        fars = (far, far_across, far_partner, far_both)
+        grad_table = table_grad(ordered.reshape(-1), first.reshape(-1), dx_all, fars, shard_rows, tall)
         return (base + other).astype(BF16), grad_table, grad_w_in, grad_w_out
 
     return jax.shard_map(

time: 218 us -> 236 us (1.083)
  waiting for transfers between devices: 0.01 us -> 22.8 us
  Pallas kernels: 213 us -> 199 us
  starting transfers between devices: 0.99 us -> 10.8 us
    ppermute x1 -> x7, waiting for transfers between devices: 0.01 us -> 22.8 us  [the longest x1 12.9 us: per_device(): far_across = lax.ppermute(far, 'tensor', over_y)]
    pallas_call x1, Pallas kernels: 162 us -> 148 us  [run_group(): pl.pallas_call(functools.partial(group_kernel, shard_rows, tall), out_sha...]
    ppermute x1 -> x7, starting transfers between devices: 0.99 us -> 10.8 us  [the longest x1 5.8 us: per_device(): do_below = lax.ppermute(d_out, 'data', [(0, 1), (1, 2), (2, 3)])]
    pallas_call x1 -> x2, Pallas kernels: 39 us -> 41.4 us  [the longest x1 25.3 us: table_grad(): pl.pallas_call(functools.partial(table_kernel, tall), out_shape=jax.Shape...]
  transfers between devices with their start and end apart: 1 -> 7, of which waited for: 0 -> 4; matrix products, arithmetic and copies ran while one was open for 0% -> 0% of each run, Pallas kernels for 18% -> 11%
where the time goes in v4:
time: 236 us; the launch traced here: 235 us
  Pallas kernels  199 us (84%)
  waiting for transfers between devices  22.8 us (10%)
  starting transfers between devices  10.8 us (5%)
    pallas_call x1, Pallas kernels, run_group(): pl.pallas_call(functools.partial(group_kernel, shard_rows, tall), out_sha...  148 us
    pallas_call x1, Pallas kernels, table_grad(): pl.pallas_call(functools.partial(table_kernel, tall), out_shape=jax.Shape...  25.3 us
    pallas_call x1, Pallas kernels, pass_on_weights(): pl.pallas_call(pass_kernel, out_shape=(jax.ShapeDtypeStruct((m, f), F32),...  16.1 us
    ppermute x1, waiting for transfers between devices, per_device(): far_across = lax.ppermute(far, 'tensor', over_y)  12.9 us
    pallas_call x1, Pallas kernels, look_up(): pl.pallas_call(functools.partial(lookup_kernel, shard_rows), out_shape=ja...  9.84 us
    ppermute x1, starting transfers between devices, per_device(): do_below = lax.ppermute(d_out, 'data', [(0, 1), (1, 2), (2, 3)])  5.8 us
    ppermute x1, waiting for transfers between devices, per_device(): other = lax.ppermute(ysum, 'tensor', over_y)  5.71 us
  transfers between devices with their start and end apart: 7, of which 4 were waited for; matrix products, arithmetic and copies ran while one was open for 0% of the time, Pallas kernels for 11%

profile of v4, /device:TPU:0, one launch (start us, length us, event | category | flops | bytes accessed | tf_op | source)
XLA Modules:
  0.0 235.3 jit_solution(3209806328735982376)
XLA Ops:
  0.6 5.8 %collective-permute-start.1 = (bf16[128,2048]{1,0:T(8,128)(2,1)}, bf16[128,2048]{1,0:T(8,128)(2,1)}, u32[]{:S(2)}, u32[]{:S(2)}) collective-permute-start(bf16[128,2048]{1,0:T(8,128)(2,1)} %do_hbm.1), channel_id=1, source_target_pairs={{0,4},{4,8},{8,12},{1,5},{5,9},{9,13},{2,6},{6,10},{10,14},{3,7},{... | collective-permute-start | bytes 1572872 | tf_op jit(solution)/shard_map/ppermute | solution.py:775
  6.4 1.5 collective-permute-start
  7.9 1.3 collective-permute-start.2
  9.2 9.8 %look_up.1.xm_hbm = bf16[512,2048]{1,0:T(8,128)(2,1)} custom-call(s32[4,128]{1,0:T(4,128)} %bitcast.6, s32[4,128]{1,0:T(4,128)} %bitcast.7, bf16[1000,8,2048]{2,1,0:T(8,128)(2,1)} %bitcast.5), custom_call_target="tpu_custom_call" | custom-call | flops 16777216 | bytes 20971520 | tf_op jit(solution)/shard_map/look_up/pallas_call | solution.py:623
  19.1 0.0 collective-permute-done.1.do_below
  19.1 1.0 collective-permute-done.do_across
  20.1 3.1 %collective-permute-done.2.do_above = bf16[128,2048]{1,0:T(8,128)(2,1)} collective-permute-done((bf16[128,2048]{1,0:T(8,128)(2,1)}, bf16[128,2048]{1,0:T(8,128)(2,1)}, u32[]{:S(2)}, u32[]{:S(2)}) %collective-permute-start.2) | collective-permute-done | bytes 524320 | tf_op jit(solution)/shard_map/ppermute | solution.py:776
  23.3 147.7 %group_step.1 = (f32[128,2048]{1,0:T(8,128)}, f32[128,2048]{1,0:T(8,128)}, s32[16,128]{1,0:T(8,128)}, s32[1,128]{1,0:T(1,128)}, bf16[2048,2048]{1,0:T(8,128)(2,1...) custom-call(s32[4,128]{1,0:T(4,128)} %bitcast.8, bf16[512,2048]{1,0:T(8,128)(2,1)} %look_up.1.xm_hbm, ...), custom_call_target="tpu_custom_call" | custom-call | flops 53150220288 | bytes 268435456 | tf_op jit(solution)/shard_map/group_step/pallas_call | solution.py:548
  171.0 1.6 collective-permute-start.4
  172.6 0.1 collective-permute-start.5
  172.7 0.5 collective-permute-start.3
  173.2 12.9 %collective-permute-done.4.far_across = bf16[128,2048]{1,0:T(8,128)(2,1)S(1)} collective-permute-done((bf16[128,2048]{1,0:T(8,128)(2,1)}, bf16[128,2048]{1,0:T(8,128)(2,1)S(1)}, u32[]{:S(2)}, u32[]{:S(2)}) %collective-permute-start.4) | collective-permute-done | bytes 524320 | tf_op jit(solution)/shard_map/ppermute | solution.py:782
  186.1 0.0 copy-start.1
  186.1 0.0 collective-permute-start.6
  186.1 0.0 copy-start
  186.1 16.1 %pass_weights.1 = (f32[2048,1408]{1,0:T(8,128)}, f32[1408,2048]{1,0:T(8,128)}) custom-call(f32[2048,1408]{1,0:T(8,128)} %get-tuple-element.20.dw1_in, f32[1408,2048]{1,0:T(8,128)} %get-tuple-element.21.dw2_in), custom_call_target="tpu_custom_call" | custom-call | flops 23068672000 | bytes 46137344 | tf_op jit(solution)/shard_map/pass_weights/pallas_call | solution.py:670
  202.2 0.0 copy-done.1
  202.2 5.7 %collective-permute-done.3 = f32[128,2048]{1,0:T(8,128)S(1)} collective-permute-done((f32[128,2048]{1,0:T(8,128)}, f32[128,2048]{1,0:T(8,128)S(1)}, u32[]{:S(2)}, u32[]{:S(2)}) %collective-permute-start.3) | collective-permute-done | bytes 1048608 | tf_op jit(solution)/shard_map/ppermute | solution.py:784
  208.0 0.0 copy-done
  208.0 0.9 add_convert_fusion
  208.9 0.0 collective-permute-done.5.far_partner
  208.9 0.0 copy-start.2
  208.9 0.0 collective-permute-done.6.far_both
  208.9 0.0 copy-start.3
  208.9 0.8 copy-done.2
  209.7 0.2 copy-done.3
  209.9 25.3 %table_grad.1 = f32[8000,2048]{1,0:T(8,128)} custom-call(s32[2048]{0:T(1024)} %bitcast.10, s32[128]{0:T(128)} %bitcast.11, bf16[2048,2048]{1,0:T(8,128)(2,1)} %get-tuple-element.18.dx_in, bf16[128,2048]{1,0:T(8,128)(2,1)} %get-tuple-element.19.far_own, bf16[128,2048]{1,0:T(8,128)(2,1)} %copy-done.1, bf16[128,2048]{1,0:T(8,128)(2,1)} %copy-done.2, ...), custom_call_target="tpu_custom_call" | custom-call | flops 26214400000 | bytes 65536000 | tf_op jit(solution)/shard_map/table_grad/pallas_call | solution.py:747
Async XLA Ops:
  0.6 18.5 %collective-permute-start.1 = (bf16[128,2048]{1,0:T(8,128)(2,1)}, bf16[128,2048]{1,0:T(8,128)(2,1)}, u32[]{:S(2)}, u32[]{:S(2)}) collective-permute-start(bf16[128,2048]{1,0:T(8,128)(2,1)} %do_hbm.1), channel_id=1, source_target_pairs={{0,4},{4,8},{8,12},{1,5},{5,9},{9,13},{2,6},{6,10},{10,14},{3,7},{... | collective-permute-start | bytes 1572872 | tf_op jit(solution)/shard_map/ppermute | solution.py:775
  6.4 13.7 %collective-permute-start = (bf16[128,2048]{1,0:T(8,128)(2,1)}, bf16[128,2048]{1,0:T(8,128)(2,1)}, u32[]{:S(2)}, u32[]{:S(2)}) collective-permute-start(bf16[128,2048]{1,0:T(8,128)(2,1)} %do_hbm.1), channel_id=1, source_target_pairs={{0,2},{1,3},{2,0},{3,1},{4,6},{5,7},{6,4},{7,5},{8,10},{9,11},{10,... | collective-permute-start | bytes 1572872 | tf_op jit(solution)/shard_map/ppermute | solution.py:774
  7.9 15.3 %collective-permute-start.2 = (bf16[128,2048]{1,0:T(8,128)(2,1)}, bf16[128,2048]{1,0:T(8,128)(2,1)}, u32[]{:S(2)}, u32[]{:S(2)}) collective-permute-start(bf16[128,2048]{1,0:T(8,128)(2,1)} %do_hbm.1), channel_id=1, source_target_pairs={{4,0},{8,4},{12,8},{5,1},{9,5},{13,9},{6,2},{10,6},{14,10},{7,3},{... | collective-permute-start | bytes 1572872 | tf_op jit(solution)/shard_map/ppermute | solution.py:776
  171.0 15.1 %collective-permute-start.4 = (bf16[128,2048]{1,0:T(8,128)(2,1)}, bf16[128,2048]{1,0:T(8,128)(2,1)S(1)}, u32[]{:S(2)}, u32[]{:S(2)}) collective-permute-start(bf16[128,2048]{1,0:T(8,128)(2,1)} %get-tuple-element.19.far_own), channel_id=1, source_target_pairs={{0,2},{1,3},{2,0},{3,1},{4,6},{5,7},{6,4},{7,5},{8,10},{9,11},{10,... | collective-permute-start | bytes 1572872 | tf_op jit(solution)/shard_map/ppermute | solution.py:782
  172.6 36.3 %collective-permute-start.5 = (bf16[128,2048]{1,0:T(8,128)(2,1)}, bf16[128,2048]{1,0:T(8,128)(2,1)S(1)}, u32[]{:S(2)}, u32[]{:S(2)}) collective-permute-start(bf16[128,2048]{1,0:T(8,128)(2,1)} %get-tuple-element.19.far_own), channel_id=1, source_target_pairs={{0,1},{1,0},{2,3},{3,2},{4,5},{5,4},{6,7},{7,6},{8,9},{9,8},{10,11... | collective-permute-start | bytes 1572872 | tf_op jit(solution)/shard_map/ppermute | solution.py:783
  172.7 35.2 %collective-permute-start.3 = (f32[128,2048]{1,0:T(8,128)}, f32[128,2048]{1,0:T(8,128)S(1)}, u32[]{:S(2)}, u32[]{:S(2)}) collective-permute-start(f32[128,2048]{1,0:T(8,128)} %get-tuple-element.15), channel_id=1, source_target_pairs={{0,2},{1,3},{2,0},{3,1},{4,6},{5,7},{6,4},{7,5},{8,10},{9,11},{10,... | collective-permute-start | bytes 3145736 | tf_op jit(solution)/shard_map/ppermute | solution.py:784
  186.1 16.2 %copy-start.1 = (bf16[128,2048]{1,0:T(8,128)(2,1)}, bf16[128,2048]{1,0:T(8,128)(2,1)S(1)}, u32[]{:S(2)}) copy-start(bf16[128,2048]{1,0:T(8,128)(2,1)S(1)} %collective-permute-done.4.far_across) | copy-start | bytes 1572868
  186.1 22.8 %collective-permute-start.6 = (bf16[128,2048]{1,0:T(8,128)(2,1)S(1)}, bf16[128,2048]{1,0:T(8,128)(2,1)S(1)}, u32[]{:S(2)}, u32[]{:S(2)}) collective-permute-start(bf16[128,2048]{1,0:T(8,128)(2,1)S(1)} %collective-permute-done.4.far_across), channel_id=1, source_target_pairs={{0,1},{1,0},{2,3},{3,2},{4,5},{5,4},{6,7},{7,6},{8,9},{9,8},{10,11... | collective-permute-start | bytes 1572872 | tf_op jit(solution)/shard_map/ppermute | solution.py:786
  186.1 21.9 %copy-start = (f32[128,2048]{1,0:T(8,128)S(1)}, f32[128,2048]{1,0:T(8,128)}, u32[]{:S(2)}) copy-start(f32[128,2048]{1,0:T(8,128)} %get-tuple-element.14) | copy-start | bytes 3145732
  208.9 0.8 copy-start.2
  208.9 1.0 copy-start.3

commit v5 on v4

--- a/solution.py
+++ b/solution.py
@@ -23,7 +23,7 @@
 R_XM, R_X, R_NO, R_PC, R_PY, N_R = 48, 52, 56, 60, 68, 72
 S_IDS, S_DZ, S_DY, S_DC, S_NZ, S_NC, S_XZ, S_XY, S_XC = 0, 3, 8, 12, 16, 26, 30, 40, 48
 S_XM, S_X, S_NO, S_PC, S_PY, N_S = 52, 56, 60, 64, 72, 76
-L_W1, L_W2, L_XM, L_DX, L_YS, L_YB, L_DW, L_DO, N_L = 0, 1, 2, 3, 4, 5, 6, 8, 12
+L_W1, L_W2, L_XM, L_DX, L_YS, L_YB, L_DW, L_DO, L_PF, N_L = 0, 1, 2, 3, 4, 5, 6, 8, 9, 11
 
 
 def loop(lo, hi, body):
@@ -95,8 +95,8 @@
     loop(0, lines, put)
 
 
-def group_kernel(shard_rows, tall, ids_ref, xm_hbm, w1_hbm, w2_hbm, g_ref, do_hbm, do_across, do_below, do_above,
-                 base_o, ysum_o, ord_o, first_o, dx_o, far_o, dw1_o, dw2_o,
+def group_kernel(shard_rows, tall, ids_ref, xm_hbm, w1_hbm, w2_hbm, g_ref, do_hbm,
+                 base_o, ysum_o, ord_o, first_o, dx_o, far_o, farx_o, dw1_o, dw2_o,
                  w1, w2, n, d, xm, xc, xy, hs, dus, pd, pf, rd, rf, yd, yb, dxo, idl, keys, place, ordered, first,
                  lsem, ssem, rsem):
     t, m = do_hbm.shape
@@ -156,17 +156,9 @@
     for k in range(3):
         pl.semaphore_signal(barrier, inc=1, device_id={"data": order[k]}, device_id_type=MESH)
 
-    def load_d(act):
-        act(local(do_hbm, blk(d, z, c, y), L_DO))
-        act(local(do_across, blk(d, z, c, 1 - y), L_DO + 1))
-        pl.when(z > 0)(lambda: act(local(do_below, blk(d, z - 1, c, y), L_DO + 2)))
-        pl.when(z < 3)(lambda: act(local(do_above, blk(d, z + 1, c, y), L_DO + 3)))
-
-    def local_wait(cp):
-        cp.wait()
-
+    own_d = blk(d, z, c, y)
+    local(do_hbm, own_d, L_DO).start()
     local(xm_hbm, xm, L_XM).start()
-    load_d(start)
     local(w1_hbm, w1, L_W1).start()
     local(w2_hbm, w2, L_W2).start()
     pl.semaphore_wait(barrier, 5)
@@ -174,6 +166,8 @@
     def piece(q):
         return pl.ds(q * tq, tq)
 
+    local(do_hbm, own_d, L_DO).wait()
+    along(own_d, own_d, S_DZ, R_DZ, start)
     local(xm_hbm, xm, L_XM).wait()
 
     def xm_part(q):
@@ -208,15 +202,14 @@
 
         rows_loop(tq, join)
         x_part(q).start()
-        if q == 0:
-            load_d(local_wait)
-
-            @pl.when(middle)
-            def _():
-                d_on(0)
-                d_on(1)
-
-    d_pair(z, start)
+    d_across(z, start)
+    d_got(0)
+
+    @pl.when(middle)
+    def _():
+        d_on(0)
+        d_got(1)
+        d_on(1)
 
     gain = jnp.concatenate([g_ref[pl.ds(i, 1), :] for i in range(m // LANES)], axis=1).astype(F32)
 
@@ -282,6 +275,8 @@
         arrived(n.at[pl.ds(row(z, 1 - c) + q * tq, tq)], R_NO + q)
     local(w1_hbm, w1, L_W1).wait()
     hidden(z, pf)
+    arrived(blk(d, z, c, 1 - y), R_DY + z)
+    d_pair(z, start)
     arrived(duo(d, z, 1 - c), R_DC + z)
     local(w2_hbm, w2, L_W2).wait()
     grad_hidden(z, pf)
@@ -384,6 +379,9 @@
         here = dx_part(order[k], y, h)
         return (here, here) if k == 1 else (here if k == 0 else far_part(h), far_part(h))
 
+    def far_out(act):
+        act(remote(far_part(0), farx_o, S_XY + order[2], R_XY + order[2], across))
+
     def dx_across(zz, src, h, act):
         act(remote(src, dx_part(zz, y, h), S_XY + 4 * h + zz, R_XY + 4 * h + zz, across))
 
@@ -402,6 +400,8 @@
                 pass_on(k, dx_next(k, h), S_XZ + 5 * h, R_XZ + 4 * h, start)
             if k < 2:
                 dx_across(zz, dx_part(zz, y, h), h, start)
+            elif h == 0:
+                far_out(start)
 
     def dx_hand(zz):
         for h in range(2):
@@ -431,6 +431,7 @@
     y_keep.start()
     for q in range(PQ):
         part_pair(pd, rd, 0, q).wait_send()
+        part_pair(pf, rf, 1, q).wait_send()
 
     def unit(k):
         zz = order[k]
@@ -458,41 +459,70 @@
         dx_got(0, True)
         dx_got(1, True)
 
+    tw = 2 * t
+    n1 = m // tw
+    late_rows = pl.ds(row(order[2], 0), 4 * t)
+    early_rows = pl.ds(pl.multiple_of(half * (4 * t), 4 * t), 12 * t)
+
+    def w_at(i):
+        return pl.ds(pl.multiple_of(i * tw, tw), tw)
+
+    def slot(s):
+        return pf.at[pl.ds(s * tw, tw), pl.ds(0, f)]
+
+    def w1_tile(i, s, back):
+        here, there = slot(s), dw1_o.at[w_at(i)]
+        return local(here, there, L_PF + s) if back else local(there, here, L_PF + s)
+
+    def early(j):
+        for s in range(2):
+            i = 2 * j + s
+            pl.when(j >= 1)(lambda s=s, i=i: w1_tile(i - 2, s, True).wait())
+            slot(s)[...] = lax.dot_general(n[early_rows, w_at(i)], dus[early_rows, :], TN, preferred_element_type=F32)
+            w1_tile(i, s, True).start()
+
+    loop(0, n1 // 2, early)
+    for s in range(2):
+        w1_tile(n1 - 2 + s, s, True).wait()
     pl.when(end)(lambda: n_rest(2, False))
     unit(2)
 
-    tw = 2 * t
-
-    def stage(i, width):
-        return pd.at[pl.ds(pl.multiple_of(lax.rem(i, 2) * tw, tw), tw), pl.ds(0, width)]
-
-    def flush(i, dst):
-        return local(stage(i, dst.shape[1]), dst.at[pl.ds(pl.multiple_of(i * tw, tw), tw)], L_DW + lax.rem(i, 2))
-
-    def weight_tile(i, lhs, rhs, dst):
-        @pl.when(i >= 2)
-        def _():
-            flush(i - 2, dst).wait()
-
-        at = pl.ds(pl.multiple_of(i * tw, tw), tw)
-        stage(i, dst.shape[1])[...] = lax.dot_general(lhs[:, at], rhs[...], TN, preferred_element_type=F32)
-        flush(i, dst).start()
-
-    n1, n2 = m // tw, f // tw
+    def both(j):
+        for s in range(2):
+            i = 2 * j + s
+            pl.when(j >= 1)(lambda s=s, i=i: w1_tile(i - 2, s, True).wait())
+            w1_tile(i, s, False).start()
+        weight_tile(j)
+        for s in range(2):
+            i = 2 * j + s
+            w1_tile(i, s, False).wait()
+            slot(s)[...] += lax.dot_general(n[late_rows, w_at(i)], dus[late_rows, :], TN, preferred_element_type=F32)
+            w1_tile(i, s, True).start()
+
+    def weight_tile(i):
+        pl.when(i >= 2)(lambda: flush(i - 2).wait())
+        stage(i)[...] = lax.dot_general(hs[:, w_at(i)], d[...], TN, preferred_element_type=F32)
+        flush(i).start()
+
+    def stage(i):
+        return pd.at[pl.ds(pl.multiple_of(lax.rem(i, 2) * tw, tw), tw)]
+
+    def flush(i):
+        return local(stage(i), dw2_o.at[w_at(i)], L_DW + lax.rem(i, 2))
+
+    n2, paired = f // tw, n1 // 2
+    steps = min(n2, paired)
     pl.when(end)(lambda: dx_got(0, False))
-    loop(0, n1 // 2, lambda i: weight_tile(i, n, dus, dw1_o))
+    pl.when(middle)(lambda: dx_got(2, True))
+    loop(0, steps // 2, both)
     pl.when(end)(lambda: dx_got(1, False))
-    pl.when(middle)(lambda: dx_got(2, True))
-    loop(n1 // 2, n1, lambda i: weight_tile(i, n, dus, dw1_o))
-    for i in (n1 - 2, n1 - 1):
-        flush(i, dw1_o).wait()
+    loop(steps // 2, steps, both)
     local(dxo, blk(dx_o, z, c, y), L_DX).wait()
     dx_hand(z)
     dx_hand(order[0])
-    loop(0, n2 // 2 + 1, lambda i: weight_tile(i, hs, d, dw2_o))
-    loop(n2 // 2 + 1, n2, lambda i: weight_tile(i, hs, d, dw2_o))
+    loop(steps, n2, weight_tile)
     for i in (n2 - 2, n2 - 1):
-        flush(i, dw2_o).wait()
+        flush(i).wait()
     if f % tw:
         rest = pd.at[pl.ds(0, f % tw)]
         rest[...] = lax.dot_general(hs[:, n2 * tw :], d[...], TN, preferred_element_type=F32)
@@ -502,13 +532,16 @@
     pl.when(end)(lambda: dx_got(2, False))
     if f % tw:
         last.wait()
+    for s in range(2):
+        w1_tile(2 * paired - 2 + s, s, True).wait()
 
     y_send.wait()
     y_keep.wait()
+    along(own_d, own_d, S_DZ, R_DZ, sent)
     for zz in (z, *order):
+        d_across(zz, sent)
         d_pair(zz, sent)
     for k in range(3):
-        d_across(order[k], sent)
         n_pair(order[k], sent)
         remote(ids_ref, idl.at[z], S_IDS + k, R_IDS + z, {"data": order[k]}).wait_send()
     dx_along(sent)
@@ -530,15 +563,16 @@
         xm_part(q).wait_send()
         n_own(q, sent)
     for q in range(PQ):
-        part_pair(pf, rf, 1, q).wait_send()
         part_across(q).wait_send()
+    arrived(farx_o, R_XY + order[2])
+    far_out(sent)
     for zz in (z, *order[:2]):
         arrived(duo(dx_o, zz, 1 - c), R_XC + zz)
         dx_pair(zz, sent)
 
 
-def run_group(ids, xm, w1, w2, gain, d_outs, shard_rows, tall):
-    t, m = d_outs[0].shape
+def run_group(ids, xm, w1, w2, gain, d_out, shard_rows, tall):
+    t, m = d_out.shape
     f = w1.shape[1]
     lines = 4 * ids.shape[0]
     any_, vmem = pl.BlockSpec(memory_space=pl.ANY), pl.BlockSpec(memory_space=pltpu.VMEM)
@@ -549,10 +583,10 @@
         functools.partial(group_kernel, shard_rows, tall),
         out_shape=(
             sds((t, m), F32), sds((t, m), F32), sds((lines, LANES), I32), sds((1, LANES), I32), sds((16 * t, m), BF16),
-            sds((t, m), BF16), sds((m, f), F32), sds((f, m), F32),
+            sds((t, m), BF16), sds((t // 2, m), BF16), sds((m, f), F32), sds((f, m), F32),
         ),
-        in_specs=[vmem, any_, any_, any_, vmem, any_, any_, any_, any_],
-        out_specs=(any_, any_, vmem, vmem, any_, any_, any_, any_),
+        in_specs=[vmem, any_, any_, any_, vmem, any_],
+        out_specs=(any_, any_, vmem, vmem, any_, any_, any_, any_, any_),
         scratch_shapes=[
             V((m, f), BF16), V((f, m), BF16), V((16 * t, m), BF16), V((16 * t, m), BF16),
             V((4 * t, m), BF16), V((2 * t, m), BF16), V((2 * t, m), BF16),
@@ -566,7 +600,7 @@
         compiler_params=pltpu.CompilerParams(collective_id=0, has_side_effects=True, vmem_limit_bytes=67043328),
         cost_estimate=pl.CostEstimate(flops=18 * dots, bytes_accessed=64 * 16 * t * m, transcendentals=16 * t * f),
         name="group_step",
-    )(ids, xm, w1, w2, gain, *d_outs)
+    )(ids, xm, w1, w2, gain, d_out)
 
 
 def lookup_kernel(shard_rows, ids_smem, ids_vmem, table, out_hbm, got, rows, sem, out_sem):
@@ -638,50 +672,47 @@
 RING = 6
 
 
-def pass_kernel(dw1_in, dw2_in, dw1_o, dw2_o, w1, w2, in_sem, w_sem):
-    m, f = w1.shape
-
-    def pieces(i, back):
-        for k, (src, buf, dst, n) in enumerate(((dw1_in, w1, dw1_o, m // 8), (dw2_in, w2, dw2_o, f // 8))):
-            at = pl.ds(pl.multiple_of(i * n, 8), n)
-            if back:
-                yield pltpu.make_async_copy(buf.at[at], dst.at[at], w_sem)
-            else:
-                yield pltpu.make_async_copy(src.at[at], buf.at[at], in_sem.at[2 * i + k])
+def pass_pieces(src, buf, dst, in_sem, out_sem):
+    rows = src.shape[0] // 8
 
     def fetch(i):
-        for cp in pieces(i, False):
-            cp.start()
+        at = pl.ds(pl.multiple_of(i * rows, 8), rows)
+        return pltpu.make_async_copy(src.at[at], buf.at[at], in_sem.at[i])
 
     def put(i):
-        for come, go in zip(pieces(i, False), pieces(i, True)):
-            come.wait()
-            go.start()
-
+        at = pl.ds(pl.multiple_of(i * rows, 8), rows)
+        return pltpu.make_async_copy(buf.at[at], dst.at[at], out_sem)
+
+    def step(i):
+        fetch(i).wait()
+        put(i).start()
+
+    return lambda i: fetch(i).start(), step, lambda: pltpu.make_async_copy(buf, dst, out_sem).wait()
+
+
+def pass_kernel(src, dst, buf, in_sem, out_sem):
+    fetch, step, drain = pass_pieces(src, buf, dst, in_sem, out_sem)
     loop(0, 8, fetch)
-    loop(0, 8, put)
-    pltpu.make_async_copy(w1, dw1_o, w_sem).wait()
-    pltpu.make_async_copy(w2, dw2_o, w_sem).wait()
-
-
-def pass_on_weights(dw1, dw2):
-    m, f = dw1.shape
+    loop(0, 8, step)
+    drain()
+
+
+def pass_on(w):
     any_ = pl.BlockSpec(memory_space=pl.ANY)
     return pl.pallas_call(
         pass_kernel,
-        out_shape=(jax.ShapeDtypeStruct((m, f), F32), jax.ShapeDtypeStruct((f, m), F32)),
-        in_specs=[any_, any_],
-        out_specs=[any_, any_],
-        scratch_shapes=[
-            pltpu.VMEM((m, f), F32), pltpu.VMEM((f, m), F32), pltpu.SemaphoreType.DMA((16,)), pltpu.SemaphoreType.DMA,
-        ],
+        out_shape=jax.ShapeDtypeStruct(w.shape, w.dtype),
+        in_specs=[any_],
+        out_specs=any_,
+        scratch_shapes=[pltpu.VMEM(w.shape, w.dtype), pltpu.SemaphoreType.DMA((8,)), pltpu.SemaphoreType.DMA],
         compiler_params=pltpu.CompilerParams(vmem_limit_bytes=60 << 20),
-        cost_estimate=pl.CostEstimate(flops=8000 * m * f, bytes_accessed=16 * m * f, transcendentals=0),
+        cost_estimate=pl.CostEstimate(flops=8000 * w.size, bytes_accessed=8 * w.size, transcendentals=0),
         name="pass_weights",
-    )(dw1, dw2)
-
-
-def table_kernel(tall, key_ref, first_ref, dx_in, far_own, far_across, far_partner, far_both, out_hbm, dxb, dxf, ring, dx_sem, t_sem):
+    )(w)
+
+
+def table_kernel(tall, key_ref, first_ref, w_in, dx_in, far_own, far_x0, far_x1, far_partner, far_b0, far_b1,
+                 out_hbm, w_out, dxb, dxf, ring, w_buf, dx_sem, t_sem, in_sem, out_sem):
     count, _ = dxb.shape
     t = count // 16
     shift = count.bit_length() - 1
@@ -689,19 +720,25 @@
     z, r = lax.axis_index("data"), lax.axis_index("tensor")
     y, c = lax.div(r, 2), lax.rem(r, 2)
     late = lax.div(z, 2)
+    w_fetch, w_step, w_drain = pass_pieces(w_in, w_buf, w_out, in_sem, out_sem)
 
     def near(k):
         at = pl.ds(pl.multiple_of(late * (4 * t) + k * (2 * t), t), 2 * t)
         return at, pltpu.make_async_copy(dx_in.at[at], dxb.at[at], dx_sem.at[k])
 
-    def far(k, src, cc, yy):
-        at = pl.ds(pl.multiple_of((1 - late) * (12 * t) + cc * (2 * t) + yy * t, t), t)
+    def far(k, src, cc, yy, h):
+        n = src.shape[0]
+        at = pl.ds(pl.multiple_of((1 - late) * (12 * t) + cc * (2 * t) + yy * t + h * n, n), n)
         return at, pltpu.make_async_copy(src, dxb.at[at], dx_sem.at[6 + k])
 
-    fars = ((far_own, c, y), (far_across, c, 1 - y), (far_partner, 1 - c, y), (far_both, 1 - c, 1 - y))
+    fars = (
+        (far_own, c, y, 0), (far_partner, 1 - c, y, 0), (far_x0, c, 1 - y, 0), (far_b0, 1 - c, 1 - y, 0),
+        (far_x1, c, 1 - y, 1), (far_b1, 1 - c, 1 - y, 1),
+    )
     loop(0, 6, lambda k: near(k)[1].start())
     for k, what in enumerate(fars):
         far(k, *what)[1].start()
+    loop(0, 8, w_fetch)
 
     def widen_piece(at, cp):
         cp.wait()
@@ -735,31 +772,34 @@
         low = first_ref[i]
         lax.fori_loop(low, first_ref[i + 1], add, key_ref[jnp.minimum(low, count - 1)])
         tile_out(i).start()
+        pl.when(i < 8)(lambda: w_step(i))
 
     loop(0, steps, tile)
     loop(steps - RING, steps, lambda i: tile_out(i).wait())
-
-
-def table_grad(ordered, first, dx_all, fars, shard_rows, tall):
+    w_drain()
+
+
+def table_grad(ordered, first, w, dx_all, fars, shard_rows, tall):
     count, m = dx_all.shape
     any_ = pl.BlockSpec(memory_space=pl.ANY)
     V, S = pltpu.VMEM, pltpu.SemaphoreType.DMA
     return pl.pallas_call(
         functools.partial(table_kernel, tall),
-        out_shape=jax.ShapeDtypeStruct((shard_rows, m), F32),
+        out_shape=(jax.ShapeDtypeStruct((shard_rows, m), F32), jax.ShapeDtypeStruct(w.shape, F32)),
         grid_spec=pltpu.PrefetchScalarGridSpec(
             num_scalar_prefetch=2,
             grid=(1,),
-            in_specs=[any_] * 5,
-            out_specs=any_,
+            in_specs=[any_] * 8,
+            out_specs=[any_] * 2,
             scratch_shapes=[
-                V((count, m), BF16), V((count, m), F32), V((RING, tall, m), F32), S((10,)), S((RING,)),
+                V((count, m), BF16), V((count, m), F32), V((RING, tall, m), F32), V(w.shape, F32),
+                S((12,)), S((RING,)), S((8,)), S,
             ],
         ),
         compiler_params=pltpu.CompilerParams(vmem_limit_bytes=60 << 20),
-        cost_estimate=pl.CostEstimate(flops=16000 * shard_rows * m // 10, bytes_accessed=4 * shard_rows * m, transcendentals=0),
+        cost_estimate=pl.CostEstimate(flops=1600 * shard_rows * m, bytes_accessed=4 * shard_rows * m, transcendentals=0),
         name="table_grad",
-    )(ordered, first, dx_all, *fars)
+    )(ordered, first, w, dx_all, *fars)
 
 
 def solution(mesh):
@@ -771,21 +811,20 @@
         shard_rows = embed_table.shape[0]
         tall = next(k for k in (160, 8) if shard_rows % k == 0)
         ids = token_ids.reshape(-1, LANES)
-        do_across = lax.ppermute(d_out, "tensor", over_y)
-        do_below = lax.ppermute(d_out, "data", [(0, 1), (1, 2), (2, 3)])
-        do_above = lax.ppermute(d_out, "data", [(1, 0), (2, 1), (3, 2)])
         masked = look_up(ids, embed_table)
         gain = norm_gain.reshape(-1, LANES)
-        base, ysum, ordered, first, dx_all, far, dw1, dw2 = run_group(
-            ids, masked, w_in, w_out, gain, (d_out, do_across, do_below, do_above), shard_rows, tall
+        base, ysum, ordered, first, dx_all, far, far_x0, dw1, dw2 = run_group(
+            ids, masked, w_in, w_out, gain, d_out, shard_rows, tall
         )
-        far_across = lax.ppermute(far, "tensor", over_y)
+        late = far[far.shape[0] // 2 :]
+        far_x1 = lax.ppermute(late, "tensor", over_y)
         far_partner = lax.ppermute(far, "tensor", over_core)
+        far_b0 = lax.ppermute(far_x0, "tensor", over_core)
         other = lax.ppermute(ysum, "tensor", over_y)
-        grad_w_in, grad_w_out = pass_on_weights(dw1, dw2)
-        far_both = lax.ppermute(far_across, "tensor", over_core)
-        fars = (far, far_across, far_partner, far_both)
-        grad_table = table_grad(ordered.reshape(-1), first.reshape(-1), dx_all, fars, shard_rows, tall)
+        grad_w_in = pass_on(dw1)
+        far_b1 = lax.ppermute(far_x1, "tensor", over_core)
+        fars = (far, far_x0, far_x1, far_partner, far_b0, far_b1)
+        grad_table, grad_w_out = table_grad(ordered.reshape(-1), first.reshape(-1), dw2, dx_all, fars, shard_rows, tall)
         return (base + other).astype(BF16), grad_table, grad_w_in, grad_w_out
 
     return jax.shard_map(

time: 236 us -> 227 us (0.962)
  waiting for transfers between devices: 22.8 us -> 6.47 us
  Pallas kernels: 199 us -> 214 us
  starting transfers between devices: 10.8 us -> 2.6 us
    pallas_call x1, Pallas kernels: 148 us -> 164 us  [run_group(): pl.pallas_call(functools.partial(group_kernel, shard_rows, tall), out_sha...]
    ppermute x5 -> x3, waiting for transfers between devices: 17.1 us -> 6.46 us  [the longest x1 6.46 us: per_device(): far_x1 = lax.ppermute(late, 'tensor', over_y)]
    ppermute x5 -> x3, starting transfers between devices: 10.2 us -> 1 us  [the longest x1 0.51 us: per_device(): far_b0 = lax.ppermute(far_x0, 'tensor', over_core)]
    ppermute x1, waiting for transfers between devices: 5.71 us -> 0.01 us  [per_device(): other = lax.ppermute(ysum, 'tensor', over_y)]
  transfers between devices with their start and end apart: 7 -> 5, of which waited for: 4 -> 1; matrix products, arithmetic and copies ran while one was open for 0% -> 0% of each run, Pallas kernels for 11% -> 17%
where the time goes in v5:
time: 227 us; the launch traced here: 226 us
  Pallas kernels  214 us (94%)
  waiting for transfers between devices  6.47 us (3%)
  starting transfers between devices  2.6 us (1%)
    pallas_call x1, Pallas kernels, run_group(): pl.pallas_call(functools.partial(group_kernel, shard_rows, tall), out_sha...  164 us
    pallas_call x1, Pallas kernels, table_grad(): pl.pallas_call(functools.partial(table_kernel, tall), out_shape=(jax.Shap...  30.7 us
    pallas_call x1, Pallas kernels, look_up(): pl.pallas_call(functools.partial(lookup_kernel, shard_rows), out_shape=ja...  9.84 us
    pallas_call x1, Pallas kernels, pass_on(): pl.pallas_call(pass_kernel, out_shape=jax.ShapeDtypeStruct(w.shape, w.dty...  8.76 us
    ppermute x1, waiting for transfers between devices, per_device(): far_x1 = lax.ppermute(late, 'tensor', over_y)  6.46 us
  transfers between devices with their start and end apart: 5, of which 1 were waited for; matrix products, arithmetic and copies ran while one was open for 0% of the time, Pallas kernels for 17%

profile of v5, /device:TPU:0, one launch (start us, length us, event | category | flops | bytes accessed | tf_op | source)
XLA Modules:
  0.0 226.3 jit_solution(13732061456950529436)
XLA Ops:
  0.6 9.8 %look_up.1.xm_hbm = bf16[512,2048]{1,0:T(8,128)(2,1)} custom-call(s32[4,128]{1,0:T(4,128)} %bitcast.6, s32[4,128]{1,0:T(4,128)} %bitcast.7, bf16[1000,8,2048]{2,1,0:T(8,128)(2,1)} %bitcast.5), custom_call_target="tpu_custom_call" | custom-call | flops 16777216 | bytes 20971520 | tf_op jit(solution)/shard_map/look_up/pallas_call | solution.py:657
  10.5 164.4 %group_step.1 = (f32[128,2048]{1,0:T(8,128)}, f32[128,2048]{1,0:T(8,128)}, s32[16,128]{1,0:T(8,128)}, s32[1,128]{1,0:T(1,128)}, bf16[2048,2048]{1,0:T(8,128)(2,1...) custom-call(s32[4,128]{1,0:T(4,128)} %bitcast.8, ...), custom_call_target="tpu_custom_call" | custom-call | flops 53150220288 | bytes 268435456 | tf_op jit(solution)/shard_map/group_step/pallas_call | solution.py:582
  174.9 1.0 slice.3
  175.8 0.5 collective-permute-start.1
  176.3 0.0 collective-permute-start.2
  176.3 0.5 collective-permute-start.3
  176.8 1.6 collective-permute-start
  178.4 6.5 %collective-permute-done.1.far_x1 = bf16[64,2048]{1,0:T(8,128)(2,1)S(1)} collective-permute-done((bf16[64,2048]{1,0:T(8,128)(2,1)S(1)}, bf16[64,2048]{1,0:T(8,128)(2,1)S(1)}, u32[]{:S(2)}, u32[]{:S(2)}) %collective-permute-start.1) | collective-permute-done | bytes 262176 | tf_op jit(solution)/shard_map/ppermute | solution.py:820
  184.9 0.0 copy-start.2
  184.9 0.0 collective-permute-start.4
  184.9 8.8 %pass_weights.1 = f32[2048,1408]{1,0:T(8,128)} custom-call(f32[2048,1408]{1,0:T(8,128)} %get-tuple-element.24.src), custom_call_target="tpu_custom_call" | custom-call | flops 23068672000 | bytes 23068672 | tf_op jit(solution)/shard_map/pass_weights/pallas_call | solution.py:702
  193.7 0.0 copy-done.2
  193.7 0.0 collective-permute-done.3.far_b0
  193.7 0.0 copy-start.3
  193.7 0.0 collective-permute-done.4.far_b1
  193.7 0.0 copy-start.4
  193.7 0.0 collective-permute-done.2.far_partner
  193.7 0.0 copy-start.1
  193.7 0.6 copy-done.3
  194.4 0.1 copy-done.4
  194.5 0.2 copy-done.1
  194.6 0.0 copy-start
  194.6 30.7 %table_grad.1 = (f32[8000,2048]{1,0:T(8,128)}, f32[1408,2048]{1,0:T(8,128)}) custom-call(s32[2048]{0:T(1024)} %bitcast.10, s32[128]{0:T(128)} %bitcast.11, f32[1408,2048]{1,0:T(8,128)} %get-tuple-element.19.w_in, bf16[2048,2048]{1,0:T(8,128)(2,1)} %get-tuple-element.20.dx_in, bf16[128,2048]{1,0:T(8,128)(2,1)} %get-tuple-element.21.far_own, ...), custom_call_target="tpu_custom_call" | custom-call | flops 26214400000 | bytes 65536000 | tf_op jit(solution)/shard_map/table_grad/pallas_call | solution.py:786
  225.3 0.0 collective-permute-done
  225.3 0.0 copy-done
  225.4 0.9 add_convert_fusion
Async XLA Ops:
  175.8 9.1 %collective-permute-start.1 = (bf16[64,2048]{1,0:T(8,128)(2,1)S(1)}, bf16[64,2048]{1,0:T(8,128)(2,1)S(1)}, u32[]{:S(2)}, u32[]{:S(2)}) collective-permute-start(bf16[64,2048]{1,0:T(8,128)(2,1)S(1)} %slice.3), channel_id=1, source_target_pairs={{0,2},{1,3},{2,0},{3,1},{4,6},{5,7},{6,4},{7,5},{8,10},{9,11},{10,... | collective-permute-start | bytes 786440 | tf_op jit(solution)/shard_map/ppermute | solution.py:820
  176.3 17.4 %collective-permute-start.2 = (bf16[128,2048]{1,0:T(8,128)(2,1)}, bf16[128,2048]{1,0:T(8,128)(2,1)S(1)}, u32[]{:S(2)}, u32[]{:S(2)}) collective-permute-start(bf16[128,2048]{1,0:T(8,128)(2,1)} %get-tuple-element.21.far_own), channel_id=1, source_target_pairs={{0,1},{1,0},{2,3},{3,2},{4,5},{5,4},{6,7},{7,6},{8,9},{9,8},{10,11... | collective-permute-start | bytes 1572872 | tf_op jit(solution)/shard_map/ppermute | solution.py:821
  176.3 17.4 %collective-permute-start.3 = (bf16[64,2048]{1,0:T(8,128)(2,1)}, bf16[64,2048]{1,0:T(8,128)(2,1)S(1)}, u32[]{:S(2)}, u32[]{:S(2)}) collective-permute-start(bf16[64,2048]{1,0:T(8,128)(2,1)} %get-tuple-element.22.far_x0), channel_id=1, source_target_pairs={{0,1},{1,0},{2,3},{3,2},{4,5},{5,4},{6,7},{7,6},{8,9},{9,8},{10,11... | collective-permute-start | bytes 786440 | tf_op jit(solution)/shard_map/ppermute | solution.py:822
  176.8 48.5 %collective-permute-start = (f32[128,2048]{1,0:T(8,128)}, f32[128,2048]{1,0:T(8,128)S(1)}, u32[]{:S(2)}, u32[]{:S(2)}) collective-permute-start(f32[128,2048]{1,0:T(8,128)} %get-tuple-element.16), channel_id=1, source_target_pairs={{0,2},{1,3},{2,0},{3,1},{4,6},{5,7},{6,4},{7,5},{8,10},{9,11},{10,... | collective-permute-start | bytes 3145736 | tf_op jit(solution)/shard_map/ppermute | solution.py:823
  184.9 8.8 %copy-start.2 = (bf16[64,2048]{1,0:T(8,128)(2,1)}, bf16[64,2048]{1,0:T(8,128)(2,1)S(1)}, u32[]{:S(2)}) copy-start(bf16[64,2048]{1,0:T(8,128)(2,1)S(1)} %collective-permute-done.1.far_x1) | copy-start | bytes 786436
  184.9 8.8 %collective-permute-start.4 = (bf16[64,2048]{1,0:T(8,128)(2,1)S(1)}, bf16[64,2048]{1,0:T(8,128)(2,1)S(1)}, u32[]{:S(2)}, u32[]{:S(2)}) collective-permute-start(bf16[64,2048]{1,0:T(8,128)(2,1)S(1)} %collective-permute-done.1.far_x1), channel_id=1, source_target_pairs={{0,1},{1,0},{2,3},{3,2},{4,5},{5,4},{6,7},{7,6},{8,9},{9,8},{10,11... | collective-permute-start | bytes 786440 | tf_op jit(solution)/shard_map/ppermute | solution.py:825
  193.7 0.7 copy-start.3
  193.7 0.8 copy-start.4
  193.7 0.9 copy-start.1
  194.6 30.7 %copy-start = (f32[128,2048]{1,0:T(8,128)S(1)}, f32[128,2048]{1,0:T(8,128)}, u32[]{:S(2)}) copy-start(f32[128,2048]{1,0:T(8,128)} %get-tuple-element.15) | copy-start | bytes 3145732

commit v6 on v5

--- a/solution.py
+++ b/solution.py
@@ -96,7 +96,7 @@
 
 
 def group_kernel(shard_rows, tall, ids_ref, xm_hbm, w1_hbm, w2_hbm, g_ref, do_hbm,
-                 base_o, ysum_o, ord_o, first_o, dx_o, far_o, farx_o, dw1_o, dw2_o,
+                 base_o, ysum_o, ord_o, first_o, dx_o, far_o, dw1_o, dw2_o,
                  w1, w2, n, d, xm, xc, xy, hs, dus, pd, pf, rd, rf, yd, yb, dxo, idl, keys, place, ordered, first,
                  lsem, ssem, rsem):
     t, m = do_hbm.shape
@@ -166,6 +166,10 @@
     def piece(q):
         return pl.ds(q * tq, tq)
 
+    for k in range(3):
+        remote(ids_ref, idl.at[z], S_IDS + k, R_IDS + z, {"data": order[k]}).start()
+    idl[z] = ids_ref[...]
+
     local(do_hbm, own_d, L_DO).wait()
     along(own_d, own_d, S_DZ, R_DZ, start)
     local(xm_hbm, xm, L_XM).wait()
@@ -190,9 +194,6 @@
 
     for q in range(XQ):
         xm_part(q).start()
-    for k in range(3):
-        remote(ids_ref, idl.at[z], S_IDS + k, R_IDS + z, {"data": order[k]}).start()
-    idl[z] = ids_ref[...]
     for q in range(XQ):
         arrived(xc.at[piece(q)], R_XM + q)
 
@@ -203,6 +204,12 @@
         rows_loop(tq, join)
         x_part(q).start()
     d_across(z, start)
+
+    for k in range(3):
+        arrived(idl.at[order[k]], R_IDS + order[k])
+    sort_keys(idl, keys, place, ordered, first, shard_rows, tall, r * shard_rows)
+    ord_o[...] = ordered[...].astype(I32)
+    first_o[...] = first[...].astype(I32)
     d_got(0)
 
     @pl.when(middle)
@@ -344,12 +351,6 @@
         n_on(1)
         n_pair(order[1], start)
 
-    for k in range(3):
-        arrived(idl.at[order[k]], R_IDS + order[k])
-    sort_keys(idl, keys, place, ordered, first, shard_rows, tall, r * shard_rows)
-    ord_o[...] = ordered[...].astype(I32)
-    first_o[...] = first[...].astype(I32)
-
     for q in range(PQ):
         arrived(yd.at[:, cols(q)], R_PY + q)
 
@@ -379,9 +380,6 @@
         here = dx_part(order[k], y, h)
         return (here, here) if k == 1 else (here if k == 0 else far_part(h), far_part(h))
 
-    def far_out(act):
-        act(remote(far_part(0), farx_o, S_XY + order[2], R_XY + order[2], across))
-
     def dx_across(zz, src, h, act):
         act(remote(src, dx_part(zz, y, h), S_XY + 4 * h + zz, R_XY + 4 * h + zz, across))
 
@@ -400,8 +398,6 @@
                 pass_on(k, dx_next(k, h), S_XZ + 5 * h, R_XZ + 4 * h, start)
             if k < 2:
                 dx_across(zz, dx_part(zz, y, h), h, start)
-            elif h == 0:
-                far_out(start)
 
     def dx_hand(zz):
         for h in range(2):
@@ -564,8 +560,6 @@
         n_own(q, sent)
     for q in range(PQ):
         part_across(q).wait_send()
-    arrived(farx_o, R_XY + order[2])
-    far_out(sent)
     for zz in (z, *order[:2]):
         arrived(duo(dx_o, zz, 1 - c), R_XC + zz)
         dx_pair(zz, sent)
@@ -583,10 +577,10 @@
         functools.partial(group_kernel, shard_rows, tall),
         out_shape=(
             sds((t, m), F32), sds((t, m), F32), sds((lines, LANES), I32), sds((1, LANES), I32), sds((16 * t, m), BF16),
-            sds((t, m), BF16), sds((t // 2, m), BF16), sds((m, f), F32), sds((f, m), F32),
+            sds((t, m), BF16), sds((m, f), F32), sds((f, m), F32),
         ),
         in_specs=[vmem, any_, any_, any_, vmem, any_],
-        out_specs=(any_, any_, vmem, vmem, any_, any_, any_, any_, any_),
+        out_specs=(any_, any_, vmem, vmem, any_, any_, any_, any_),
         scratch_shapes=[
             V((m, f), BF16), V((f, m), BF16), V((16 * t, m), BF16), V((16 * t, m), BF16),
             V((4 * t, m), BF16), V((2 * t, m), BF16), V((2 * t, m), BF16),
@@ -672,47 +666,61 @@
 RING = 6
 
 
-def pass_pieces(src, buf, dst, in_sem, out_sem):
+def pass_pieces(src, buf, dst, in_sem, out_sem, first, count):
     rows = src.shape[0] // 8
 
+    def piece(i):
+        return pl.ds(pl.multiple_of((first + i) * rows, 8), rows)
+
     def fetch(i):
-        at = pl.ds(pl.multiple_of(i * rows, 8), rows)
-        return pltpu.make_async_copy(src.at[at], buf.at[at], in_sem.at[i])
+        return pltpu.make_async_copy(src.at[piece(i)], buf.at[pl.ds(pl.multiple_of(i * rows, 8), rows)], in_sem.at[i])
 
     def put(i):
-        at = pl.ds(pl.multiple_of(i * rows, 8), rows)
-        return pltpu.make_async_copy(buf.at[at], dst.at[at], out_sem)
+        return pltpu.make_async_copy(buf.at[pl.ds(pl.multiple_of(i * rows, 8), rows)], dst.at[piece(i)], out_sem)
 
     def step(i):
         fetch(i).wait()
         put(i).start()
 
-    return lambda i: fetch(i).start(), step, lambda: pltpu.make_async_copy(buf, dst, out_sem).wait()
-
-
-def pass_kernel(src, dst, buf, in_sem, out_sem):
-    fetch, step, drain = pass_pieces(src, buf, dst, in_sem, out_sem)
-    loop(0, 8, fetch)
-    loop(0, 8, step)
-    drain()
-
-
-def pass_on(w):
+    def drain():
+        pltpu.make_async_copy(buf, dst.at[pl.ds(first * rows, count * rows)], out_sem).wait()
+
+    return lambda i: fetch(i).start(), step, drain
+
+
+HALF = 4
+
+
+def pass_kernel(w1_in, w2_in, w1_out, w2_out, buf1, buf2, in1, in2, out1, out2):
+    fetch1, step1, drain1 = pass_pieces(w1_in, buf1, w1_out, in1, out1, 0, 8)
+    fetch2, step2, drain2 = pass_pieces(w2_in, buf2, w2_out, in2, out2, 0, HALF)
+    loop(0, 8, fetch1)
+    loop(0, HALF, fetch2)
+    loop(0, 8, step1)
+    loop(0, HALF, step2)
+    drain1()
+    drain2()
+
+
+def pass_on(w1, w2):
     any_ = pl.BlockSpec(memory_space=pl.ANY)
+    V, S = pltpu.VMEM, pltpu.SemaphoreType.DMA
+    f, m = w2.shape
     return pl.pallas_call(
         pass_kernel,
-        out_shape=jax.ShapeDtypeStruct(w.shape, w.dtype),
-        in_specs=[any_],
-        out_specs=any_,
-        scratch_shapes=[pltpu.VMEM(w.shape, w.dtype), pltpu.SemaphoreType.DMA((8,)), pltpu.SemaphoreType.DMA],
+        out_shape=(jax.ShapeDtypeStruct(w1.shape, F32), jax.ShapeDtypeStruct(w2.shape, F32)),
+        in_specs=[any_] * 2,
+        out_specs=[any_] * 2,
+        scratch_shapes=[V(w1.shape, F32), V((f * HALF // 8, m), F32), S((8,)), S((HALF,)), S, S],
         compiler_params=pltpu.CompilerParams(vmem_limit_bytes=60 << 20),
-        cost_estimate=pl.CostEstimate(flops=8000 * w.size, bytes_accessed=8 * w.size, transcendentals=0),
+        cost_estimate=pl.CostEstimate(flops=8000 * w1.size, bytes_accessed=12 * w1.size, transcendentals=0),
         name="pass_weights",
-    )(w)
-
-
-def table_kernel(tall, key_ref, first_ref, w_in, dx_in, far_own, far_x0, far_x1, far_partner, far_b0, far_b1,
+    )(w1, w2)
+
+
+def table_kernel(tall, key_ref, first_ref, w_in, w_half, dx_in, far_own, far_x, far_p, far_b,
                  out_hbm, w_out, dxb, dxf, ring, w_buf, dx_sem, t_sem, in_sem, out_sem):
+    del w_half
     count, _ = dxb.shape
     t = count // 16
     shift = count.bit_length() - 1
@@ -720,25 +728,21 @@
     z, r = lax.axis_index("data"), lax.axis_index("tensor")
     y, c = lax.div(r, 2), lax.rem(r, 2)
     late = lax.div(z, 2)
-    w_fetch, w_step, w_drain = pass_pieces(w_in, w_buf, w_out, in_sem, out_sem)
+    w_fetch, w_step, w_drain = pass_pieces(w_in, w_buf, w_out, in_sem, out_sem, HALF, 8 - HALF)
 
     def near(k):
         at = pl.ds(pl.multiple_of(late * (4 * t) + k * (2 * t), t), 2 * t)
         return at, pltpu.make_async_copy(dx_in.at[at], dxb.at[at], dx_sem.at[k])
 
-    def far(k, src, cc, yy, h):
-        n = src.shape[0]
-        at = pl.ds(pl.multiple_of((1 - late) * (12 * t) + cc * (2 * t) + yy * t + h * n, n), n)
+    def far(k, src, cc, yy):
+        at = pl.ds(pl.multiple_of((1 - late) * (12 * t) + cc * (2 * t) + yy * t, t), t)
         return at, pltpu.make_async_copy(src, dxb.at[at], dx_sem.at[6 + k])
 
-    fars = (
-        (far_own, c, y, 0), (far_partner, 1 - c, y, 0), (far_x0, c, 1 - y, 0), (far_b0, 1 - c, 1 - y, 0),
-        (far_x1, c, 1 - y, 1), (far_b1, 1 - c, 1 - y, 1),
-    )
+    fars = ((far_own, c, y), (far_p, 1 - c, y), (far_x, c, 1 - y), (far_b, 1 - c, 1 - y))
     loop(0, 6, lambda k: near(k)[1].start())
     for k, what in enumerate(fars):
         far(k, *what)[1].start()
-    loop(0, 8, w_fetch)
+    loop(0, 8 - HALF, w_fetch)
 
     def widen_piece(at, cp):
         cp.wait()
@@ -749,7 +753,10 @@
 
         rows_loop(at.size, widen)
 
-    loop(0, 6, lambda k: widen_piece(*near(k)))
+    for k in range(6):
+        widen_piece(*near(k))
+        if k >= 2:
+            w_step(k - 2)
     for k, what in enumerate(fars):
         widen_piece(*far(k, *what))
 
@@ -772,15 +779,15 @@
         low = first_ref[i]
         lax.fori_loop(low, first_ref[i + 1], add, key_ref[jnp.minimum(low, count - 1)])
         tile_out(i).start()
-        pl.when(i < 8)(lambda: w_step(i))
 
     loop(0, steps, tile)
     loop(steps - RING, steps, lambda i: tile_out(i).wait())
     w_drain()
 
 
-def table_grad(ordered, first, w, dx_all, fars, shard_rows, tall):
+def table_grad(ordered, first, w, w_half, dx_all, fars, shard_rows, tall):
     count, m = dx_all.shape
+    f = w.shape[0]
     any_ = pl.BlockSpec(memory_space=pl.ANY)
     V, S = pltpu.VMEM, pltpu.SemaphoreType.DMA
     return pl.pallas_call(
@@ -789,17 +796,18 @@
         grid_spec=pltpu.PrefetchScalarGridSpec(
             num_scalar_prefetch=2,
             grid=(1,),
-            in_specs=[any_] * 8,
+            in_specs=[any_] * 7,
             out_specs=[any_] * 2,
             scratch_shapes=[
-                V((count, m), BF16), V((count, m), F32), V((RING, tall, m), F32), V(w.shape, F32),
-                S((12,)), S((RING,)), S((8,)), S,
+                V((count, m), BF16), V((count, m), F32), V((RING, tall, m), F32), V((f - f * HALF // 8, m), F32),
+                S((10,)), S((RING,)), S((8 - HALF,)), S,
             ],
         ),
+        input_output_aliases={3: 1},
         compiler_params=pltpu.CompilerParams(vmem_limit_bytes=60 << 20),
         cost_estimate=pl.CostEstimate(flops=1600 * shard_rows * m, bytes_accessed=4 * shard_rows * m, transcendentals=0),
         name="table_grad",
-    )(ordered, first, w, dx_all, *fars)
+    )(ordered, first, w, w_half, dx_all, *fars)
 
 
 def solution(mesh):
@@ -813,18 +821,17 @@
         ids = token_ids.reshape(-1, LANES)
         masked = look_up(ids, embed_table)
         gain = norm_gain.reshape(-1, LANES)
-        base, ysum, ordered, first, dx_all, far, far_x0, dw1, dw2 = run_group(
+        base, ysum, ordered, first, dx_all, far, dw1, dw2 = run_group(
             ids, masked, w_in, w_out, gain, d_out, shard_rows, tall
         )
-        late = far[far.shape[0] // 2 :]
-        far_x1 = lax.ppermute(late, "tensor", over_y)
-        far_partner = lax.ppermute(far, "tensor", over_core)
-        far_b0 = lax.ppermute(far_x0, "tensor", over_core)
+        far_x = lax.ppermute(far, "tensor", over_y)
+        far_p = lax.ppermute(far, "tensor", over_core)
         other = lax.ppermute(ysum, "tensor", over_y)
-        grad_w_in = pass_on(dw1)
-        far_b1 = lax.ppermute(far_x1, "tensor", over_core)
-        fars = (far, far_x0, far_x1, far_partner, far_b0, far_b1)
-        grad_table, grad_w_out = table_grad(ordered.reshape(-1), first.reshape(-1), dw2, dx_all, fars, shard_rows, tall)
+        grad_w_in, w_half = pass_on(dw1, dw2)
+        far_b = lax.ppermute(far_x, "tensor", over_core)
+        grad_table, grad_w_out = table_grad(
+            ordered.reshape(-1), first.reshape(-1), dw2, w_half, dx_all, (far, far_x, far_p, far_b), shard_rows, tall
+        )
         return (base + other).astype(BF16), grad_table, grad_w_in, grad_w_out
 
     return jax.shard_map(

time: 227 us -> 239 us (1.053)
  waiting for transfers between devices: 6.47 us -> 22.2 us
  Pallas kernels: 214 us -> 211 us
    ppermute x1, waiting for transfers between devices: 0.01 us -> 9.29 us  [per_device(): other = lax.ppermute(ysum, 'tensor', over_y)]
    ppermute x4 -> x3, waiting for transfers between devices: 6.46 us -> 12.9 us  [the longest x1 12.9 us: per_device(): far_x = lax.ppermute(far, 'tensor', over_y)]
    pallas_call x1, Pallas kernels: 8.76 us -> 12.6 us  [pass_on(): pl.pallas_call(pass_kernel, out_shape=(jax.ShapeDtypeStruct(w1.shape, F32...]
    pallas_call x1, Pallas kernels: 164 us -> 161 us  [run_group(): pl.pallas_call(functools.partial(group_kernel, shard_rows, tall), out_sha...]
    pallas_call x1, Pallas kernels: 30.7 us -> 27.8 us  [table_grad(): pl.pallas_call(functools.partial(table_kernel, tall), out_shape=(jax.Shap...]
  transfers between devices with their start and end apart: 5 -> 4, of which waited for: 1 -> 2; matrix products, arithmetic and copies ran while one was open for 0% -> 0% of each run, Pallas kernels for 17% -> 5%
where the time goes in v6:
time: 239 us; the launch traced here: 238 us
  Pallas kernels  211 us (88%)
  waiting for transfers between devices  22.2 us (9%)
    pallas_call x1, Pallas kernels, run_group(): pl.pallas_call(functools.partial(group_kernel, shard_rows, tall), out_sha...  161 us
    pallas_call x1, Pallas kernels, table_grad(): pl.pallas_call(functools.partial(table_kernel, tall), out_shape=(jax.Shap...  27.8 us
    ppermute x1, waiting for transfers between devices, per_device(): far_x = lax.ppermute(far, 'tensor', over_y)  12.9 us
    pallas_call x1, Pallas kernels, pass_on(): pl.pallas_call(pass_kernel, out_shape=(jax.ShapeDtypeStruct(w1.shape, F32...  12.6 us
    pallas_call x1, Pallas kernels, look_up(): pl.pallas_call(functools.partial(lookup_kernel, shard_rows), out_shape=ja...  9.84 us
    ppermute x1, waiting for transfers between devices, per_device(): other = lax.ppermute(ysum, 'tensor', over_y)  9.29 us
  transfers between devices with their start and end apart: 4, of which 2 were waited for; matrix products, arithmetic and copies ran while one was open for 0% of the time, Pallas kernels for 5%

profile of v6, /device:TPU:0, one launch (start us, length us, event | category | flops | bytes accessed | tf_op | source)
XLA Modules:
  0.0 238.3 jit_solution(6465589985782839916)
XLA Ops:
  0.6 9.8 %look_up.1.xm_hbm = bf16[512,2048]{1,0:T(8,128)(2,1)} custom-call(s32[4,128]{1,0:T(4,128)} %bitcast.6, s32[4,128]{1,0:T(4,128)} %bitcast.7, bf16[1000,8,2048]{2,1,0:T(8,128)(2,1)} %bitcast.5), custom_call_target="tpu_custom_call" | custom-call | flops 16777216 | bytes 20971520 | tf_op jit(solution)/shard_map/look_up/pallas_call | solution.py:651
  10.5 161.0 %group_step.1 = (f32[128,2048]{1,0:T(8,128)}, f32[128,2048]{1,0:T(8,128)}, s32[16,128]{1,0:T(8,128)}, s32[1,128]{1,0:T(1,128)}, bf16[2048,2048]{1,0:T(8,128)(2,1...) custom-call(s32[4,128]{1,0:T(4,128)} %bitcast.8, bf16[512,2048]{1,0:T(8,128)(2,1)} %look_up.1.xm_hbm, ...), custom_call_target="tpu_custom_call" | custom-call | flops 53150220288 | bytes 268435456 | tf_op jit(solution)/shard_map/group_step/pallas_call | solution.py:576
  171.5 1.3 collective-permute-start.1
  172.8 0.1 collective-permute-start.2
  172.9 0.8 collective-permute-start
  173.7 12.9 %collective-permute-done.1.far_x = bf16[128,2048]{1,0:T(8,128)(2,1)S(1)} collective-permute-done((bf16[128,2048]{1,0:T(8,128)(2,1)}, bf16[128,2048]{1,0:T(8,128)(2,1)S(1)}, u32[]{:S(2)}, u32[]{:S(2)}) %collective-permute-start.1) | collective-permute-done | bytes 524320 | tf_op jit(solution)/shard_map/ppermute | solution.py:827
  186.6 0.0 copy-start.1
  186.6 0.0 collective-permute-start.3
  186.6 0.0 copy-start
  186.6 12.6 %pass_weights.1 = (f32[2048,1408]{1,0:T(8,128)}, f32[1408,2048]{1,0:T(8,128)}) custom-call(f32[2048,1408]{1,0:T(8,128)} %get-tuple-element.21.w1_in, f32[1408,2048]{1,0:T(8,128)} %get-tuple-element.20.w2_in.w_in), custom_call_target="tpu_custom_call" | custom-call | flops 23068672000 | bytes 34603008 | tf_op jit(solution)/shard_map/pass_weights/pallas_call | solution.py:709
  199.1 0.0 copy-done.1
  199.1 9.3 %collective-permute-done = f32[128,2048]{1,0:T(8,128)S(1)} collective-permute-done((f32[128,2048]{1,0:T(8,128)}, f32[128,2048]{1,0:T(8,128)S(1)}, u32[]{:S(2)}, u32[]{:S(2)}) %collective-permute-start) | collective-permute-done | bytes 1048608 | tf_op jit(solution)/shard_map/ppermute | solution.py:829
  208.4 0.0 copy-done
  208.4 0.9 add_convert_fusion
  209.4 0.0 collective-permute-done.2.far_p
  209.4 0.0 copy-start.2
  209.4 0.0 collective-permute-done.3.far_b
  209.4 0.0 copy-start.3
  209.4 0.8 copy-done.2
  210.2 0.2 copy-done.3
  210.3 27.8 %table_grad.1 = (f32[8000,2048]{1,0:T(8,128)}, f32[1408,2048]{1,0:T(8,128)}) custom-call(s32[2048]{0:T(1024)} %bitcast.10, s32[128]{0:T(128)} %bitcast.11, f32[1408,2048]{1,0:T(8,128)} %get-tuple-element.20.w2_in.w_in, f32[1408,2048]{1,0:T(8,128)} %get-tuple-element.22.w_half, ...), custom_call_target="tpu_custom_call", output_to_operand_aliasing={{1}: (3, {})} | custom-call | flops 26214400000 | bytes 65536000 | tf_op jit(solution)/shard_map/table_grad/pallas_call | solution.py:793
Async XLA Ops:
  171.5 15.1 %collective-permute-start.1 = (bf16[128,2048]{1,0:T(8,128)(2,1)}, bf16[128,2048]{1,0:T(8,128)(2,1)S(1)}, u32[]{:S(2)}, u32[]{:S(2)}) collective-permute-start(bf16[128,2048]{1,0:T(8,128)(2,1)} %get-tuple-element.24.far_own), channel_id=1, source_target_pairs={{0,2},{1,3},{2,0},{3,1},{4,6},{5,7},{6,4},{7,5},{8,10},{9,11},{10,... | collective-permute-start | bytes 1572872 | tf_op jit(solution)/shard_map/ppermute | solution.py:827
  172.8 36.6 %collective-permute-start.2 = (bf16[128,2048]{1,0:T(8,128)(2,1)}, bf16[128,2048]{1,0:T(8,128)(2,1)S(1)}, u32[]{:S(2)}, u32[]{:S(2)}) collective-permute-start(bf16[128,2048]{1,0:T(8,128)(2,1)} %get-tuple-element.24.far_own), channel_id=1, source_target_pairs={{0,1},{1,0},{2,3},{3,2},{4,5},{5,4},{6,7},{7,6},{8,9},{9,8},{10,11... | collective-permute-start | bytes 1572872 | tf_op jit(solution)/shard_map/ppermute | solution.py:828
  172.9 35.6 %collective-permute-start = (f32[128,2048]{1,0:T(8,128)}, f32[128,2048]{1,0:T(8,128)S(1)}, u32[]{:S(2)}, u32[]{:S(2)}) collective-permute-start(f32[128,2048]{1,0:T(8,128)} %get-tuple-element.17), channel_id=1, source_target_pairs={{0,2},{1,3},{2,0},{3,1},{4,6},{5,7},{6,4},{7,5},{8,10},{9,11},{10,... | collective-permute-start | bytes 3145736 | tf_op jit(solution)/shard_map/ppermute | solution.py:829
  186.6 12.6 %copy-start.1 = (bf16[128,2048]{1,0:T(8,128)(2,1)}, bf16[128,2048]{1,0:T(8,128)(2,1)S(1)}, u32[]{:S(2)}) copy-start(bf16[128,2048]{1,0:T(8,128)(2,1)S(1)} %collective-permute-done.1.far_x) | copy-start | bytes 1572868
  186.6 22.8 %collective-permute-start.3 = (bf16[128,2048]{1,0:T(8,128)(2,1)S(1)}, bf16[128,2048]{1,0:T(8,128)(2,1)S(1)}, u32[]{:S(2)}, u32[]{:S(2)}) collective-permute-start(bf16[128,2048]{1,0:T(8,128)(2,1)S(1)} %collective-permute-done.1.far_x), channel_id=1, source_target_pairs={{0,1},{1,0},{2,3},{3,2},{4,5},{5,4},{6,7},{7,6},{8,9},{9,8},{10,11... | collective-permute-start | bytes 1572872 | tf_op jit(solution)/shard_map/ppermute | solution.py:831
  186.6 21.9 %copy-start = (f32[128,2048]{1,0:T(8,128)S(1)}, f32[128,2048]{1,0:T(8,128)}, u32[]{:S(2)}) copy-start(f32[128,2048]{1,0:T(8,128)} %get-tuple-element.16) | copy-start | bytes 3145732
  209.4 0.8 copy-start.2
  209.4 1.0 copy-start.3
